TPU v7x, 512 devices: a whole 4x8x8 slice. The times are simulated.
512 devices in a mesh: roll: 64 (over z, y_lo, core), tensor: 8 (over x, y_hi).
Axes of the slice: x: 4, y: 8 (y_hi: 2, y_lo: 4; y = y_hi * 4 + y_lo), z: 8, core: 2. Of those that a mesh axis runs over, the one named last changes fastest.
Arguments:
- grad_out: bfloat16 [24576, 5120], P('roll', 'tensor'), may hold values from -6 to 6
- out_weight: bfloat16 [5120, 4096], P('roll', 'tensor'), may hold values from -0.078125 to 0.078125
- queries: bfloat16 [24576, 4096], P('roll', 'tensor'), may hold values from -6 to 6
- resp_key: bfloat16 [24576, 1024], P('roll', 'tensor'), may hold values from -5 to 5
- resp_value: bfloat16 [24576, 1024], P('roll', 'tensor'), may hold values from -5 to 5
- prefix_key: bfloat16 [256, 1024], P('roll', 'tensor'), may hold values from -5 to 5
- prefix_value: bfloat16 [256, 1024], P('roll', 'tensor'), may hold values from -5 to 5
- lengths: int32 [64], P('roll'), may hold values from 1 to 384
Outputs:
- grad_query: bfloat16 [24576, 4096], P('roll', 'tensor')
- grad_resp_key: bfloat16 [24576, 1024], P('roll', 'tensor')
- grad_resp_value: bfloat16 [24576, 1024], P('roll', 'tensor')
- grad_prefix_key: float32 [256, 1024], P('roll', 'tensor')
- grad_prefix_value: float32 [256, 1024], P('roll', 'tensor')
All inputs are finite; a program needn't handle non-finite values.
Results may differ from a plain program's by a relative error of at most 0.0063.
Values may be sent and summed in bfloat16 or wider, within the bound.
No kernel may reach another device: no remote copies, remote signals or barrier semaphores. Data moves between devices by JAX's collectives and lax.ppermute only.
A program may use at most 64 MiB of HBM per device.

v0:
```python
from functools import partial

import jax
import jax.numpy as jnp
from jax import lax
from jax.sharding import Mesh
from jax.sharding import PartitionSpec as P

HD = 128
ROWS = 384
ROLL = ("roll_0", "roll_1", "roll_2")


def in_order(parts, dim):
    parts = jnp.moveaxis(parts, 0, dim)
    shape = parts.shape
    return parts.reshape(*shape[:dim], shape[dim] * shape[dim + 1], *shape[dim + 2 :])


def stacked_from(x, axes, turns):
    parts = x[None]
    for k in turns:
        parts = lax.all_gather(parts, axes[k], axis=0, tiled=True)
    held = [lax.axis_size(axes[k]) for k in reversed(turns)]
    parts = parts.reshape(*held, *x.shape)
    turned = sorted(range(len(turns)), key=lambda place: turns[len(turns) - 1 - place])
    return parts.transpose(*turned, *range(len(turns), parts.ndim)).reshape(-1, *x.shape)


def gathered_by_axis(x, axes, turns, dim):
    return in_order(stacked_from(x, axes, turns), dim)


def side_by_side(arrays, axis, dim, along):
    widths = [a.shape[along] for a in arrays]
    both = jnp.concatenate(arrays, axis=along)
    whole = lax.all_gather(both, axis, axis=dim, tiled=True)
    return tuple(jnp.split(whole, [sum(widths[:k]) for k in range(1, len(widths))], axis=along))


def split_up(x, dim, length):
    before, after = (x.shape[:dim], x.shape[dim + 1 :])
    return jnp.moveaxis(x.reshape(*before, length, -1, *after), dim, 0)


def summed_on_arrival(x, axis, dim):
    length = lax.axis_size(axis)
    parts = lax.all_to_all(split_up(x, dim, length), axis, 0, 0, tiled=True)
    return jnp.sum(parts, axis=0)


def side_by_side_2(arrays, axis, dim, along):
    both = jnp.concatenate(arrays, axis=along)
    whole, at, done = (summed_on_arrival(both, axis, dim), 0, [])
    for a in arrays:
        done.append(lax.slice_in_dim(whole, at, at + a.shape[along], axis=along))
        at += a.shape[along]
    return tuple(done)


def block_terms(query_rows, grad_rows, offset, all_keys, all_values, prefix_rows, keep_prefix):
    row_count = query_rows.shape[0]
    local_heads = all_keys.shape[1] // HD
    group_size = query_rows.shape[1] // all_keys.shape[1]
    score_scale = HD ** (-0.5)
    query_heads = query_rows.reshape(row_count, local_heads, group_size, HD)
    grad_heads = grad_rows.reshape(row_count, local_heads, group_size, HD)
    key_heads = all_keys.reshape(-1, local_heads, HD)
    value_heads = all_values.reshape(-1, local_heads, HD)
    scores = (
        jnp.einsum("ikgd,jkd->kgij", query_heads, key_heads, preferred_element_type=jnp.float32)
        * score_scale
    )
    query_place = offset + jnp.arange(row_count, dtype=jnp.int32)[:, None]
    key_place = jnp.arange(key_heads.shape[0], dtype=jnp.int32)[None, :]
    allowed = (key_place < prefix_rows) | (key_place - prefix_rows <= query_place)
    scores = jnp.where(allowed, scores, -jnp.inf)
    row_max = jnp.max(scores, axis=-1, keepdims=True)
    shifted = jnp.exp(scores - row_max)
    row_total = jnp.sum(shifted, axis=-1, keepdims=True)
    soft_weights = shifted / row_total
    weights_low = soft_weights.astype(jnp.bfloat16)
    prob_grad = jnp.einsum(
        "ikgd,jkd->kgij", grad_heads, value_heads, preferred_element_type=jnp.float32
    )
    row_delta = jnp.sum(soft_weights * prob_grad, axis=-1, keepdims=True)
    score_low = (soft_weights * (prob_grad - row_delta) * score_scale).astype(jnp.bfloat16)
    query_grad = jnp.einsum(
        "kgij,jkd->ikgd", score_low, key_heads, preferred_element_type=jnp.float32
    )
    query_grad = query_grad.reshape(row_count, -1).astype(jnp.bfloat16)
    key_count = score_low.shape[-1]
    key_grad = jnp.einsum(
        "kgij,ikgd->jkd", score_low, query_heads, preferred_element_type=jnp.float32
    )
    value_grad = jnp.einsum(
        "kgij,ikgd->jkd", weights_low, grad_heads, preferred_element_type=jnp.float32
    )
    return (
        query_grad,
        key_grad.reshape(key_count, -1),
        value_grad.reshape(key_count, -1),
        row_max,
        row_total,
        row_delta,
    )


def body(grad_out, out_weight, queries, resp_key, resp_value, prefix_key, prefix_value, lengths):
    rows_here = queries.shape[0]
    responses = rows_here // ROWS
    full_grad = lax.all_gather(grad_out, "tensor", axis=1, tiled=True)
    projected = jnp.dot(
        full_grad,
        gathered_by_axis(out_weight, ROLL, (1, 0, 2), 0),
        preferred_element_type=jnp.float32,
    )
    position = jnp.arange(rows_here, dtype=jnp.int32)
    matches = (position // ROWS)[:, None] == jnp.arange(responses, dtype=jnp.int32)[None, :]
    row_limit = jnp.sum(jnp.where(matches, lengths[None, :], 0), axis=1)
    valid_rows = (position % ROWS < row_limit).astype(jnp.float32)
    out_grad = (projected * valid_rows[:, None]).astype(jnp.bfloat16)
    prefix_keys, prefix_values = side_by_side((prefix_key, prefix_value), ROLL, 0, 1)
    prefix_rows = prefix_keys.shape[0]
    key_width = prefix_key.shape[1]
    block_rows = min(128, ROWS)
    query_parts, key_parts, value_parts, saved = ([], [], [], [])
    all_keys = jnp.concatenate([prefix_keys, resp_key], axis=0)
    all_values = jnp.concatenate([prefix_values, resp_value], axis=0)
    key_rows = all_keys.shape[0]
    key_sum = jnp.zeros((key_rows, key_width), jnp.float32)
    value_sum = jnp.zeros((key_rows, key_width), jnp.float32)
    for part_index in range(ROWS // block_rows):
        offset = part_index * block_rows
        compute_block = partial(
            block_terms,
            queries[offset : offset + block_rows],
            out_grad[offset : offset + block_rows],
            offset,
            all_keys,
            all_values,
            prefix_rows,
            True,
        )
        result = compute_block()
        query_grad, key_grad, value_grad, row_max, row_total, row_delta = result
        query_parts.append(query_grad)
        key_sum = key_sum + key_grad
        value_sum = value_sum + value_grad
        saved.append((0, offset, offset, row_max, row_total, row_delta))
    prefix_key_sum = key_sum[:prefix_rows]
    prefix_value_sum = value_sum[:prefix_rows]
    key_sum = key_sum[prefix_rows:]
    value_sum = value_sum[prefix_rows:]
    key_parts.append(key_sum.astype(jnp.bfloat16))
    value_parts.append(value_sum.astype(jnp.bfloat16))
    grad_prefix_key, grad_prefix_value = side_by_side_2(
        (prefix_key_sum, prefix_value_sum), ROLL, 0, 1
    )
    grad_query = jnp.concatenate(query_parts, axis=0)
    grad_resp_key = key_parts[0]
    grad_resp_value = value_parts[0]
    return (grad_query, grad_resp_key, grad_resp_value, grad_prefix_key, grad_prefix_value)


def solution(mesh):
    torus = Mesh(
        mesh.devices.reshape(8, 4, 2, mesh.shape["tensor"]),
        ("roll_0", "roll_1", "roll_2", "tensor"),
    )
    placed = (
        P(ROLL, "tensor"),
        P(ROLL, "tensor"),
        P(ROLL, "tensor"),
        P(ROLL, "tensor"),
        P(ROLL, "tensor"),
        P(ROLL, "tensor"),
        P(ROLL, "tensor"),
        P(ROLL),
    )
    return jax.shard_map(
        body,
        mesh=torus,
        in_specs=placed,
        out_specs=(
            P(ROLL, "tensor"),
            P(ROLL, "tensor"),
            P(ROLL, "tensor"),
            P(ROLL, "tensor"),
            P(ROLL, "tensor"),
        ),
        check_vma=False,
    )
```

profile of v0, /device:TPU:1, one launch (start us, length us, event | category | flops | bytes accessed | tf_op | source)
XLA Modules:
  0.0 262.5 jit_solution(3908151491509216259)
XLA Ops:
  7.2 14.7 %all-gather = bf16[320,512]{1,0:T(8,128)(2,1)} all-gather(bf16[80,512]{1,0:T(8,128)(2,1)} %param.9), channel_id=2, replica_groups=mesh['roll_0'=8,'roll_1'=4,'roll_2'=2,'tensor'=8] {'roll_1'}, dimensions={0}, use_global_device_ids=true | all-gather | bytes 409600 | tf_op jit(solution)/shard_map/all_gather | solution.py:23
  21.9 48.3 %all-gather.8.cloned.1.call-done = bf16[32,80,512]{2,1,0:T(8,128)(2,1)} async-done(((bf16[4,80,512]{2,1,0:T(8,128)(2,1)}), bf16[32,80,512]{2,1,0:T(8,128)(2,1)}) %all-gather.8.cloned.1.call-update) | async-done | bytes 2621456 | tf_op jit(solution)/shard_map/all_gather | solution.py:23
  70.4 0.7 all-gather.6.cloned.1.call-update
  71.1 83.0 %all-gather.1 = bf16[64,4,256]{2,1,0:T(4,128)(2,1)S(1)} all-gather(bf16[1,4,256]{2,1,0:T(4,128)(2,1)S(1)} %maximum_bitcast_fusion.5), channel_id=1, replica_groups=mesh['roll_0'=8,'roll_1'=4,'roll_2'=2,'tensor'=8] {'roll_0','roll_1','ro..., dimensions={0}, use_global_device_ids=true | all-gather | bytes 133120 | tf_op jit(solution)/shard_map/all_gather | solution.py:37
  157.6 5.3 %copy.102 = bf16[8,4,2,80,512]{4,3,2,1,0:T(8,128)(2,1)} copy(bf16[8,4,2,80,512]{4,3,1,0,2:T(8,128)(2,1)} %bitcast.153) | data formatting | bytes 10485760 | tf_op jit(solution)/shard_map/transpose | solution.py:27
  163.0 42.9 %all-gather.6.cloned.1.call-done = bf16[384,5120]{1,0:T(8,128)(2,1)} async-done(((bf16[384,640]{1,0:T(8,128)(2,1)}), bf16[384,5120]{1,0:T(8,128)(2,1)}) %all-gather.6.cloned.1.call-update) | async-done | bytes 3932176 | tf_op jit(solution)/shard_map/all_gather | solution.py:112
  205.9 5.9 %fusion.6 = bf16[384,512]{1,0:T(8,128)(2,1)S(1)} fusion(bf16[384,5120]{1,0:T(8,128)(2,1)} %all-gather.6.cloned.1.call-done, bf16[5120,512]{1,0:T(8,128)(2,1)} %bitcast.154, f32[384]{0:T(512)S(1)} %fusion.31), kind=kOutput, calls=%fused_computation.22 | convolution fusion | flops 2013659136 | bytes 9569792 | tf_op jit(solution)/shard_map/dot_general | solution.py:113
  211.7 0.7 fusion.40
  212.4 1.7 copy.153
  214.1 0.8 copy.154
  214.8 2.5 convolution_bitcast_fusion.4
  217.4 1.1 convolution_bitcast_fusion.3
  218.8 1.4 multiply_reduce_fusion.1
  220.2 1.4 multiply_reduce_fusion
  222.1 0.6 copy-done.14
  223.2 0.9 copy-done.4
  225.2 0.6 copy-done.1
  228.1 0.8 reshape.248
  228.9 12.9 %all-to-all-start = ((f32[64,4,256]{2,1,0:T(4,128)}), f32[64,4,256]{2,1,0:T(4,128)S(1)}, u32[]{:S(2)}, u32[]{:S(2)}) async-start(f32[64,4,256]{2,1,0:T(4,128)} %reshape.248), calls=%async_computation | async-start | bytes 524288 | tf_op jit(solution)/shard_map/all_to_all | solution.py:48
  241.8 0.8 copy.130
  242.6 0.8 copy.129
  244.3 0.8 pad_maximum_fusion
  245.1 10.3 %all-to-all-done = f32[64,4,256]{2,1,0:T(4,128)S(1)} async-done(((f32[64,4,256]{2,1,0:T(4,128)}), f32[64,4,256]{2,1,0:T(4,128)S(1)}, u32[]{:S(2)}, u32[]{:S(2)}) %all-to-all-start) | async-done | bytes 262176 | tf_op jit(solution)/shard_map/all_to_all | solution.py:48
  255.4 0.6 fusion.42
  (75 shorter events, 8.7 us)
Async XLA Ops:
  7.2 63.1 %all-gather.8.cloned.1.call-start = ((), (), s32[]{:S(2)}) async-start(), calls=%async_computation.2 | async-start | bytes 2949120 | tf_op jit(solution)/shard_map/all_gather | solution.py:23
  21.9 135.7 %all-gather.10.cloned.1.call-start = ((), (), s32[]{:S(2)}) async-start(), calls=%async_computation.3 | async-start | bytes 7864320 | tf_op jit(solution)/shard_map/all_gather | solution.py:23
  70.3 0.8 copy-start.11
  70.3 0.8 copy-start.12
  70.3 83.8 %copy-start.8 = (bf16[384,512]{1,0:T(8,128)(2,1)S(1)}, bf16[384,512]{1,0:T(8,128)(2,1)}, u32[]{:S(2)}) copy-start(bf16[384,512]{1,0:T(8,128)(2,1)} %param.10) | copy-start | bytes 1179652
  70.3 135.6 %all-gather.6.cloned.1.call-start = ((), (), s32[]{:S(2)}) async-start(), calls=%async_computation.1 | async-start | bytes 4423680 | tf_op jit(solution)/shard_map/all_gather | solution.py:112
  71.1 84.4 %copy-start.7 = (bf16[384,128]{1,0:T(8,128)(2,1)S(1)}, bf16[384,128]{1,0:T(8,128)(2,1)}, u32[]{:S(2)}) copy-start(bf16[384,128]{1,0:T(8,128)(2,1)} %param.11) | copy-start | bytes 294916
  155.8 1.1 copy-start.2
  156.9 63.3 %copy-start = (f32[1,4,128,640]{2,3,1,0:T(8,128)}, f32[1,4,128,640]{2,3,1,0:T(8,128)S(1)}, u32[]{:S(2)}) copy-start(f32[1,4,128,640]{2,3,1,0:T(8,128)S(1)} %get-tuple-element.39) | copy-start | bytes 3932164
  214.8 2.6 copy-start.9
  217.4 1.3 copy-start.3
  217.4 1.3 copy-start.10
  217.4 1.4 copy-start.13
  221.7 1.0 copy-start.14
  221.7 1.1 copy-start.15
  222.8 1.3 copy-start.4
  222.8 1.7 copy-start.6
  224.5 1.3 copy-start.1
  224.5 1.7 copy-start.5
  228.9 26.4 %all-to-all-start = ((f32[64,4,256]{2,1,0:T(4,128)}), f32[64,4,256]{2,1,0:T(4,128)S(1)}, u32[]{:S(2)}, u32[]{:S(2)}) async-start(f32[64,4,256]{2,1,0:T(4,128)} %reshape.248), calls=%async_computation | async-start | bytes 524288 | tf_op jit(solution)/shard_map/all_to_all | solution.py:48
Sparse Core Ops, SparseCore 0:
  22.0 48.2 all-gather.7
  72.4 26.1 all-gather.9
  101.7 104.0 all-gather.5
where the time goes:
time: 263 us
  waiting for transfers between devices  102 us (39%)
  blocking collectives  97.6 us (37%)
  local copies, waits for them, and re-layouts  16.2 us (6%)
  matrix products  16 us (6%)
  between operations  14.7 us (6%)
  starting transfers between devices  13 us (5%)
  other arithmetic  2.8 us (1%)
    all_gather x1, blocking collectives, side_by_side(): whole = lax.all_gather(both, axis, axis=dim, tiled=True)  83 us
    all_gather x2, waiting for transfers between devices, stacked_from(): parts = lax.all_gather(parts, axes[k], axis=0, tiled=True)  48.3 us
    all_gather x1, waiting for transfers between devices, body(): full_grad = lax.all_gather(grad_out, 'tensor', axis=1, tiled=True)  42.9 us
    all_gather x1, blocking collectives, stacked_from(): parts = lax.all_gather(parts, axes[k], axis=0, tiled=True)  14.7 us
    all_to_all x1, starting transfers between devices, summed_on_arrival(): parts = lax.all_to_all(split_up(x, dim, length), axis, 0, 0, tiled=True)  12.9 us
    all_to_all x1, waiting for transfers between devices, summed_on_arrival(): parts = lax.all_to_all(split_up(x, dim, length), axis, 0, 0, tiled=True)  10.3 us
    dot_general x1, matrix products, body(): jnp.dot(full_grad, gathered_by_axis(out_weight, ROLL, (1, 0, 2), 0), pref...  5.87 us
    unnamed x38, local copies, waits for them, and re-layouts  5.72 us
  transfers between devices with their start and end apart: 4, of which 3 were waited for; matrix products, arithmetic and copies ran while one was open for 4% of the time, Pallas kernels for 0%

commit v1 on v0

v1 whole, which is shorter than its diff:
```python
from functools import partial

import jax
import jax.numpy as jnp
from jax import lax
from jax.experimental import pallas as pl
from jax.experimental.pallas import tpu as pltpu
from jax.sharding import Mesh
from jax.sharding import PartitionSpec as P

HD = 128
ROWS = 384
BLOCK = 128
GROUP = 4
PREFIX = 256
SCALE = HD**-0.5
F32 = jnp.float32
BF16 = jnp.bfloat16
ROLL = ("z", "yl", "c")
TENSOR = ("x", "yh")
NZ, NY, NX = 8, 4, 4
NT = (((1,), (1,)), ((), ()))


def swap(v, axis, bit=1):
    size = lax.axis_size(axis)
    return lax.ppermute(v, axis, [(i, i ^ bit) for i in range(size)])


def ring_x(v):
    pairs = []
    for x in range(NX):
        pairs.append((x, (x + 1) % NX))
        pairs.append((NX + x, NX + (x - 1) % NX))
    return lax.ppermute(v, ("c", "x"), pairs)


def ring_z(v):
    pairs = []
    for z in range(NZ):
        pairs.append((2 * z, 2 * ((z + 1) % NZ)))
        pairs.append((2 * z + 1, 2 * ((z - 1) % NZ) + 1))
    return lax.ppermute(v, ("z", "c"), pairs)


def in_pair(mine, other, bit, axis):
    first = jnp.where(bit == 0, mine, other)
    second = jnp.where(bit == 0, other, mine)
    return jnp.concatenate([first, second], axis=axis)


def soft_kernel(q_ref, rk_ref, pkv_ref, *p_refs):
    keys = jnp.concatenate([pkv_ref[:, :HD], rk_ref[...]], axis=0)
    for i, p_ref in enumerate(p_refs):
        low = PREFIX + BLOCK * i
        rows = slice(BLOCK * i, BLOCK * (i + 1))
        queries = jnp.concatenate(
            [q_ref[rows, HD * h : HD * (h + 1)] for h in range(GROUP)], axis=0
        )
        scores = (
            lax.dot_general(keys[: low + BLOCK], queries, NT, preferred_element_type=F32) * SCALE
        )
        open_part = scores[:low]
        key_place = lax.broadcasted_iota(jnp.int32, (BLOCK, GROUP * BLOCK), 0)
        row_place = lax.broadcasted_iota(jnp.int32, (BLOCK, GROUP * BLOCK), 1) % BLOCK
        edge = jnp.where(key_place <= row_place, scores[low:], -jnp.inf)
        top = jnp.maximum(
            jnp.max(open_part, axis=0, keepdims=True), jnp.max(edge, axis=0, keepdims=True)
        )
        open_part = jnp.exp(open_part - top)
        edge = jnp.exp(edge - top)
        total = jnp.sum(open_part, axis=0, keepdims=True) + jnp.sum(edge, axis=0, keepdims=True)
        share = 1.0 / total
        p_ref[:low] = (open_part * share).astype(BF16)
        p_ref[low:] = (edge * share).astype(BF16)


def grad_kernel(
    place_ref,
    length_ref,
    *refs,
):
    g_in, w_in = refs[:8], refs[8:17]
    p_refs = refs[17:20]
    q_ref, rk_ref, rv_ref, pkv_ref = refs[20:24]
    gq_ref, grk_ref, grv_ref, gp_ref = refs[24:28]
    g_buf, w_buf, acc, og, sem = refs[28:]
    x, yh, z, core = place_ref[0], place_ref[1], place_ref[2], place_ref[3]
    way = 1 - 2 * core
    copies = []
    for k, src in enumerate(w_in):
        if k < 7:
            step = (k + 1) // 2
            sign = way if k % 2 == 0 else -way
            slot = lax.rem(z + step * sign + 8, 8)
            dst = w_buf.at[slot]
        else:
            half = core if k == 7 else 1 - core
            slot = lax.rem(z + 4, 8)
            dst = w_buf.at[slot, pl.ds(pl.multiple_of(320 * half, 320), 320)]
        copies.append(pltpu.make_async_copy(src, dst, sem.at[k]))
    for k, src in enumerate(g_in):
        copies.append(pltpu.make_async_copy(src, g_buf.at[k], sem.at[9 + k]))
    for c in copies:
        c.start()
    for c in copies:
        c.wait()

    def project(k, _):
        side = jnp.where(k < 4, yh, 1 - yh)
        source = lax.rem(x - lax.rem(k, 4) * way + 8, 4)
        w = w_buf[2 * source + side]
        part = jnp.dot(g_buf[k], w, preferred_element_type=F32)
        acc[...] = jnp.where(k == 0, part, acc[...] + part)
        return 0

    lax.fori_loop(0, 8, project, 0)
    row = lax.broadcasted_iota(jnp.int32, (ROWS, GROUP * HD), 0)
    og[...] = jnp.where(row < length_ref[0], acc[...], 0.0).astype(BF16)

    keys = jnp.concatenate([pkv_ref[:, :HD], rk_ref[...]], axis=0)
    values = jnp.concatenate([pkv_ref[:, HD:], rv_ref[...]], axis=0)
    keys_t = keys.astype(F32).T.astype(BF16)
    key_grad = [None] * 4
    value_grad = [None] * 4
    for i, p_ref in enumerate(p_refs):
        width = PREFIX + BLOCK * (i + 1)
        rows = slice(BLOCK * i, BLOCK * (i + 1))
        stack = lambda r: jnp.concatenate(
            [r[rows, HD * h : HD * (h + 1)] for h in range(GROUP)], axis=0
        )
        queries, grads = stack(q_ref), stack(og)
        prob_grad = lax.dot_general(values[:width], grads, NT, preferred_element_type=F32)
        weights = p_ref[...]
        wide = weights.astype(F32)
        product = wide * prob_grad
        delta = jnp.sum(product, axis=0, keepdims=True)
        score_low = ((product - wide * delta) * SCALE).astype(BF16)
        kg = jnp.dot(score_low, queries, preferred_element_type=F32)
        vg = jnp.dot(weights, grads, preferred_element_type=F32)
        qt = jnp.dot(keys_t[:, :width], score_low, preferred_element_type=F32)
        for h in range(GROUP):
            gq_ref[rows, HD * h : HD * (h + 1)] = qt[:, BLOCK * h : BLOCK * (h + 1)].T.astype(BF16)
        for j in range(i + 2):
            part = slice(0, PREFIX) if j == 0 else slice(PREFIX + BLOCK * (j - 1), PREFIX + BLOCK * j)
            key_grad[j] = kg[part] if key_grad[j] is None else key_grad[j] + kg[part]
            value_grad[j] = vg[part] if value_grad[j] is None else value_grad[j] + vg[part]
    gp_ref[:, :HD] = key_grad[0]
    gp_ref[:, HD:] = value_grad[0]
    for j in range(3):
        rows = slice(BLOCK * j, BLOCK * (j + 1))
        grk_ref[rows] = key_grad[j + 1].astype(BF16)
        grv_ref[rows] = value_grad[j + 1].astype(BF16)


VM = pl.BlockSpec(memory_space=pltpu.VMEM)
SM = pl.BlockSpec(memory_space=pltpu.SMEM)
ANY = pl.BlockSpec(memory_space=pl.ANY)


def soft(queries, resp_key, prefix):
    return pl.pallas_call(
        soft_kernel,
        out_shape=[
            jax.ShapeDtypeStruct((PREFIX + BLOCK * (i + 1), GROUP * BLOCK), BF16) for i in range(3)
        ],
        in_specs=[VM] * 3,
        out_specs=[VM] * 3,
        cost_estimate=pl.CostEstimate(
            flops=2 * 1536 * 640 * 128, bytes_accessed=3000000, transcendentals=1000000
        ),
        name="soft",
    )(queries, resp_key, prefix)


def grads(place, lengths, g, w, p, queries, resp_key, resp_value, prefix):
    return pl.pallas_call(
        grad_kernel,
        out_shape=[
            jax.ShapeDtypeStruct((ROWS, GROUP * HD), BF16),
            jax.ShapeDtypeStruct((ROWS, HD), BF16),
            jax.ShapeDtypeStruct((ROWS, HD), BF16),
            jax.ShapeDtypeStruct((PREFIX, 2 * HD), F32),
        ],
        in_specs=[SM] * 2 + [ANY] * 17 + [VM] * 7,
        out_specs=[VM] * 4,
        scratch_shapes=[
            pltpu.VMEM((8, ROWS, 640), BF16),
            pltpu.VMEM((8, 640, 512), BF16),
            pltpu.VMEM((ROWS, 512), F32),
            pltpu.VMEM((ROWS, 512), BF16),
            pltpu.SemaphoreType.DMA((17,)),
        ],
        cost_estimate=pl.CostEstimate(
            flops=2 * 384 * 5120 * 512, bytes_accessed=14000000, transcendentals=0
        ),
        name="grads",
    )(place, lengths, *g, *w, *p, queries, resp_key, resp_value, prefix)


def body(grad_out, out_weight, queries, resp_key, resp_value, prefix_key, prefix_value, lengths):
    x, yh = lax.axis_index("x"), lax.axis_index("yh")
    z, yl, core = lax.axis_index("z"), lax.axis_index("yl"), lax.axis_index("c")
    both = jnp.concatenate([prefix_key, prefix_value], axis=1)
    prefix = lax.all_to_all(
        jnp.broadcast_to(both[None], (64,) + both.shape), ROLL, 0, 0, tiled=True
    ).reshape(PREFIX, 2 * HD)

    g = [grad_out]
    for _ in range(3):
        g.append(ring_x(g[-1]))
    other = swap(grad_out, "yh")
    g.append(other)
    for _ in range(3):
        g.append(ring_x(g[-1]))

    two = in_pair(out_weight, swap(out_weight, "yl", 1), yl % 2, 0)
    four = in_pair(two, swap(two, "yl", 2), yl // 2, 0)
    piece = in_pair(
        four.reshape(4, 1, 80, 512), swap(four, "c").reshape(4, 1, 80, 512), core, 1
    ).reshape(640, 512)
    w = [piece]
    ahead = piece
    for _ in range(3):
        ahead = ring_z(ahead)
        w += [ahead, swap(ahead, "c")]
    half = jnp.where(core == 0, ahead[:320], ahead[320:])
    last = ring_z(half)
    w += [last, swap(last, "c")]

    p = soft(queries, resp_key, prefix)
    place = jnp.stack([x, yh, z, core]).astype(jnp.int32)
    gq, grk, grv, gp = grads(
        place, lengths, g, w, p, queries, resp_key, resp_value, prefix
    )
    parts = lax.all_to_all(gp.reshape(64, 4, 2 * HD), ROLL, 0, 0, tiled=True)
    total = jnp.sum(parts, axis=0)
    return gq, grk, grv, total[:, :HD], total[:, HD:]


def solution(mesh):
    torus = Mesh(mesh.devices.reshape(NZ, NY, 2, NX, 2), ROLL + TENSOR)
    placed = P(ROLL, TENSOR)
    return jax.shard_map(
        body,
        mesh=torus,
        in_specs=(placed,) * 7 + (P(ROLL),),
        out_specs=(placed,) * 5,
        check_vma=False,
    )
```

time: 263 us -> 166 us (0.63)
  blocking collectives: 97.6 us -> 17.4 us
  starting transfers between devices: 13 us -> 82.8 us
  waiting for transfers between devices: 102 us -> 42.2 us
  matrix products: 16 us -> 0 us
  Pallas kernels: 0 us -> 15.6 us
  between operations: 14.7 us -> 1.77 us
  local copies, waits for them, and re-layouts: 16.2 us -> 3.83 us
    all_gather x2 -> x0, blocking collectives: 97.6 us -> none  [the longest x1 83 us: side_by_side(): whole = lax.all_gather(both, axis, axis=dim, tiled=True)]
    all_gather x3 -> x0, waiting for transfers between devices: 91.2 us -> none  [the longest x2 48.3 us: stacked_from(): parts = lax.all_gather(parts, axes[k], axis=0, tiled=True)]
    ppermute x0 -> x18, starting transfers between devices: none -> 72.5 us  [the longest x8 35.7 us: swap(): return lax.ppermute(v, axis, [(i, i ^ bit) for i in range(size)])]
    ppermute x0 -> x18, waiting for transfers between devices: none -> 32.7 us  [the longest x8 22.2 us: swap(): return lax.ppermute(v, axis, [(i, i ^ bit) for i in range(size)])]
    all_to_all x0 -> x1, blocking collectives: none -> 17.4 us  [body(): parts = lax.all_to_all(gp.reshape(64, 4, 2 * HD), ROLL, 0, 0, tiled=True)]
    dot_general x16 -> x0, matrix products: 16 us -> none  [the longest x1 5.87 us: body(): jnp.dot(full_grad, gathered_by_axis(out_weight, ROLL, (1, 0, 2), 0), pref...]
    pallas_call x0 -> x2, Pallas kernels: none -> 15.6 us  [the longest x1 12.3 us: grads(): pl.pallas_call(grad_kernel, out_shape=[jax.ShapeDtypeStruct((ROWS, GROUP...]
    transpose x1 -> x0, local copies, waits for them, and re-layouts: 5.34 us -> none  [stacked_from(): parts.transpose(*turned, *range(len(turns), parts.ndim))]
  transfers between devices with their start and end apart: 4 -> 19, of which waited for: 3 -> 7; matrix products, arithmetic and copies ran while one was open for 4% -> 1% of each run, Pallas kernels for 0% -> 2%
where the time goes in v1:
time: 166 us
  starting transfers between devices  82.8 us (50%)
  waiting for transfers between devices  42.2 us (25%)
  blocking collectives  17.4 us (10%)
  Pallas kernels  15.6 us (9%)
  local copies, waits for them, and re-layouts  3.83 us (2%)
  other arithmetic  1.95 us (1%)
  between operations  1.77 us (1%)
    ppermute x8, starting transfers between devices, swap(): return lax.ppermute(v, axis, [(i, i ^ bit) for i in range(size)])  35.7 us
    ppermute x8, waiting for transfers between devices, swap(): return lax.ppermute(v, axis, [(i, i ^ bit) for i in range(size)])  22.2 us
    ppermute x6, starting transfers between devices, ring_x(): return lax.ppermute(v, ('c', 'x'), pairs)  21.5 us
    all_to_all x1, blocking collectives, body(): parts = lax.all_to_all(gp.reshape(64, 4, 2 * HD), ROLL, 0, 0, tiled=True)  17.4 us
    ppermute x4, starting transfers between devices, ring_z(): return lax.ppermute(v, ('z', 'c'), pairs)  15.2 us
    pallas_call x1, Pallas kernels, grads(): pl.pallas_call(grad_kernel, out_shape=[jax.ShapeDtypeStruct((ROWS, GROUP...  12.3 us
    all_to_all x1, starting transfers between devices, body(): lax.all_to_all(jnp.broadcast_to(both[None], (64,) + both.shape), ROLL, 0,...  10.3 us
    all_to_all x1, waiting for transfers between devices, body(): lax.all_to_all(jnp.broadcast_to(both[None], (64,) + both.shape), ROLL, 0,...  9.5 us
  transfers between devices with their start and end apart: 19, of which 7 were waited for; matrix products, arithmetic and copies ran while one was open for 1% of the time, Pallas kernels for 2%

profile of v1, /device:TPU:1, one launch (start us, length us, event | category | flops | bytes accessed | tf_op | source)
XLA Modules:
  0.0 165.5 jit_solution(15535581903148252321)
XLA Ops:
  0.6 4.0 %collective-permute-start.7 = (bf16[80,512]{1,0:T(8,128)(2,1)}, bf16[80,512]{1,0:T(8,128)(2,1)S(1)}, u32[]{:S(2)}, u32[]{:S(2)}) collective-permute-start(bf16[80,512]{1,0:T(8,128)(2,1)} %param.9), channel_id=1, source_target_pairs={{0,16},{16,0},{32,48},{48,32},{1,17},{17,1},{33,49},{49,33},{2,18}... | collective-permute-start | bytes 245768 | tf_op jit(solution)/shard_map/ppermute | solution.py:27
  7.6 4.4 %collective-permute-start.8 = (bf16[160,512]{1,0:T(8,128)(2,1)S(1)}, bf16[160,512]{1,0:T(8,128)(2,1)S(1)}, u32[]{:S(2)}, u32[]{:S(2)}) collective-permute-start(bf16[160,512]{1,0:T(8,128)(2,1)S(1)} %pad_maximum_fusion.2), channel_id=1, source_target_pairs={{0,32},{16,48},{32,0},{48,16},{1,33},{17,49},{33,1},{49,17},{2,34}... | collective-permute-start | bytes 491528 | tf_op jit(solution)/shard_map/ppermute | solution.py:27
  12.0 4.5 %collective-permute-done.8 = bf16[160,512]{1,0:T(8,128)(2,1)S(1)} collective-permute-done((bf16[160,512]{1,0:T(8,128)(2,1)S(1)}, bf16[160,512]{1,0:T(8,128)(2,1)S(1)}, u32[]{:S(2)}, u32[]{:S(2)}) %collective-permute-start.8) | collective-permute-done | bytes 163872 | tf_op jit(solution)/shard_map/ppermute | solution.py:27
  16.6 10.6 %collective-permute-start.9 = (bf16[320,512]{1,0:T(8,128)(2,1)S(1)}, bf16[320,512]{1,0:T(8,128)(2,1)S(1)}, u32[]{:S(2)}, u32[]{:S(2)}) collective-permute-start(bf16[320,512]{1,0:T(8,128)(2,1)S(1)} %pad_maximum_fusion.1), channel_id=1, source_target_pairs={{0,8},{8,0},{1,9},{9,1},{2,10},{10,2},{3,11},{11,3},{4,12},{12,4},... | collective-permute-start | bytes 983048 | tf_op jit(solution)/shard_map/ppermute | solution.py:27
  28.7 6.3 %collective-permute-start.10 = (bf16[640,512]{1,0:T(8,128)(2,1)S(1)}, bf16[640,512]{1,0:T(8,128)(2,1)S(1)}, u32[]{:S(2)}, u32[]{:S(2)}) collective-permute-start(bf16[640,512]{1,0:T(8,128)(2,1)S(1)} %bitcast.11), channel_id=1, source_target_pairs={{0,64},{8,456},{64,128},{72,8},{128,192},{136,72},{192,256},{200,1... | collective-permute-start | bytes 1966088 | tf_op jit(solution)/shard_map/ppermute | solution.py:43
  35.0 7.5 %collective-permute-done.10.refs_9_ = bf16[640,512]{1,0:T(8,128)(2,1)S(1)} collective-permute-done((bf16[640,512]{1,0:T(8,128)(2,1)S(1)}, bf16[640,512]{1,0:T(8,128)(2,1)S(1)}, u32[]{:S(2)}, u32[]{:S(2)}) %collective-permute-start.10) | collective-permute-done | bytes 655392 | tf_op jit(solution)/shard_map/ppermute | solution.py:43
  42.5 5.0 %collective-permute-start.12 = (bf16[640,512]{1,0:T(8,128)(2,1)S(1)}, bf16[640,512]{1,0:T(8,128)(2,1)S(1)}, u32[]{:S(2)}, u32[]{:S(2)}) collective-permute-start(bf16[640,512]{1,0:T(8,128)(2,1)S(1)} %collective-permute-done.10.refs_9_), channel_id=1, source_target_pairs={{0,64},{8,456},{64,128},{72,8},{128,192},{136,72},{192,256},{200,1... | collective-permute-start | bytes 1966088 | tf_op jit(solution)/shard_map/ppermute | solution.py:43
  47.5 4.4 %collective-permute-start = (bf16[384,640]{1,0:T(8,128)(2,1)S(1)}, bf16[384,640]{1,0:T(8,128)(2,1)S(1)}, u32[]{:S(2)}, u32[]{:S(2)}) collective-permute-start(bf16[384,640]{1,0:T(8,128)(2,1)S(1)} %copy-done.5), channel_id=1, source_target_pairs={{0,2},{8,14},{2,4},{10,8},{4,6},{12,10},{6,0},{14,12},{1,3},{9,15}... | collective-permute-start | bytes 1474568 | tf_op jit(solution)/shard_map/ppermute | solution.py:35
  51.9 7.5 %collective-permute-start.3 = (bf16[384,640]{1,0:T(8,128)(2,1)S(1)}, bf16[384,640]{1,0:T(8,128)(2,1)S(1)}, u32[]{:S(2)}, u32[]{:S(2)}) collective-permute-start(bf16[384,640]{1,0:T(8,128)(2,1)S(1)} %copy-done.5), channel_id=1, source_target_pairs={{0,1},{1,0},{2,3},{3,2},{4,5},{5,4},{6,7},{7,6},{8,9},{9,8},{10,11... | collective-permute-start | bytes 1474568 | tf_op jit(solution)/shard_map/ppermute | solution.py:27
  59.4 3.6 %collective-permute-start.1 = (bf16[384,640]{1,0:T(8,128)(2,1)S(1)}, bf16[384,640]{1,0:T(8,128)(2,1)S(1)}, u32[]{:S(2)}, u32[]{:S(2)}) collective-permute-start(bf16[384,640]{1,0:T(8,128)(2,1)S(1)} %collective-permute-done.refs_1_), channel_id=1, source_target_pairs={{0,2},{8,14},{2,4},{10,8},{4,6},{12,10},{6,0},{14,12},{1,3},{9,15}... | collective-permute-start | bytes 1474568 | tf_op jit(solution)/shard_map/ppermute | solution.py:35
  64.9 14.5 %collective-permute-done.3.refs_4_ = bf16[384,640]{1,0:T(8,128)(2,1)S(1)} collective-permute-done((bf16[384,640]{1,0:T(8,128)(2,1)S(1)}, bf16[384,640]{1,0:T(8,128)(2,1)S(1)}, u32[]{:S(2)}, u32[]{:S(2)}) %collective-permute-start.3) | collective-permute-done | bytes 491552 | tf_op jit(solution)/shard_map/ppermute | solution.py:27
  79.4 3.4 %collective-permute-start.4 = (bf16[384,640]{1,0:T(8,128)(2,1)S(1)}, bf16[384,640]{1,0:T(8,128)(2,1)S(1)}, u32[]{:S(2)}, u32[]{:S(2)}) collective-permute-start(bf16[384,640]{1,0:T(8,128)(2,1)S(1)} %collective-permute-done.3.refs_4_), channel_id=1, source_target_pairs={{0,2},{8,14},{2,4},{10,8},{4,6},{12,10},{6,0},{14,12},{1,3},{9,15}... | collective-permute-start | bytes 1474568 | tf_op jit(solution)/shard_map/ppermute | solution.py:35
  82.8 3.2 %collective-permute-start.2 = (bf16[384,640]{1,0:T(8,128)(2,1)S(1)}, bf16[384,640]{1,0:T(8,128)(2,1)S(1)}, u32[]{:S(2)}, u32[]{:S(2)}) collective-permute-start(bf16[384,640]{1,0:T(8,128)(2,1)S(1)} %collective-permute-done.1.refs_2_), channel_id=1, source_target_pairs={{0,2},{8,14},{2,4},{10,8},{4,6},{12,10},{6,0},{14,12},{1,3},{9,15}... | collective-permute-start | bytes 1474568 | tf_op jit(solution)/shard_map/ppermute | solution.py:35
  86.0 2.9 %collective-permute-done.4.refs_5_ = bf16[384,640]{1,0:T(8,128)(2,1)S(1)} collective-permute-done((bf16[384,640]{1,0:T(8,128)(2,1)S(1)}, bf16[384,640]{1,0:T(8,128)(2,1)S(1)}, u32[]{:S(2)}, u32[]{:S(2)}) %collective-permute-start.4) | collective-permute-done | bytes 491552 | tf_op jit(solution)/shard_map/ppermute | solution.py:35
  89.0 4.6 %collective-permute-start.5 = (bf16[384,640]{1,0:T(8,128)(2,1)S(1)}, bf16[384,640]{1,0:T(8,128)(2,1)}, u32[]{:S(2)}, u32[]{:S(2)}) collective-permute-start(bf16[384,640]{1,0:T(8,128)(2,1)S(1)} %collective-permute-done.4.refs_5_), channel_id=1, source_target_pairs={{0,2},{8,14},{2,4},{10,8},{4,6},{12,10},{6,0},{14,12},{1,3},{9,15}... | collective-permute-start | bytes 1474568 | tf_op jit(solution)/shard_map/ppermute | solution.py:35
  95.7 2.4 %collective-permute-start.11 = (bf16[640,512]{1,0:T(8,128)(2,1)S(1)}, bf16[640,512]{1,0:T(8,128)(2,1)S(1)}, u32[]{:S(2)}, u32[]{:S(2)}) collective-permute-start(bf16[640,512]{1,0:T(8,128)(2,1)S(1)} %collective-permute-done.10.refs_9_), channel_id=1, source_target_pairs={{0,8},{8,0},{1,9},{9,1},{2,10},{10,2},{3,11},{11,3},{4,12},{12,4},... | collective-permute-start | bytes 1966088 | tf_op jit(solution)/shard_map/ppermute | solution.py:27
  100.1 2.4 %collective-permute-start.15 = (bf16[640,512]{1,0:T(8,128)(2,1)S(1)}, bf16[640,512]{1,0:T(8,128)(2,1)}, u32[]{:S(2)}, u32[]{:S(2)}) collective-permute-start(bf16[640,512]{1,0:T(8,128)(2,1)S(1)} %collective-permute-done.14.refs_13_), channel_id=1, source_target_pairs={{0,8},{8,0},{1,9},{9,1},{2,10},{10,2},{3,11},{11,3},{4,12},{12,4},... | collective-permute-start | bytes 1966088 | tf_op jit(solution)/shard_map/ppermute | solution.py:27
  102.4 2.4 %collective-permute-start.6 = (bf16[384,640]{1,0:T(8,128)(2,1)}, bf16[384,640]{1,0:T(8,128)(2,1)}, u32[]{:S(2)}, u32[]{:S(2)}) collective-permute-start(bf16[384,640]{1,0:T(8,128)(2,1)} %collective-permute-done.5.refs_6_), channel_id=1, source_target_pairs={{0,2},{8,14},{2,4},{10,8},{4,6},{12,10},{6,0},{14,12},{1,3},{9,15}... | collective-permute-start | bytes 1474568 | tf_op jit(solution)/shard_map/ppermute | solution.py:35
  104.8 2.6 %collective-permute-start.17 = (bf16[320,512]{1,0:T(8,128)(2,1)}, bf16[320,512]{1,0:T(8,128)(2,1)}, u32[]{:S(2)}, u32[]{:S(2)}) collective-permute-start(bf16[320,512]{1,0:T(8,128)(2,1)} %collective-permute-done.16.refs_15_), channel_id=1, source_target_pairs={{0,8},{8,0},{1,9},{9,1},{2,10},{10,2},{3,11},{11,3},{4,12},{12,4},... | collective-permute-start | bytes 983048 | tf_op jit(solution)/shard_map/ppermute | solution.py:27
  108.1 10.3 %all-to-all-start = ((bf16[64,4,256]{2,1,0:T(4,128)(2,1)}), bf16[64,4,256]{2,1,0:T(4,128)(2,1)S(1)}, u32[]{:S(2)}, u32[]{:S(2)}) async-start(bf16[64,4,256]{2,1,0:T(4,128)(2,1)} %broadcast_in_dim.2), calls=%async_computation | async-start | bytes 262144 | tf_op jit(solution)/shard_map/all_to_all | solution.py:205
  119.8 9.5 %all-to-all-done = bf16[64,4,256]{2,1,0:T(4,128)(2,1)S(1)} async-done(((bf16[64,4,256]{2,1,0:T(4,128)(2,1)}), bf16[64,4,256]{2,1,0:T(4,128)(2,1)S(1)}, u32[]{:S(2)}, u32[]{:S(2)}) %all-to-all-start) | async-done | bytes 131104 | tf_op jit(solution)/shard_map/all_to_all | solution.py:205
  130.0 3.4 %soft.1 = (bf16[384,512]{1,0:T(8,128)(2,1)}, bf16[512,512]{1,0:T(8,128)(2,1)}, bf16[640,512]{1,0:T(8,128)(2,1)}) custom-call(bf16[384,512]{1,0:T(8,128)(2,1)} %refs_20_.1, bf16[384,128]{1,0:T(8,128)(2,1)} %refs_21_.1, bf16[256,256]{1,0:T(8,128)(2,1)} %reshape.67.pkv_ref.refs_23_), custom_call_target="tpu_custom_call" | custom-call | flops 251658240 | bytes 3000000 | tf_op jit(solution)/shard_map/soft/pallas_call | solution.py:162
  134.2 12.3 %grads.1 = (bf16[384,512]{1,0:T(8,128)(2,1)}, bf16[384,128]{1,0:T(8,128)(2,1)}, bf16[384,128]{1,0:T(8,128)(2,1)}, f32[256,256]{1,0:T(8,128)}) custom-call(s32[4]{0:T(128)} %pad_add_fusion.place_ref, s32[1]{0:T(128)S(6)} %copy.15.length_ref, bf16[384,640]{1,0:T(8,128)(2,1)} %refs_0_.1, bf16[384,640]{1,0:T(8,128)(2,1)} %copy-done.6, ...), custom_call_target="tpu_custom_call" | custom-call | flops 2013265920 | bytes 14000000 | tf_op jit(solution)/shard_map/grads/pallas_call | solution.py:177
  147.5 17.4 %all_to_all.10 = f32[64,4,256]{2,1,0:T(4,128)S(1)} all-to-all(f32[64,4,256]{2,1,0:T(4,128)S(1)} %reshape.68), channel_id=1, replica_groups=mesh['z'=8,'yl'=4,'c'=2,'x'=4,'yh'=2] {'z','yl','c'}, dimensions={0} | all-to-all | bytes 524288 | tf_op jit(solution)/shard_map/all_to_all | solution.py:236
  (57 shorter events, 15.0 us)
Async XLA Ops:
  0.6 6.1 %collective-permute-start.7 = (bf16[80,512]{1,0:T(8,128)(2,1)}, bf16[80,512]{1,0:T(8,128)(2,1)S(1)}, u32[]{:S(2)}, u32[]{:S(2)}) collective-permute-start(bf16[80,512]{1,0:T(8,128)(2,1)} %param.9), channel_id=1, source_target_pairs={{0,16},{16,0},{32,48},{48,32},{1,17},{17,1},{33,49},{49,33},{2,18}... | collective-permute-start | bytes 245768 | tf_op jit(solution)/shard_map/ppermute | solution.py:27
  7.6 8.9 %collective-permute-start.8 = (bf16[160,512]{1,0:T(8,128)(2,1)S(1)}, bf16[160,512]{1,0:T(8,128)(2,1)S(1)}, u32[]{:S(2)}, u32[]{:S(2)}) collective-permute-start(bf16[160,512]{1,0:T(8,128)(2,1)S(1)} %pad_maximum_fusion.2), channel_id=1, source_target_pairs={{0,32},{16,48},{32,0},{48,16},{1,33},{17,49},{33,1},{49,17},{2,34}... | collective-permute-start | bytes 491528 | tf_op jit(solution)/shard_map/ppermute | solution.py:27
  16.6 11.9 %collective-permute-start.9 = (bf16[320,512]{1,0:T(8,128)(2,1)S(1)}, bf16[320,512]{1,0:T(8,128)(2,1)S(1)}, u32[]{:S(2)}, u32[]{:S(2)}) collective-permute-start(bf16[320,512]{1,0:T(8,128)(2,1)S(1)} %pad_maximum_fusion.1), channel_id=1, source_target_pairs={{0,8},{8,0},{1,9},{9,1},{2,10},{10,2},{3,11},{11,3},{4,12},{12,4},... | collective-permute-start | bytes 983048 | tf_op jit(solution)/shard_map/ppermute | solution.py:27
  28.7 79.5 %copy-start = (bf16[4,2,80,512]{3,2,1,0:T(8,128)(2,1)}, bf16[4,2,80,512]{3,2,1,0:T(8,128)(2,1)S(1)}, u32[]{:S(2)}) copy-start(bf16[4,2,80,512]{3,2,1,0:T(8,128)(2,1)S(1)} %pad_maximum_fusion) | copy-start | bytes 1966084
  28.7 78.7 %copy-start.11 = (bf16[4,128]{1,0:T(4,128)(2,1)S(1)}, bf16[4,128]{1,0:T(4,128)(2,1)}, u32[]{:S(2)}) copy-start(bf16[4,128]{1,0:T(4,128)(2,1)} %param.14) | copy-start | bytes 3076
  28.7 78.7 %copy-start.12 = (bf16[4,128]{1,0:T(4,128)(2,1)S(1)}, bf16[4,128]{1,0:T(4,128)(2,1)}, u32[]{:S(2)}) copy-start(bf16[4,128]{1,0:T(4,128)(2,1)} %param.13) | copy-start | bytes 3076
  28.7 13.8 %collective-permute-start.10 = (bf16[640,512]{1,0:T(8,128)(2,1)S(1)}, bf16[640,512]{1,0:T(8,128)(2,1)S(1)}, u32[]{:S(2)}, u32[]{:S(2)}) collective-permute-start(bf16[640,512]{1,0:T(8,128)(2,1)S(1)} %bitcast.11), channel_id=1, source_target_pairs={{0,64},{8,456},{64,128},{72,8},{128,192},{136,72},{192,256},{200,1... | collective-permute-start | bytes 1966088 | tf_op jit(solution)/shard_map/ppermute | solution.py:43
  42.5 90.9 %copy-start.2 = (bf16[640,512]{1,0:T(8,128)(2,1)}, bf16[640,512]{1,0:T(8,128)(2,1)S(1)}, u32[]{:S(2)}) copy-start(bf16[640,512]{1,0:T(8,128)(2,1)S(1)} %collective-permute-done.10.refs_9_) | copy-start | bytes 1966084
  42.5 20.5 %collective-permute-start.12 = (bf16[640,512]{1,0:T(8,128)(2,1)S(1)}, bf16[640,512]{1,0:T(8,128)(2,1)S(1)}, u32[]{:S(2)}, u32[]{:S(2)}) collective-permute-start(bf16[640,512]{1,0:T(8,128)(2,1)S(1)} %collective-permute-done.10.refs_9_), channel_id=1, source_target_pairs={{0,64},{8,456},{64,128},{72,8},{128,192},{136,72},{192,256},{200,1... | collective-permute-start | bytes 1966088 | tf_op jit(solution)/shard_map/ppermute | solution.py:43
  47.5 11.9 %collective-permute-start = (bf16[384,640]{1,0:T(8,128)(2,1)S(1)}, bf16[384,640]{1,0:T(8,128)(2,1)S(1)}, u32[]{:S(2)}, u32[]{:S(2)}) collective-permute-start(bf16[384,640]{1,0:T(8,128)(2,1)S(1)} %copy-done.5), channel_id=1, source_target_pairs={{0,2},{8,14},{2,4},{10,8},{4,6},{12,10},{6,0},{14,12},{1,3},{9,15}... | collective-permute-start | bytes 1474568 | tf_op jit(solution)/shard_map/ppermute | solution.py:35
  51.9 27.5 %collective-permute-start.3 = (bf16[384,640]{1,0:T(8,128)(2,1)S(1)}, bf16[384,640]{1,0:T(8,128)(2,1)S(1)}, u32[]{:S(2)}, u32[]{:S(2)}) collective-permute-start(bf16[384,640]{1,0:T(8,128)(2,1)S(1)} %copy-done.5), channel_id=1, source_target_pairs={{0,1},{1,0},{2,3},{3,2},{4,5},{5,4},{6,7},{7,6},{8,9},{9,8},{10,11... | collective-permute-start | bytes 1474568 | tf_op jit(solution)/shard_map/ppermute | solution.py:27
  59.4 23.4 %collective-permute-start.1 = (bf16[384,640]{1,0:T(8,128)(2,1)S(1)}, bf16[384,640]{1,0:T(8,128)(2,1)S(1)}, u32[]{:S(2)}, u32[]{:S(2)}) collective-permute-start(bf16[384,640]{1,0:T(8,128)(2,1)S(1)} %collective-permute-done.refs_1_), channel_id=1, source_target_pairs={{0,2},{8,14},{2,4},{10,8},{4,6},{12,10},{6,0},{14,12},{1,3},{9,15}... | collective-permute-start | bytes 1474568 | tf_op jit(solution)/shard_map/ppermute | solution.py:35
  63.0 70.4 %copy-start.3 = (bf16[640,512]{1,0:T(8,128)(2,1)}, bf16[640,512]{1,0:T(8,128)(2,1)S(1)}, u32[]{:S(2)}) copy-start(bf16[640,512]{1,0:T(8,128)(2,1)S(1)} %collective-permute-done.12.refs_11_) | copy-start | bytes 1966084
  63.0 30.6 %collective-permute-start.14 = (bf16[640,512]{1,0:T(8,128)(2,1)S(1)}, bf16[640,512]{1,0:T(8,128)(2,1)S(1)}, u32[]{:S(2)}, u32[]{:S(2)}) collective-permute-start(bf16[640,512]{1,0:T(8,128)(2,1)S(1)} %collective-permute-done.12.refs_11_), channel_id=1, source_target_pairs={{0,64},{8,456},{64,128},{72,8},{128,192},{136,72},{192,256},{200,1... | collective-permute-start | bytes 1966088 | tf_op jit(solution)/shard_map/ppermute | solution.py:43
  79.4 9.6 %collective-permute-start.4 = (bf16[384,640]{1,0:T(8,128)(2,1)S(1)}, bf16[384,640]{1,0:T(8,128)(2,1)S(1)}, u32[]{:S(2)}, u32[]{:S(2)}) collective-permute-start(bf16[384,640]{1,0:T(8,128)(2,1)S(1)} %collective-permute-done.3.refs_4_), channel_id=1, source_target_pairs={{0,2},{8,14},{2,4},{10,8},{4,6},{12,10},{6,0},{14,12},{1,3},{9,15}... | collective-permute-start | bytes 1474568 | tf_op jit(solution)/shard_map/ppermute | solution.py:35
  82.8 17.2 %collective-permute-start.2 = (bf16[384,640]{1,0:T(8,128)(2,1)S(1)}, bf16[384,640]{1,0:T(8,128)(2,1)S(1)}, u32[]{:S(2)}, u32[]{:S(2)}) collective-permute-start(bf16[384,640]{1,0:T(8,128)(2,1)S(1)} %collective-permute-done.1.refs_2_), channel_id=1, source_target_pairs={{0,2},{8,14},{2,4},{10,8},{4,6},{12,10},{6,0},{14,12},{1,3},{9,15}... | collective-permute-start | bytes 1474568 | tf_op jit(solution)/shard_map/ppermute | solution.py:35
  89.0 13.4 %collective-permute-start.5 = (bf16[384,640]{1,0:T(8,128)(2,1)S(1)}, bf16[384,640]{1,0:T(8,128)(2,1)}, u32[]{:S(2)}, u32[]{:S(2)}) collective-permute-start(bf16[384,640]{1,0:T(8,128)(2,1)S(1)} %collective-permute-done.4.refs_5_), channel_id=1, source_target_pairs={{0,2},{8,14},{2,4},{10,8},{4,6},{12,10},{6,0},{14,12},{1,3},{9,15}... | collective-permute-start | bytes 1474568 | tf_op jit(solution)/shard_map/ppermute | solution.py:35
  93.6 11.2 %collective-permute-start.16 = (bf16[320,512]{1,0:T(8,128)(2,1)S(1)}, bf16[320,512]{1,0:T(8,128)(2,1)}, u32[]{:S(2)}, u32[]{:S(2)}) collective-permute-start(bf16[320,512]{1,0:T(8,128)(2,1)S(1)} %slice_select_fusion), channel_id=1, source_target_pairs={{0,64},{8,456},{64,128},{72,8},{128,192},{136,72},{192,256},{200,1... | collective-permute-start | bytes 983048 | tf_op jit(solution)/shard_map/ppermute | solution.py:43
  95.7 37.7 %collective-permute-start.11 = (bf16[640,512]{1,0:T(8,128)(2,1)S(1)}, bf16[640,512]{1,0:T(8,128)(2,1)S(1)}, u32[]{:S(2)}, u32[]{:S(2)}) collective-permute-start(bf16[640,512]{1,0:T(8,128)(2,1)S(1)} %collective-permute-done.10.refs_9_), channel_id=1, source_target_pairs={{0,8},{8,0},{1,9},{9,1},{2,10},{10,2},{3,11},{11,3},{4,12},{12,4},... | collective-permute-start | bytes 1966088 | tf_op jit(solution)/shard_map/ppermute | solution.py:27
  98.0 35.3 %collective-permute-start.13 = (bf16[640,512]{1,0:T(8,128)(2,1)S(1)}, bf16[640,512]{1,0:T(8,128)(2,1)}, u32[]{:S(2)}, u32[]{:S(2)}) collective-permute-start(bf16[640,512]{1,0:T(8,128)(2,1)S(1)} %collective-permute-done.12.refs_11_), channel_id=1, source_target_pairs={{0,8},{8,0},{1,9},{9,1},{2,10},{10,2},{3,11},{11,3},{4,12},{12,4},... | collective-permute-start | bytes 1966088 | tf_op jit(solution)/shard_map/ppermute | solution.py:27
  100.1 33.3 %collective-permute-start.15 = (bf16[640,512]{1,0:T(8,128)(2,1)S(1)}, bf16[640,512]{1,0:T(8,128)(2,1)}, u32[]{:S(2)}, u32[]{:S(2)}) collective-permute-start(bf16[640,512]{1,0:T(8,128)(2,1)S(1)} %collective-permute-done.14.refs_13_), channel_id=1, source_target_pairs={{0,8},{8,0},{1,9},{9,1},{2,10},{10,2},{3,11},{11,3},{4,12},{12,4},... | collective-permute-start | bytes 1966088 | tf_op jit(solution)/shard_map/ppermute | solution.py:27
  102.4 30.9 %collective-permute-start.6 = (bf16[384,640]{1,0:T(8,128)(2,1)}, bf16[384,640]{1,0:T(8,128)(2,1)}, u32[]{:S(2)}, u32[]{:S(2)}) collective-permute-start(bf16[384,640]{1,0:T(8,128)(2,1)} %collective-permute-done.5.refs_6_), channel_id=1, source_target_pairs={{0,2},{8,14},{2,4},{10,8},{4,6},{12,10},{6,0},{14,12},{1,3},{9,15}... | collective-permute-start | bytes 1474568 | tf_op jit(solution)/shard_map/ppermute | solution.py:35
  104.8 28.5 %collective-permute-start.17 = (bf16[320,512]{1,0:T(8,128)(2,1)}, bf16[320,512]{1,0:T(8,128)(2,1)}, u32[]{:S(2)}, u32[]{:S(2)}) collective-permute-start(bf16[320,512]{1,0:T(8,128)(2,1)} %collective-permute-done.16.refs_15_), channel_id=1, source_target_pairs={{0,8},{8,0},{1,9},{9,1},{2,10},{10,2},{3,11},{11,3},{4,12},{12,4},... | collective-permute-start | bytes 983048 | tf_op jit(solution)/shard_map/ppermute | solution.py:27
  108.1 21.1 %all-to-all-start = ((bf16[64,4,256]{2,1,0:T(4,128)(2,1)}), bf16[64,4,256]{2,1,0:T(4,128)(2,1)S(1)}, u32[]{:S(2)}, u32[]{:S(2)}) async-start(bf16[64,4,256]{2,1,0:T(4,128)(2,1)} %broadcast_in_dim.2), calls=%async_computation | async-start | bytes 262144 | tf_op jit(solution)/shard_map/all_to_all | solution.py:205
  (8 other events, 108.7 us)

commit v2 on v1

v2 whole, which is shorter than its diff:
```python
import jax
import jax.numpy as jnp
from jax import lax
from jax.experimental import pallas as pl
from jax.experimental.pallas import tpu as pltpu
from jax.sharding import Mesh
from jax.sharding import PartitionSpec as P

HD = 128
ROWS = 384
BLOCK = 128
GROUP = 4
PREFIX = 256
SCALE = HD**-0.5
F32 = jnp.float32
BF16 = jnp.bfloat16
ROLL = ("z", "yl", "c")
TENSOR = ("x", "yh")
NZ, NY, NX = 8, 4, 4
NT = (((1,), (1,)), ((), ()))


def swap(v, axis, bit=1):
    size = lax.axis_size(axis)
    return lax.ppermute(v, axis, [(i, i ^ bit) for i in range(size)])


def ring_x(v):
    pairs = []
    for x in range(NX):
        pairs.append((x, (x + 1) % NX))
        pairs.append((NX + x, NX + (x - 1) % NX))
    return lax.ppermute(v, ("c", "x"), pairs)


def ring_z(v):
    pairs = []
    for z in range(NZ):
        pairs.append((2 * z, 2 * ((z + 1) % NZ)))
        pairs.append((2 * z + 1, 2 * ((z - 1) % NZ) + 1))
    return lax.ppermute(v, ("z", "c"), pairs)


def in_pair(mine, other, bit, axis):
    first = jnp.where(bit == 0, mine, other)
    second = jnp.where(bit == 0, other, mine)
    return jnp.concatenate([first, second], axis=axis)


def stacked(ref, i):
    rows = slice(BLOCK * i, BLOCK * (i + 1))
    return jnp.concatenate([ref[rows, HD * h : HD * (h + 1)] for h in range(GROUP)], axis=0)


def soft_kernel(q_ref, rk_ref, pkv_ref, *p_refs):
    keys = jnp.concatenate([pkv_ref[:, :HD], rk_ref[...]], axis=0)
    for i, p_ref in enumerate(p_refs):
        low = PREFIX + BLOCK * i
        scores = (
            lax.dot_general(keys[: low + BLOCK], stacked(q_ref, i), NT, preferred_element_type=F32)
            * SCALE
        )
        open_part = scores[:low]
        key_place = lax.broadcasted_iota(jnp.int32, (BLOCK, GROUP * BLOCK), 0)
        row_place = lax.broadcasted_iota(jnp.int32, (BLOCK, GROUP * BLOCK), 1) % BLOCK
        edge = jnp.where(key_place <= row_place, scores[low:], -jnp.inf)
        top = jnp.maximum(
            jnp.max(open_part, axis=0, keepdims=True), jnp.max(edge, axis=0, keepdims=True)
        )
        open_part = jnp.exp(open_part - top)
        edge = jnp.exp(edge - top)
        total = jnp.sum(open_part, axis=0, keepdims=True) + jnp.sum(edge, axis=0, keepdims=True)
        share = 1.0 / total
        p_ref[:low] = open_part * share
        p_ref[low:] = edge * share


def project_kernel(place_ref, *refs):
    g_in, w_in = refs[:7], refs[7:16]
    acc, w_last = refs[16:18]
    g_buf, w_buf, sem = refs[18:]
    x, yh, z, core = place_ref[0], place_ref[1], place_ref[2], place_ref[3]
    way = 1 - 2 * core
    w_copies = []
    for k, src in enumerate(w_in):
        if k < 7:
            step = (k + 1) // 2
            sign = way if k % 2 == 0 else -way
            dst = w_buf.at[lax.rem(z + step * sign + 8, 8)]
        else:
            half = core if k == 7 else 1 - core
            dst = w_buf.at[lax.rem(z + 4, 8), pl.ds(pl.multiple_of(320 * half, 320), 320)]
        w_copies.append(pltpu.make_async_copy(src, dst, sem.at[k]))
    g_copies = [
        pltpu.make_async_copy(src, g_buf.at[k], sem.at[9 + k]) for k, src in enumerate(g_in)
    ]
    for c in w_copies + g_copies:
        c.start()
    for c in w_copies + g_copies:
        c.wait()

    def block_of(k):
        side = jnp.where(k < 4, yh, 1 - yh)
        return 2 * lax.rem(x - lax.rem(k, 4) * way + 8, 4) + side

    acc[...] = jnp.dot(g_buf[0], w_buf[block_of(0)], preferred_element_type=F32)

    def project(k, _):
        acc[...] += jnp.dot(g_buf[k], w_buf[block_of(k)], preferred_element_type=F32)
        return 0

    lax.fori_loop(1, 7, project, 0)
    w_last[...] = w_buf[block_of(7)]


def front_kernel(length_ref, acc, g_last, w_last, p0, p1, p2, q_ref, rv_ref, pkv_ref, gp_ref, og_ref, s0, s1, s2):
    total = acc[...] + jnp.dot(g_last[...], w_last[...], preferred_element_type=F32)
    row = lax.broadcasted_iota(jnp.int32, (ROWS, GROUP * HD), 0)
    out_grad = jnp.where(row < length_ref[0], total, 0.0).astype(BF16)
    for i in range(3):
        for h in range(GROUP):
            at = GROUP * BLOCK * i + BLOCK * h
            og_ref[at : at + BLOCK] = out_grad[
                BLOCK * i : BLOCK * (i + 1), HD * h : HD * (h + 1)
            ]
    values = jnp.concatenate([pkv_ref[:, HD:], rv_ref[...]], axis=0)
    key_grad = jnp.zeros((PREFIX, HD), F32)
    value_grad = jnp.zeros((PREFIX, HD), F32)
    for i, (p_ref, s_ref) in enumerate(zip((p0, p1, p2), (s0, s1, s2))):
        width = PREFIX + BLOCK * (i + 1)
        grads = og_ref[GROUP * BLOCK * i : GROUP * BLOCK * (i + 1)]
        prob_grad = lax.dot_general(values[:width], grads, NT, preferred_element_type=F32)
        weights = p_ref[...]
        delta = jnp.sum(weights * prob_grad, axis=0, keepdims=True)
        score_low = (weights * (prob_grad - delta) * SCALE).astype(BF16)
        s_ref[...] = score_low
        key_grad += jnp.dot(score_low[:PREFIX], stacked(q_ref, i), preferred_element_type=F32)
        value_grad += jnp.dot(weights[:PREFIX].astype(BF16), grads, preferred_element_type=F32)
    for j in range(PREFIX // 4):
        gp_ref[j, :, :HD] = key_grad[4 * j : 4 * j + 4]
        gp_ref[j, :, HD:] = value_grad[4 * j : 4 * j + 4]


def back_kernel(og_ref, s0, s1, s2, p0, p1, p2, q_ref, rk_ref, pkv_ref, gq_ref, grk_ref, grv_ref):
    keys = jnp.concatenate([pkv_ref[:, :HD], rk_ref[...]], axis=0)
    keys_t = keys.astype(F32).T.astype(BF16)
    key_grad = [None] * 3
    value_grad = [None] * 3
    for i, (p_ref, s_ref) in enumerate(zip((p0, p1, p2), (s0, s1, s2))):
        width = PREFIX + BLOCK * (i + 1)
        rows = slice(BLOCK * i, BLOCK * (i + 1))
        score_low = s_ref[...]
        weights = p_ref[PREFIX:].astype(BF16)
        grads = og_ref[GROUP * BLOCK * i : GROUP * BLOCK * (i + 1)]
        kg = jnp.dot(score_low[PREFIX:], stacked(q_ref, i), preferred_element_type=F32)
        vg = jnp.dot(weights, grads, preferred_element_type=F32)
        qt = jnp.dot(keys_t[:, :width], score_low, preferred_element_type=F32)
        for h in range(GROUP):
            gq_ref[rows, HD * h : HD * (h + 1)] = qt[:, BLOCK * h : BLOCK * (h + 1)].T.astype(BF16)
        for j in range(i + 1):
            part = slice(BLOCK * j, BLOCK * (j + 1))
            key_grad[j] = kg[part] if key_grad[j] is None else key_grad[j] + kg[part]
            value_grad[j] = vg[part] if value_grad[j] is None else value_grad[j] + vg[part]
    for j in range(3):
        rows = slice(BLOCK * j, BLOCK * (j + 1))
        grk_ref[rows] = key_grad[j].astype(BF16)
        grv_ref[rows] = value_grad[j].astype(BF16)


VM = pl.BlockSpec(memory_space=pltpu.VMEM)
SM = pl.BlockSpec(memory_space=pltpu.SMEM)
ANY = pl.BlockSpec(memory_space=pl.ANY)
WIDTHS = tuple(PREFIX + BLOCK * (i + 1) for i in range(3))


def call(kernel, outs, in_specs, args, flops, scratch=()):
    return pl.pallas_call(
        kernel,
        out_shape=[jax.ShapeDtypeStruct(s, d) for s, d in outs],
        in_specs=in_specs,
        out_specs=[VM] * len(outs),
        scratch_shapes=scratch,
        cost_estimate=pl.CostEstimate(flops=flops, bytes_accessed=4000000, transcendentals=0),
    )(*args)


def soft(queries, resp_key, prefix):
    outs = [((w, GROUP * BLOCK), F32) for w in WIDTHS]
    return call(soft_kernel, outs, [VM] * 3, (queries, resp_key, prefix), 1 << 30)


def project(place, g, w):
    return call(
        project_kernel,
        [((ROWS, 512), F32), ((640, 512), BF16)],
        [SM] + [ANY] * 16,
        (place, *g, *w),
        2 * 384 * 5120 * 512,
        [
            pltpu.VMEM((7, ROWS, 640), BF16),
            pltpu.VMEM((8, 640, 512), BF16),
            pltpu.SemaphoreType.DMA((16,)),
        ],
    )


def front(lengths, acc, g_last, w_last, p, queries, resp_value, prefix):
    outs = [((64, 4, 2 * HD), F32), ((GROUP * ROWS, HD), BF16)]
    outs += [((w, GROUP * BLOCK), BF16) for w in WIDTHS]
    args = (lengths, acc, g_last, w_last, *p, queries, resp_value, prefix)
    return call(front_kernel, outs, [SM] + [VM] * 9, args, 1 << 30)


def back(og, s, p, queries, resp_key, prefix):
    outs = [((ROWS, GROUP * HD), BF16), ((ROWS, HD), BF16), ((ROWS, HD), BF16)]
    return call(back_kernel, outs, [VM] * 10, (og, *s, *p, queries, resp_key, prefix), 1 << 30)


def steps(grad_out, out_weight, queries, resp_key, resp_value, prefix_key, prefix_value, lengths):
    x, yh = lax.axis_index("x"), lax.axis_index("yh")
    z, yl, core = lax.axis_index("z"), lax.axis_index("yl"), lax.axis_index("c")
    both = jnp.concatenate([prefix_key, prefix_value], axis=1)
    prefix = lax.all_to_all(
        jnp.broadcast_to(both[None], (64,) + both.shape), ROLL, 0, 0, tiled=True
    ).reshape(PREFIX, 2 * HD)

    g = [grad_out]
    for _ in range(3):
        g.append(ring_x(g[-1]))
    g.append(swap(grad_out, "yh"))
    for _ in range(3):
        g.append(ring_x(g[-1]))

    two = in_pair(out_weight, swap(out_weight, "yl", 1), yl % 2, 0)
    four = in_pair(two, swap(two, "yl", 2), yl // 2, 0)
    piece = in_pair(
        four.reshape(4, 1, 80, 512),
        swap(four, "c").reshape(4, 1, 80, 512),
        core,
        1,
    ).reshape(640, 512)
    w = [piece]
    ahead = piece
    for _ in range(3):
        ahead = ring_z(ahead)
        w += [ahead, swap(ahead, "c")]
    half = jnp.where(core == 0, ahead[:320], ahead[320:])
    last = ring_z(half)
    w += [last, swap(last, "c")]

    p = soft(queries, resp_key, prefix)
    place = jnp.stack([x, yh, z, core]).astype(jnp.int32)
    acc, w_last = project(place, g[:7], w)
    gp, og, *s = front(lengths, acc, g[7], w_last, p, queries, resp_value, prefix)
    parts = lax.all_to_all(gp, ROLL, 0, 0, tiled=True)
    gq, grk, grv = back(og, s, p, queries, resp_key, prefix)
    total = jnp.sum(parts, axis=0)
    return gq, grk, grv, total[:, :HD], total[:, HD:]


def solution(mesh):
    torus = Mesh(mesh.devices.reshape(NZ, NY, 2, NX, 2), ROLL + TENSOR)
    placed = P(ROLL, TENSOR)
    return jax.shard_map(
        steps,
        mesh=torus,
        in_specs=(placed,) * 7 + (P(ROLL),),
        out_specs=(placed,) * 5,
        check_vma=False,
    )
```

time: 166 us -> 169 us (1.018)
  blocking collectives: 17.4 us -> 0 us
  starting transfers between devices: 82.8 us -> 92 us
  Pallas kernels: 15.6 us -> 22.3 us
  waiting for transfers between devices: 42.2 us -> 45.9 us
    all_to_all x1 -> x0, blocking collectives: 17.4 us -> none  [body(): parts = lax.all_to_all(gp.reshape(64, 4, 2 * HD), ROLL, 0, 0, tiled=True)]
    pallas_call x2 -> x4, Pallas kernels: 15.6 us -> 22.3 us  [call(): pl.pallas_call(kernel, out_shape=[jax.ShapeDtypeStruct(s, d) for s, d in...]
    all_to_all x1 -> x2, starting transfers between devices: 10.3 us -> 15.6 us  [the longest x1 7.84 us: steps(): lax.all_to_all(jnp.broadcast_to(both[None], (64,) + both.shape), ROLL, 0,...]
    ppermute x6, starting transfers between devices: 21.5 us -> 25.3 us  [ring_x(): return lax.ppermute(v, ('c', 'x'), pairs)]
    all_to_all x1 -> x2, waiting for transfers between devices: 9.5 us -> 11.8 us  [the longest x1 9.22 us: steps(): parts = lax.all_to_all(gp, ROLL, 0, 0, tiled=True)]
    ppermute x8, waiting for transfers between devices: 22.2 us -> 24.3 us  [swap(): return lax.ppermute(v, axis, [(i, i ^ bit) for i in range(size)])]
  transfers between devices with their start and end apart: 19 -> 20, of which waited for: 7 -> 9; matrix products, arithmetic and copies ran while one was open for 1% -> 2% of each run, Pallas kernels for 2% -> 10%
where the time goes in v2:
time: 169 us; the launch traced here: 168 us
  starting transfers between devices  92 us (54%)
  waiting for transfers between devices  45.9 us (27%)
  Pallas kernels  22.3 us (13%)
  local copies, waits for them, and re-layouts  3.59 us (2%)
  other arithmetic  2.68 us (2%)
  between operations  1.76 us (1%)
    ppermute x8, starting transfers between devices, swap(): return lax.ppermute(v, axis, [(i, i ^ bit) for i in range(size)])  35.1 us
    ppermute x6, starting transfers between devices, ring_x(): return lax.ppermute(v, ('c', 'x'), pairs)  25.3 us
    ppermute x8, waiting for transfers between devices, swap(): return lax.ppermute(v, axis, [(i, i ^ bit) for i in range(size)])  24.3 us
    pallas_call x4, Pallas kernels, call(): pl.pallas_call(kernel, out_shape=[jax.ShapeDtypeStruct(s, d) for s, d in...  22.3 us
    ppermute x4, starting transfers between devices, ring_z(): return lax.ppermute(v, ('z', 'c'), pairs)  16 us
    all_to_all x1, waiting for transfers between devices, steps(): parts = lax.all_to_all(gp, ROLL, 0, 0, tiled=True)  9.22 us
    all_to_all x1, starting transfers between devices, steps(): lax.all_to_all(jnp.broadcast_to(both[None], (64,) + both.shape), ROLL, 0,...  7.84 us
    all_to_all x1, starting transfers between devices, steps(): parts = lax.all_to_all(gp, ROLL, 0, 0, tiled=True)  7.71 us
  transfers between devices with their start and end apart: 20, of which 9 were waited for; matrix products, arithmetic and copies ran while one was open for 2% of the time, Pallas kernels for 10%

profile of v2, /device:TPU:1, one launch (start us, length us, event | category | flops | bytes accessed | tf_op | source)
XLA Modules:
  0.0 168.1 jit_solution(10437437205212971581)
XLA Ops:
  0.6 4.0 %collective-permute-start.6 = (bf16[80,512]{1,0:T(8,128)(2,1)}, bf16[80,512]{1,0:T(8,128)(2,1)S(1)}, u32[]{:S(2)}, u32[]{:S(2)}) collective-permute-start(bf16[80,512]{1,0:T(8,128)(2,1)} %param.9), channel_id=1, source_target_pairs={{0,16},{16,0},{32,48},{48,32},{1,17},{17,1},{33,49},{49,33},{2,18}... | collective-permute-start | bytes 245768 | tf_op jit(solution)/shard_map/ppermute | solution.py:25
  7.6 4.4 %collective-permute-start.7 = (bf16[160,512]{1,0:T(8,128)(2,1)S(1)}, bf16[160,512]{1,0:T(8,128)(2,1)S(1)}, u32[]{:S(2)}, u32[]{:S(2)}) collective-permute-start(bf16[160,512]{1,0:T(8,128)(2,1)S(1)} %pad_maximum_fusion.2), channel_id=1, source_target_pairs={{0,32},{16,48},{32,0},{48,16},{1,33},{17,49},{33,1},{49,17},{2,34}... | collective-permute-start | bytes 491528 | tf_op jit(solution)/shard_map/ppermute | solution.py:25
  12.0 4.5 %collective-permute-done.7 = bf16[160,512]{1,0:T(8,128)(2,1)S(1)} collective-permute-done((bf16[160,512]{1,0:T(8,128)(2,1)S(1)}, bf16[160,512]{1,0:T(8,128)(2,1)S(1)}, u32[]{:S(2)}, u32[]{:S(2)}) %collective-permute-start.7) | collective-permute-done | bytes 163872 | tf_op jit(solution)/shard_map/ppermute | solution.py:25
  16.6 10.6 %collective-permute-start.8 = (bf16[320,512]{1,0:T(8,128)(2,1)S(1)}, bf16[320,512]{1,0:T(8,128)(2,1)S(1)}, u32[]{:S(2)}, u32[]{:S(2)}) collective-permute-start(bf16[320,512]{1,0:T(8,128)(2,1)S(1)} %pad_maximum_fusion.1), channel_id=1, source_target_pairs={{0,8},{8,0},{1,9},{9,1},{2,10},{10,2},{3,11},{11,3},{4,12},{12,4},... | collective-permute-start | bytes 983048 | tf_op jit(solution)/shard_map/ppermute | solution.py:25
  28.7 6.1 %collective-permute-start.9 = (bf16[640,512]{1,0:T(8,128)(2,1)S(1)}, bf16[640,512]{1,0:T(8,128)(2,1)S(1)}, u32[]{:S(2)}, u32[]{:S(2)}) collective-permute-start(bf16[640,512]{1,0:T(8,128)(2,1)S(1)} %bitcast.11), channel_id=1, source_target_pairs={{0,64},{8,456},{64,128},{72,8},{128,192},{136,72},{192,256},{200,1... | collective-permute-start | bytes 1966088 | tf_op jit(solution)/shard_map/ppermute | solution.py:41
  34.8 7.5 %collective-permute-done.9.refs_8_ = bf16[640,512]{1,0:T(8,128)(2,1)S(1)} collective-permute-done((bf16[640,512]{1,0:T(8,128)(2,1)S(1)}, bf16[640,512]{1,0:T(8,128)(2,1)S(1)}, u32[]{:S(2)}, u32[]{:S(2)}) %collective-permute-start.9) | collective-permute-done | bytes 655392 | tf_op jit(solution)/shard_map/ppermute | solution.py:41
  42.3 5.0 %collective-permute-start.11 = (bf16[640,512]{1,0:T(8,128)(2,1)S(1)}, bf16[640,512]{1,0:T(8,128)(2,1)S(1)}, u32[]{:S(2)}, u32[]{:S(2)}) collective-permute-start(bf16[640,512]{1,0:T(8,128)(2,1)S(1)} %collective-permute-done.9.refs_8_), channel_id=1, source_target_pairs={{0,64},{8,456},{64,128},{72,8},{128,192},{136,72},{192,256},{200,1... | collective-permute-start | bytes 1966088 | tf_op jit(solution)/shard_map/ppermute | solution.py:41
  47.4 7.5 %collective-permute-start.3 = (bf16[384,640]{1,0:T(8,128)(2,1)S(1)}, bf16[384,640]{1,0:T(8,128)(2,1)S(1)}, u32[]{:S(2)}, u32[]{:S(2)}) collective-permute-start(bf16[384,640]{1,0:T(8,128)(2,1)S(1)} %copy-done.5), channel_id=1, source_target_pairs={{0,1},{1,0},{2,3},{3,2},{4,5},{5,4},{6,7},{7,6},{8,9},{9,8},{10,11... | collective-permute-start | bytes 1474568 | tf_op jit(solution)/shard_map/ppermute | solution.py:25
  54.8 4.4 %collective-permute-start = (bf16[384,640]{1,0:T(8,128)(2,1)S(1)}, bf16[384,640]{1,0:T(8,128)(2,1)S(1)}, u32[]{:S(2)}, u32[]{:S(2)}) collective-permute-start(bf16[384,640]{1,0:T(8,128)(2,1)S(1)} %copy-done.5), channel_id=1, source_target_pairs={{0,2},{8,14},{2,4},{10,8},{4,6},{12,10},{6,0},{14,12},{1,3},{9,15}... | collective-permute-start | bytes 1474568 | tf_op jit(solution)/shard_map/ppermute | solution.py:33
  59.2 16.6 %collective-permute-done.3.refs_4_ = bf16[384,640]{1,0:T(8,128)(2,1)S(1)} collective-permute-done((bf16[384,640]{1,0:T(8,128)(2,1)S(1)}, bf16[384,640]{1,0:T(8,128)(2,1)S(1)}, u32[]{:S(2)}, u32[]{:S(2)}) %collective-permute-start.3) | collective-permute-done | bytes 491552 | tf_op jit(solution)/shard_map/ppermute | solution.py:25
  75.9 4.4 %collective-permute-start.4 = (bf16[384,640]{1,0:T(8,128)(2,1)S(1)}, bf16[384,640]{1,0:T(8,128)(2,1)S(1)}, u32[]{:S(2)}, u32[]{:S(2)}) collective-permute-start(bf16[384,640]{1,0:T(8,128)(2,1)S(1)} %collective-permute-done.3.refs_4_), channel_id=1, source_target_pairs={{0,2},{8,14},{2,4},{10,8},{4,6},{12,10},{6,0},{14,12},{1,3},{9,15}... | collective-permute-start | bytes 1474568 | tf_op jit(solution)/shard_map/ppermute | solution.py:33
  82.2 2.5 %collective-permute-start.1 = (bf16[384,640]{1,0:T(8,128)(2,1)S(1)}, bf16[384,640]{1,0:T(8,128)(2,1)}, u32[]{:S(2)}, u32[]{:S(2)}) collective-permute-start(bf16[384,640]{1,0:T(8,128)(2,1)S(1)} %collective-permute-done.refs_1_), channel_id=1, source_target_pairs={{0,2},{8,14},{2,4},{10,8},{4,6},{12,10},{6,0},{14,12},{1,3},{9,15}... | collective-permute-start | bytes 1474568 | tf_op jit(solution)/shard_map/ppermute | solution.py:33
  86.0 5.3 %collective-permute-start.5 = (bf16[384,640]{1,0:T(8,128)(2,1)S(1)}, bf16[384,640]{1,0:T(8,128)(2,1)S(1)}, u32[]{:S(2)}, u32[]{:S(2)}) collective-permute-start(bf16[384,640]{1,0:T(8,128)(2,1)S(1)} %collective-permute-done.4.refs_5_), channel_id=1, source_target_pairs={{0,2},{8,14},{2,4},{10,8},{4,6},{12,10},{6,0},{14,12},{1,3},{9,15}... | collective-permute-start | bytes 1474568 | tf_op jit(solution)/shard_map/ppermute | solution.py:33
  92.2 4.2 %collective-permute-start.2 = (bf16[384,640]{1,0:T(8,128)(2,1)}, bf16[384,640]{1,0:T(8,128)(2,1)}, u32[]{:S(2)}, u32[]{:S(2)}) collective-permute-start(bf16[384,640]{1,0:T(8,128)(2,1)} %collective-permute-done.1.refs_2_), channel_id=1, source_target_pairs={{0,2},{8,14},{2,4},{10,8},{4,6},{12,10},{6,0},{14,12},{1,3},{9,15}... | collective-permute-start | bytes 1474568 | tf_op jit(solution)/shard_map/ppermute | solution.py:33
  101.6 3.0 %collective-permute-start.15 = (bf16[320,512]{1,0:T(8,128)(2,1)}, bf16[320,512]{1,0:T(8,128)(2,1)}, u32[]{:S(2)}, u32[]{:S(2)}) collective-permute-start(bf16[320,512]{1,0:T(8,128)(2,1)} %slice_select_fusion), channel_id=1, source_target_pairs={{0,64},{8,456},{64,128},{72,8},{128,192},{136,72},{192,256},{200,1... | collective-permute-start | bytes 983048 | tf_op jit(solution)/shard_map/ppermute | solution.py:41
  108.0 7.8 %all-to-all-start = ((bf16[64,4,256]{2,1,0:T(4,128)(2,1)}), bf16[64,4,256]{2,1,0:T(4,128)(2,1)S(1)}, u32[]{:S(2)}, u32[]{:S(2)}) async-start(bf16[64,4,256]{2,1,0:T(4,128)(2,1)} %broadcast_in_dim.2), calls=%async_computation | async-start | bytes 262144 | tf_op jit(solution)/shard_map/all_to_all | solution.py:223
  118.3 4.6 %collective-permute-start.17 = (bf16[384,640]{1,0:T(8,128)(2,1)}, bf16[384,640]{1,0:T(8,128)(2,1)}, u32[]{:S(2)}, u32[]{:S(2)}) collective-permute-start(bf16[384,640]{1,0:T(8,128)(2,1)} %copy-done.9), channel_id=1, source_target_pairs={{0,2},{8,14},{2,4},{10,8},{4,6},{12,10},{6,0},{14,12},{1,3},{9,15}... | collective-permute-start | bytes 1474568 | tf_op jit(solution)/shard_map/ppermute | solution.py:33
  124.1 2.6 %all-to-all-done = bf16[64,4,256]{2,1,0:T(4,128)(2,1)S(1)} async-done(((bf16[64,4,256]{2,1,0:T(4,128)(2,1)}), bf16[64,4,256]{2,1,0:T(4,128)(2,1)S(1)}, u32[]{:S(2)}, u32[]{:S(2)}) %all-to-all-start) | async-done | bytes 131104 | tf_op jit(solution)/shard_map/all_to_all | solution.py:223
  127.3 3.7 %shard_map.120 = (f32[384,512]{1,0:T(8,128)}, f32[512,512]{1,0:T(8,128)}, f32[640,512]{1,0:T(8,128)}) custom-call(bf16[384,512]{1,0:T(8,128)(2,1)} %q_ref.5, bf16[384,128]{1,0:T(8,128)(2,1)} %rk_ref.3, bf16[256,256]{1,0:T(8,128)(2,1)} %reshape.64.pkv_ref), custom_call_target="tpu_custom_call" | custom-call | flops 1073741824 | bytes 4000000 | tf_op jit(solution)/shard_map/pallas_call | solution.py:177
  131.9 8.8 %shard_map.119 = (f32[384,512]{1,0:T(8,128)}, bf16[640,512]{1,0:T(8,128)(2,1)}) custom-call(s32[4]{0:T(128)} %pad_add_fusion.place_ref, bf16[384,640]{1,0:T(8,128)(2,1)} %refs_0_.1, bf16[384,640]{1,0:T(8,128)(2,1)} %copy-done.7, bf16[384,640]{1,0:T(8,128)(2,1)} %collective-permute-done.1.refs_2_, bf16[384,640]{1,0:T(8,128)(2,1)} %collective-permute-done.2.refs_3_, ...), custom_call_target="tpu_custom_call" | custom-call | flops 2013265920 | bytes 4000000 | tf_op jit(solution)/shard_map/pallas_call | solution.py:177
  140.7 5.5 %shard_map.121 = (f32[64,4,256]{2,1,0:T(4,128)}, bf16[1536,128]{1,0:T(8,128)(2,1)}, bf16[384,512]{1,0:T(8,128)(2,1)}, bf16[512,512]{1,0:T(8,128)(2,1)}, bf16[640,512]{1,0:T(8,128)(2,1)}) custom-call(s32[1]{0:T(128)S(6)} %copy.15.length_ref, f32[384,512]{1,0:T(8,128)} %get-tuple-element.18.acc, bf16[384,640]{1,0:T(8,128)(2,1)} %collective-permute-done.17.g_last, ...), custom_call_target="tpu_custom_call" | custom-call | flops 1073741824 | bytes 4000000 | tf_op jit(solution)/shard_map/pallas_call | solution.py:177
  146.2 7.7 %all-to-all-start.1 = ((f32[64,4,256]{2,1,0:T(4,128)}), f32[64,4,256]{2,1,0:T(4,128)S(1)}, u32[]{:S(2)}, u32[]{:S(2)}) async-start(f32[64,4,256]{2,1,0:T(4,128)} %get-tuple-element.30), calls=%async_computation.1 | async-start | bytes 524288 | tf_op jit(solution)/shard_map/all_to_all | solution.py:255
  154.0 4.3 %shard_map.122 = (bf16[384,512]{1,0:T(8,128)(2,1)}, bf16[384,128]{1,0:T(8,128)(2,1)}, bf16[384,128]{1,0:T(8,128)(2,1)}) custom-call(bf16[1536,128]{1,0:T(8,128)(2,1)} %get-tuple-element.23.og_ref, bf16[384,512]{1,0:T(8,128)(2,1)} %get-tuple-element.24.s0, bf16[512,512]{1,0:T(8,128)(2,1)} %get-tuple-element.25.s1, bf16[640,512]{1,0:T(8,128)(2,1)} %get-tuple-element.26.s2, ...), custom_call_target="tpu_custom_call" | custom-call | flops 1073741824 | bytes 4000000 | tf_op jit(solution)/shard_map/pallas_call | solution.py:177
  158.2 9.2 %all-to-all-done.1 = f32[64,4,256]{2,1,0:T(4,128)S(1)} async-done(((f32[64,4,256]{2,1,0:T(4,128)}), f32[64,4,256]{2,1,0:T(4,128)S(1)}, u32[]{:S(2)}, u32[]{:S(2)}) %all-to-all-start.1) | async-done | bytes 262176 | tf_op jit(solution)/shard_map/all_to_all | solution.py:255
  (57 shorter events, 22.2 us)
Async XLA Ops:
  0.6 6.1 %collective-permute-start.6 = (bf16[80,512]{1,0:T(8,128)(2,1)}, bf16[80,512]{1,0:T(8,128)(2,1)S(1)}, u32[]{:S(2)}, u32[]{:S(2)}) collective-permute-start(bf16[80,512]{1,0:T(8,128)(2,1)} %param.9), channel_id=1, source_target_pairs={{0,16},{16,0},{32,48},{48,32},{1,17},{17,1},{33,49},{49,33},{2,18}... | collective-permute-start | bytes 245768 | tf_op jit(solution)/shard_map/ppermute | solution.py:25
  7.6 8.9 %collective-permute-start.7 = (bf16[160,512]{1,0:T(8,128)(2,1)S(1)}, bf16[160,512]{1,0:T(8,128)(2,1)S(1)}, u32[]{:S(2)}, u32[]{:S(2)}) collective-permute-start(bf16[160,512]{1,0:T(8,128)(2,1)S(1)} %pad_maximum_fusion.2), channel_id=1, source_target_pairs={{0,32},{16,48},{32,0},{48,16},{1,33},{17,49},{33,1},{49,17},{2,34}... | collective-permute-start | bytes 491528 | tf_op jit(solution)/shard_map/ppermute | solution.py:25
  16.6 11.9 %collective-permute-start.8 = (bf16[320,512]{1,0:T(8,128)(2,1)S(1)}, bf16[320,512]{1,0:T(8,128)(2,1)S(1)}, u32[]{:S(2)}, u32[]{:S(2)}) collective-permute-start(bf16[320,512]{1,0:T(8,128)(2,1)S(1)} %pad_maximum_fusion.1), channel_id=1, source_target_pairs={{0,8},{8,0},{1,9},{9,1},{2,10},{10,2},{3,11},{11,3},{4,12},{12,4},... | collective-permute-start | bytes 983048 | tf_op jit(solution)/shard_map/ppermute | solution.py:25
  28.6 78.7 %copy-start.10 = (bf16[4,128]{1,0:T(4,128)(2,1)S(1)}, bf16[4,128]{1,0:T(4,128)(2,1)}, u32[]{:S(2)}) copy-start(bf16[4,128]{1,0:T(4,128)(2,1)} %param.14) | copy-start | bytes 3076
  28.6 78.7 %copy-start.11 = (bf16[4,128]{1,0:T(4,128)(2,1)S(1)}, bf16[4,128]{1,0:T(4,128)(2,1)}, u32[]{:S(2)}) copy-start(bf16[4,128]{1,0:T(4,128)(2,1)} %param.13) | copy-start | bytes 3076
  28.7 102.4 %copy-start = (bf16[4,2,80,512]{3,2,1,0:T(8,128)(2,1)}, bf16[4,2,80,512]{3,2,1,0:T(8,128)(2,1)S(1)}, u32[]{:S(2)}) copy-start(bf16[4,2,80,512]{3,2,1,0:T(8,128)(2,1)S(1)} %pad_maximum_fusion) | copy-start | bytes 1966084
  28.7 13.7 %collective-permute-start.9 = (bf16[640,512]{1,0:T(8,128)(2,1)S(1)}, bf16[640,512]{1,0:T(8,128)(2,1)S(1)}, u32[]{:S(2)}, u32[]{:S(2)}) collective-permute-start(bf16[640,512]{1,0:T(8,128)(2,1)S(1)} %bitcast.11), channel_id=1, source_target_pairs={{0,64},{8,456},{64,128},{72,8},{128,192},{136,72},{192,256},{200,1... | collective-permute-start | bytes 1966088 | tf_op jit(solution)/shard_map/ppermute | solution.py:41
  42.3 88.7 %copy-start.2 = (bf16[640,512]{1,0:T(8,128)(2,1)}, bf16[640,512]{1,0:T(8,128)(2,1)S(1)}, u32[]{:S(2)}) copy-start(bf16[640,512]{1,0:T(8,128)(2,1)S(1)} %collective-permute-done.9.refs_8_) | copy-start | bytes 1966084
  42.3 37.9 %collective-permute-start.11 = (bf16[640,512]{1,0:T(8,128)(2,1)S(1)}, bf16[640,512]{1,0:T(8,128)(2,1)S(1)}, u32[]{:S(2)}, u32[]{:S(2)}) collective-permute-start(bf16[640,512]{1,0:T(8,128)(2,1)S(1)} %collective-permute-done.9.refs_8_), channel_id=1, source_target_pairs={{0,64},{8,456},{64,128},{72,8},{128,192},{136,72},{192,256},{200,1... | collective-permute-start | bytes 1966088 | tf_op jit(solution)/shard_map/ppermute | solution.py:41
  47.4 28.5 %collective-permute-start.3 = (bf16[384,640]{1,0:T(8,128)(2,1)S(1)}, bf16[384,640]{1,0:T(8,128)(2,1)S(1)}, u32[]{:S(2)}, u32[]{:S(2)}) collective-permute-start(bf16[384,640]{1,0:T(8,128)(2,1)S(1)} %copy-done.5), channel_id=1, source_target_pairs={{0,1},{1,0},{2,3},{3,2},{4,5},{5,4},{6,7},{7,6},{8,9},{9,8},{10,11... | collective-permute-start | bytes 1474568 | tf_op jit(solution)/shard_map/ppermute | solution.py:25
  54.8 27.4 %collective-permute-start = (bf16[384,640]{1,0:T(8,128)(2,1)S(1)}, bf16[384,640]{1,0:T(8,128)(2,1)S(1)}, u32[]{:S(2)}, u32[]{:S(2)}) collective-permute-start(bf16[384,640]{1,0:T(8,128)(2,1)S(1)} %copy-done.5), channel_id=1, source_target_pairs={{0,2},{8,14},{2,4},{10,8},{4,6},{12,10},{6,0},{14,12},{1,3},{9,15}... | collective-permute-start | bytes 1474568 | tf_op jit(solution)/shard_map/ppermute | solution.py:33
  75.9 10.1 %collective-permute-start.4 = (bf16[384,640]{1,0:T(8,128)(2,1)S(1)}, bf16[384,640]{1,0:T(8,128)(2,1)S(1)}, u32[]{:S(2)}, u32[]{:S(2)}) collective-permute-start(bf16[384,640]{1,0:T(8,128)(2,1)S(1)} %collective-permute-done.3.refs_4_), channel_id=1, source_target_pairs={{0,2},{8,14},{2,4},{10,8},{4,6},{12,10},{6,0},{14,12},{1,3},{9,15}... | collective-permute-start | bytes 1474568 | tf_op jit(solution)/shard_map/ppermute | solution.py:33
  80.3 20.5 %collective-permute-start.13 = (bf16[640,512]{1,0:T(8,128)(2,1)S(1)}, bf16[640,512]{1,0:T(8,128)(2,1)S(1)}, u32[]{:S(2)}, u32[]{:S(2)}) collective-permute-start(bf16[640,512]{1,0:T(8,128)(2,1)S(1)} %collective-permute-done.11.refs_10_), channel_id=1, source_target_pairs={{0,64},{8,456},{64,128},{72,8},{128,192},{136,72},{192,256},{200,1... | collective-permute-start | bytes 1966088 | tf_op jit(solution)/shard_map/ppermute | solution.py:41
  82.2 10.0 %collective-permute-start.1 = (bf16[384,640]{1,0:T(8,128)(2,1)S(1)}, bf16[384,640]{1,0:T(8,128)(2,1)}, u32[]{:S(2)}, u32[]{:S(2)}) collective-permute-start(bf16[384,640]{1,0:T(8,128)(2,1)S(1)} %collective-permute-done.refs_1_), channel_id=1, source_target_pairs={{0,2},{8,14},{2,4},{10,8},{4,6},{12,10},{6,0},{14,12},{1,3},{9,15}... | collective-permute-start | bytes 1474568 | tf_op jit(solution)/shard_map/ppermute | solution.py:33
  86.0 18.6 %collective-permute-start.5 = (bf16[384,640]{1,0:T(8,128)(2,1)S(1)}, bf16[384,640]{1,0:T(8,128)(2,1)S(1)}, u32[]{:S(2)}, u32[]{:S(2)}) collective-permute-start(bf16[384,640]{1,0:T(8,128)(2,1)S(1)} %collective-permute-done.4.refs_5_), channel_id=1, source_target_pairs={{0,2},{8,14},{2,4},{10,8},{4,6},{12,10},{6,0},{14,12},{1,3},{9,15}... | collective-permute-start | bytes 1474568 | tf_op jit(solution)/shard_map/ppermute | solution.py:33
  92.2 26.1 %collective-permute-start.2 = (bf16[384,640]{1,0:T(8,128)(2,1)}, bf16[384,640]{1,0:T(8,128)(2,1)}, u32[]{:S(2)}, u32[]{:S(2)}) collective-permute-start(bf16[384,640]{1,0:T(8,128)(2,1)} %collective-permute-done.1.refs_2_), channel_id=1, source_target_pairs={{0,2},{8,14},{2,4},{10,8},{4,6},{12,10},{6,0},{14,12},{1,3},{9,15}... | collective-permute-start | bytes 1474568 | tf_op jit(solution)/shard_map/ppermute | solution.py:33
  96.4 34.6 %collective-permute-start.10 = (bf16[640,512]{1,0:T(8,128)(2,1)S(1)}, bf16[640,512]{1,0:T(8,128)(2,1)S(1)}, u32[]{:S(2)}, u32[]{:S(2)}) collective-permute-start(bf16[640,512]{1,0:T(8,128)(2,1)S(1)} %collective-permute-done.9.refs_8_), channel_id=1, source_target_pairs={{0,8},{8,0},{1,9},{9,1},{2,10},{10,2},{3,11},{11,3},{4,12},{12,4},... | collective-permute-start | bytes 1966088 | tf_op jit(solution)/shard_map/ppermute | solution.py:25
  98.3 32.7 %collective-permute-start.12 = (bf16[640,512]{1,0:T(8,128)(2,1)S(1)}, bf16[640,512]{1,0:T(8,128)(2,1)}, u32[]{:S(2)}, u32[]{:S(2)}) collective-permute-start(bf16[640,512]{1,0:T(8,128)(2,1)S(1)} %collective-permute-done.11.refs_10_), channel_id=1, source_target_pairs={{0,8},{8,0},{1,9},{9,1},{2,10},{10,2},{3,11},{11,3},{4,12},{12,4},... | collective-permute-start | bytes 1966088 | tf_op jit(solution)/shard_map/ppermute | solution.py:25
  101.6 14.3 %collective-permute-start.15 = (bf16[320,512]{1,0:T(8,128)(2,1)}, bf16[320,512]{1,0:T(8,128)(2,1)}, u32[]{:S(2)}, u32[]{:S(2)}) collective-permute-start(bf16[320,512]{1,0:T(8,128)(2,1)} %slice_select_fusion), channel_id=1, source_target_pairs={{0,64},{8,456},{64,128},{72,8},{128,192},{136,72},{192,256},{200,1... | collective-permute-start | bytes 983048 | tf_op jit(solution)/shard_map/ppermute | solution.py:41
  105.4 25.7 %collective-permute-start.14 = (bf16[640,512]{1,0:T(8,128)(2,1)S(1)}, bf16[640,512]{1,0:T(8,128)(2,1)}, u32[]{:S(2)}, u32[]{:S(2)}) collective-permute-start(bf16[640,512]{1,0:T(8,128)(2,1)S(1)} %collective-permute-done.13.refs_12_), channel_id=1, source_target_pairs={{0,8},{8,0},{1,9},{9,1},{2,10},{10,2},{3,11},{11,3},{4,12},{12,4},... | collective-permute-start | bytes 1966088 | tf_op jit(solution)/shard_map/ppermute | solution.py:25
  108.0 18.6 %all-to-all-start = ((bf16[64,4,256]{2,1,0:T(4,128)(2,1)}), bf16[64,4,256]{2,1,0:T(4,128)(2,1)S(1)}, u32[]{:S(2)}, u32[]{:S(2)}) async-start(bf16[64,4,256]{2,1,0:T(4,128)(2,1)} %broadcast_in_dim.2), calls=%async_computation | async-start | bytes 262144 | tf_op jit(solution)/shard_map/all_to_all | solution.py:223
  115.9 15.2 %collective-permute-start.16 = (bf16[320,512]{1,0:T(8,128)(2,1)}, bf16[320,512]{1,0:T(8,128)(2,1)}, u32[]{:S(2)}, u32[]{:S(2)}) collective-permute-start(bf16[320,512]{1,0:T(8,128)(2,1)} %collective-permute-done.15.refs_14_), channel_id=1, source_target_pairs={{0,8},{8,0},{1,9},{9,1},{2,10},{10,2},{3,11},{11,3},{4,12},{12,4},... | collective-permute-start | bytes 983048 | tf_op jit(solution)/shard_map/ppermute | solution.py:25
  118.3 22.4 %collective-permute-start.17 = (bf16[384,640]{1,0:T(8,128)(2,1)}, bf16[384,640]{1,0:T(8,128)(2,1)}, u32[]{:S(2)}, u32[]{:S(2)}) collective-permute-start(bf16[384,640]{1,0:T(8,128)(2,1)} %copy-done.9), channel_id=1, source_target_pairs={{0,2},{8,14},{2,4},{10,8},{4,6},{12,10},{6,0},{14,12},{1,3},{9,15}... | collective-permute-start | bytes 1474568 | tf_op jit(solution)/shard_map/ppermute | solution.py:33
  146.2 21.2 %all-to-all-start.1 = ((f32[64,4,256]{2,1,0:T(4,128)}), f32[64,4,256]{2,1,0:T(4,128)S(1)}, u32[]{:S(2)}, u32[]{:S(2)}) async-start(f32[64,4,256]{2,1,0:T(4,128)} %get-tuple-element.30), calls=%async_computation.1 | async-start | bytes 524288 | tf_op jit(solution)/shard_map/all_to_all | solution.py:255
  (8 other events, 162.4 us)

commit v3 on v2

v3 whole, which is shorter than its diff:
```python
import jax
import jax.numpy as jnp
from jax import lax
from jax.experimental import pallas as pl
from jax.experimental.pallas import tpu as pltpu
from jax.sharding import Mesh
from jax.sharding import PartitionSpec as P

HD = 128
ROWS = 384
BLOCK = 128
GROUP = 4
PREFIX = 256
SCALE = HD**-0.5
KB = 640
TAIL = 16
F32 = jnp.float32
BF16 = jnp.bfloat16
ROLL = ("z", "yl", "c")
TENSOR = ("x", "yh")
NZ, NY, NX = 8, 4, 4
NT = (((1,), (1,)), ((), ()))


def swap(v, axis, bit=1):
    size = lax.axis_size(axis)
    return lax.ppermute(v, axis, [(i, i ^ bit) for i in range(size)])


def shift_x(v, step):
    return lax.ppermute(v, "x", [(x, (x + step) % NX) for x in range(NX)])


def ring_z(v):
    pairs = []
    for z in range(NZ):
        pairs.append((2 * z, 2 * ((z + 1) % NZ)))
        pairs.append((2 * z + 1, 2 * ((z - 1) % NZ) + 1))
    return lax.ppermute(v, ("z", "c"), pairs)


def in_pair(mine, other, bit, axis):
    first = jnp.where(bit == 0, mine, other)
    second = jnp.where(bit == 0, other, mine)
    return jnp.concatenate([first, second], axis=axis)


def stacked(ref, i):
    rows = slice(BLOCK * i, BLOCK * (i + 1))
    return jnp.concatenate([ref[rows, HD * h : HD * (h + 1)] for h in range(GROUP)], axis=0)


def prefix_part(ref, at):
    halves = [
        ref[TAIL * z : TAIL * (z + 1), 256 * half + at : 256 * half + at + HD]
        for z in range(NZ)
        for half in range(2)
    ]
    return jnp.concatenate(halves, axis=0)


def soft_rows(keys, q_ref, i):
    low = PREFIX + BLOCK * i
    scores = (
        lax.dot_general(keys[: low + BLOCK], stacked(q_ref, i), NT, preferred_element_type=F32)
        * SCALE
    )
    open_part = scores[:low]
    key_place = lax.broadcasted_iota(jnp.int32, (BLOCK, GROUP * BLOCK), 0)
    row_place = lax.broadcasted_iota(jnp.int32, (BLOCK, GROUP * BLOCK), 1) % BLOCK
    edge = jnp.where(key_place <= row_place, scores[low:], -jnp.inf)
    top = jnp.maximum(
        jnp.max(open_part, axis=0, keepdims=True), jnp.max(edge, axis=0, keepdims=True)
    )
    open_part = jnp.exp(open_part - top)
    edge = jnp.exp(edge - top)
    total = jnp.sum(open_part, axis=0, keepdims=True) + jnp.sum(edge, axis=0, keepdims=True)
    share = 1.0 / total
    return open_part * share, edge * share


def front_kernel(place_ref, length_ref, *refs):
    g_in, w_in, in_refs = refs[:8], refs[8:16], refs[16:19]
    gp_ref, out_refs = refs[19], refs[20:28]
    q_ref, rk_ref, rv_ref = refs[28:31]
    og_ref, s0, s1, s2, l0, l1, l2, pkv_ref = refs[31:39]
    g_buf, w_buf, p_buf0, p_buf1, p_buf2 = refs[39:44]
    sem, w_sem, tail_sem, out_sem, g_sem = refs[44:]
    small = [
        pltpu.make_async_copy(src, dst, sem.at[2 + k])
        for k, (src, dst) in enumerate(zip(in_refs, (q_ref, rk_ref, rv_ref)))
    ]
    outs = [
        pltpu.make_async_copy(src, dst, out_sem.at[k])
        for k, (src, dst) in enumerate(
            zip((og_ref, s0, s1, s2, l0, l1, l2, pkv_ref), out_refs)
        )
    ]
    yh, z, core, x = place_ref[0], place_ref[1], place_ref[2], place_ref[3]
    way = 1 - 2 * core
    p_bufs = (p_buf0, p_buf1, p_buf2)
    steps = (0, -way, -2 * way, -3 * way, 4, way, 2 * way, 3 * way)
    copies, tails = [], []
    for k, (src, step) in enumerate(zip(w_in, steps)):
        to = lax.rem(z + step + 8, 8)
        place = pl.ds(pl.multiple_of(TAIL * to, TAIL), TAIL)
        tails.append(
            pltpu.make_async_copy(src.at[pl.ds(KB, TAIL)], pkv_ref.at[place], tail_sem.at[k])
        )
        copies.append(pltpu.make_async_copy(src.at[pl.ds(0, KB)], w_buf.at[to], w_sem.at[k]))
    for k, src in enumerate(g_in):
        side = yh if k < 4 else 1 - yh
        dst = g_buf.at[side, lax.rem(x - (0, 1, 3, 2)[k % 4] + 4, 4)]
        copies.append(pltpu.make_async_copy(src, dst, g_sem.at[k]))
    for c in small + tails + copies:
        c.start()
    for c in small + tails:
        c.wait()
    outs[7].start()
    keys = jnp.concatenate([prefix_part(pkv_ref, 0), rk_ref[...]], axis=0)
    for i, (p_ref, l_ref) in enumerate(zip(p_bufs, (l0, l1, l2))):
        low = PREFIX + BLOCK * i
        open_part, edge = soft_rows(keys, q_ref, i)
        p_ref[:low], p_ref[low:] = open_part, edge
        if i:
            l_ref[: BLOCK * i] = open_part[PREFIX:].astype(BF16)
        l_ref[BLOCK * i :] = edge.astype(BF16)
        outs[4 + i].start()

    for c in copies:
        c.wait()
    grow = jnp.concatenate([g_buf[t % 2, t // 2] for t in range(8)], axis=1)
    total = jnp.dot(grow, w_buf[...].reshape(5120, 512), preferred_element_type=F32)
    row = lax.broadcasted_iota(jnp.int32, (ROWS, GROUP * HD), 0)
    out_grad = jnp.where(row < length_ref[0], total, 0.0).astype(BF16)
    for i in range(3):
        for h in range(GROUP):
            at = GROUP * BLOCK * i + BLOCK * h
            og_ref[at : at + BLOCK] = out_grad[
                BLOCK * i : BLOCK * (i + 1), HD * h : HD * (h + 1)
            ]
    outs[0].start()
    values = jnp.concatenate([prefix_part(pkv_ref, HD), rv_ref[...]], axis=0)
    key_grad = jnp.zeros((PREFIX, HD), F32)
    value_grad = jnp.zeros((PREFIX, HD), F32)
    for i, (p_ref, s_ref) in enumerate(zip(p_bufs, (s0, s1, s2))):
        width = PREFIX + BLOCK * (i + 1)
        grads = og_ref[GROUP * BLOCK * i : GROUP * BLOCK * (i + 1)]
        prob_grad = lax.dot_general(values[:width], grads, NT, preferred_element_type=F32)
        weights = p_ref[...]
        delta = jnp.sum(weights * prob_grad, axis=0, keepdims=True)
        score_low = (weights * (prob_grad - delta) * SCALE).astype(BF16)
        s_ref[...] = score_low
        outs[1 + i].start()
        key_grad += jnp.dot(score_low[:PREFIX], stacked(q_ref, i), preferred_element_type=F32)
        value_grad += jnp.dot(weights[:PREFIX].astype(BF16), grads, preferred_element_type=F32)
    for j in range(PREFIX // 4):
        gp_ref[j, :, :HD] = key_grad[4 * j : 4 * j + 4]
        gp_ref[j, :, HD:] = value_grad[4 * j : 4 * j + 4]
    for c in outs:
        c.wait()


def back_kernel(og_ref, s0, s1, s2, l0, l1, l2, q_ref, rk_ref, pkv_ref, gq_ref, grk_ref, grv_ref):
    keys = jnp.concatenate([prefix_part(pkv_ref, 0), rk_ref[...]], axis=0)
    keys_t = keys.astype(F32).T.astype(BF16)
    key_grad = [None] * 3
    value_grad = [None] * 3
    for i, (l_ref, s_ref) in enumerate(zip((l0, l1, l2), (s0, s1, s2))):
        width = PREFIX + BLOCK * (i + 1)
        rows = slice(BLOCK * i, BLOCK * (i + 1))
        score_low = s_ref[...]
        weights = l_ref[...]
        grads = og_ref[GROUP * BLOCK * i : GROUP * BLOCK * (i + 1)]
        kg = jnp.dot(score_low[PREFIX:], stacked(q_ref, i), preferred_element_type=F32)
        vg = jnp.dot(weights, grads, preferred_element_type=F32)
        qt = jnp.dot(keys_t[:, :width], score_low, preferred_element_type=F32)
        for h in range(GROUP):
            gq_ref[rows, HD * h : HD * (h + 1)] = qt[:, BLOCK * h : BLOCK * (h + 1)].T.astype(BF16)
        for j in range(i + 1):
            part = slice(BLOCK * j, BLOCK * (j + 1))
            key_grad[j] = kg[part] if key_grad[j] is None else key_grad[j] + kg[part]
            value_grad[j] = vg[part] if value_grad[j] is None else value_grad[j] + vg[part]
    for j in range(3):
        rows = slice(BLOCK * j, BLOCK * (j + 1))
        grk_ref[rows] = key_grad[j].astype(BF16)
        grv_ref[rows] = value_grad[j].astype(BF16)


VM = pl.BlockSpec(memory_space=pltpu.VMEM)
SM = pl.BlockSpec(memory_space=pltpu.SMEM)
ANY = pl.BlockSpec(memory_space=pl.ANY)
WIDTHS = tuple(PREFIX + BLOCK * (i + 1) for i in range(3))


def call(kernel, outs, in_specs, args, flops, scratch=(), out_specs=None):
    return pl.pallas_call(
        kernel,
        out_shape=[jax.ShapeDtypeStruct(s, d) for s, d in outs],
        in_specs=in_specs,
        out_specs=out_specs or [VM] * len(outs),
        scratch_shapes=scratch,
        cost_estimate=pl.CostEstimate(flops=flops, bytes_accessed=4000000, transcendentals=0),
    )(*args)


def front(place, lengths, g, w, queries, resp_key, resp_value):
    outs = [((64, 4, 2 * HD), F32), ((GROUP * ROWS, HD), BF16)]
    outs += [((w, GROUP * BLOCK), BF16) for w in WIDTHS]
    outs += [((w - PREFIX, GROUP * BLOCK), BF16) for w in WIDTHS]
    outs += [((NZ * TAIL, 512), BF16)]
    return call(
        front_kernel,
        outs,
        [SM] * 2 + [ANY] * 19,
        (place, lengths, *g, *w, queries, resp_key, resp_value),
        2 * 384 * 5120 * 512,
        [pltpu.VMEM((ROWS, n), BF16) for n in (512, HD, HD)]
        + [pltpu.VMEM(*o) for o in outs[1:]]
        + [pltpu.VMEM((2, NX, ROWS, KB), BF16), pltpu.VMEM((8, KB, 512), BF16)]
        + [pltpu.VMEM((w, GROUP * BLOCK), F32) for w in WIDTHS]
        + [pltpu.SemaphoreType.DMA((8,)) for _ in range(5)],
        [VM] + [ANY] * 8,
    )


def back(og, s, low, queries, resp_key, prefix):
    outs = [((ROWS, GROUP * HD), BF16), ((ROWS, HD), BF16), ((ROWS, HD), BF16)]
    return call(back_kernel, outs, [VM] * 10, (og, *s, *low, queries, resp_key, prefix), 1 << 30)


def steps(grad_out, out_weight, queries, resp_key, resp_value, prefix_key, prefix_value, lengths):
    x, yh, yl = lax.axis_index("x"), lax.axis_index("yh"), lax.axis_index("yl")
    z, core = lax.axis_index("z"), lax.axis_index("c")
    both = jnp.concatenate([prefix_key, prefix_value], axis=1)

    shard = jnp.concatenate([out_weight, jnp.pad(both, ((0, 4), (0, 256)))], axis=0)
    shards = [shard] + [swap(shard, "yl", k) for k in (1, 2, 3)]
    near = in_pair(shards[0], shards[1], yl % 2, 0)
    far = in_pair(shards[2], shards[3], yl % 2, 0)
    four = in_pair(near, far, yl // 2, 0).reshape(4, 1, 88, 512)
    pair = in_pair(four, swap(four, "c"), core, 1)
    tail = pair[:, :, 80:84, :256].reshape(2, TAIL, 256)
    piece = jnp.concatenate(
        [pair[:, :, :80].reshape(KB, 512), jnp.concatenate([tail[0], tail[1]], axis=1)], axis=0
    )
    def along_x(v):
        return [v] + [shift_x(v, k) for k in (1, 3, 2)]

    g = along_x(grad_out) + along_x(swap(grad_out, "yh"))
    aheads = [piece]
    for _ in range(4):
        aheads.append(ring_z(aheads[-1]))
    across = [swap(aheads[k], "c") for k in (1, 2, 3)]
    place = jnp.stack([yh, z, core, x]).astype(jnp.int32)
    gp, og, *rest = front(
        place, lengths, g, (*aheads, *across), queries, resp_key, resp_value
    )
    s, low, prefix = rest[:3], rest[3:6], rest[6]
    parts = lax.all_to_all(gp, ROLL, 0, 0, tiled=True)
    gq, grk, grv = back(og, s, low, queries, resp_key, prefix)
    total = jnp.sum(parts, axis=0)
    return gq, grk, grv, total[:, :HD], total[:, HD:]


def solution(mesh):
    torus = Mesh(mesh.devices.reshape(NZ, NY, 2, NX, 2), ROLL + TENSOR)
    placed = P(ROLL, TENSOR)
    return jax.shard_map(
        steps,
        mesh=torus,
        in_specs=(placed,) * 7 + (P(ROLL),),
        out_specs=(placed,) * 5,
        check_vma=False,
    )
```

time: 169 us -> 152 us (0.90)
  starting transfers between devices: 92 us -> 72.5 us
  waiting for transfers between devices: 45.9 us -> 56.7 us
  Pallas kernels: 22.3 us -> 14.8 us
    ppermute x6, waiting for transfers between devices: 2.21 us -> 22.7 us  [shift_x(): return lax.ppermute(v, 'x', [(x, (x + step) % NX) for x in range(NX)])]
    ppermute x8, waiting for transfers between devices: 24.3 us -> 16.3 us  [swap(): return lax.ppermute(v, axis, [(i, i ^ bit) for i in range(size)])]
    all_to_all x1 -> x0, starting transfers between devices: 7.84 us -> none  [steps(): lax.all_to_all(jnp.broadcast_to(both[None], (64,) + both.shape), ROLL, 0,...]
    pallas_call x4 -> x2, Pallas kernels: 22.3 us -> 14.8 us  [call(): pl.pallas_call(kernel, out_shape=[jax.ShapeDtypeStruct(s, d) for s, d in...]
    ppermute x8, starting transfers between devices: 35.1 us -> 28.1 us  [swap(): return lax.ppermute(v, axis, [(i, i ^ bit) for i in range(size)])]
    ppermute x6, starting transfers between devices: 25.3 us -> 21.3 us  [shift_x(): return lax.ppermute(v, 'x', [(x, (x + step) % NX) for x in range(NX)])]
    all_to_all x1 -> x0, waiting for transfers between devices: 2.56 us -> none  [steps(): lax.all_to_all(jnp.broadcast_to(both[None], (64,) + both.shape), ROLL, 0,...]
    all_to_all x1, starting transfers between devices: 7.71 us -> 5.4 us  [steps(): parts = lax.all_to_all(gp, ROLL, 0, 0, tiled=True)]
  transfers between devices with their start and end apart: 20 -> 19, of which waited for: 9 -> 8; matrix products, arithmetic and copies ran while one was open for 2% -> 1% of each run, Pallas kernels for 10% -> 2%
where the time goes in v3:
time: 152 us; the launch traced here: 151 us
  starting transfers between devices  72.5 us (48%)
  waiting for transfers between devices  56.7 us (37%)
  Pallas kernels  14.8 us (10%)
  other arithmetic  3.49 us (2%)
  local copies, waits for them, and re-layouts  2.19 us (1%)
  between operations  1.72 us (1%)
    ppermute x8, starting transfers between devices, swap(): return lax.ppermute(v, axis, [(i, i ^ bit) for i in range(size)])  28.1 us
    ppermute x6, waiting for transfers between devices, shift_x(): return lax.ppermute(v, 'x', [(x, (x + step) % NX) for x in range(NX)])  22.7 us
    ppermute x6, starting transfers between devices, shift_x(): return lax.ppermute(v, 'x', [(x, (x + step) % NX) for x in range(NX)])  21.3 us
    ppermute x4, starting transfers between devices, ring_z(): return lax.ppermute(v, ('z', 'c'), pairs)  17.7 us
    ppermute x8, waiting for transfers between devices, swap(): return lax.ppermute(v, axis, [(i, i ^ bit) for i in range(size)])  16.3 us
    pallas_call x2, Pallas kernels, call(): pl.pallas_call(kernel, out_shape=[jax.ShapeDtypeStruct(s, d) for s, d in...  14.8 us
    all_to_all x1, waiting for transfers between devices, steps(): parts = lax.all_to_all(gp, ROLL, 0, 0, tiled=True)  10.1 us
    ppermute x4, waiting for transfers between devices, ring_z(): return lax.ppermute(v, ('z', 'c'), pairs)  7.69 us
  transfers between devices with their start and end apart: 19, of which 8 were waited for; matrix products, arithmetic and copies ran while one was open for 1% of the time, Pallas kernels for 2%

profile of v3, /device:TPU:1, one launch (start us, length us, event | category | flops | bytes accessed | tf_op | source)
XLA Modules:
  0.0 151.5 jit_solution(6234840047999529873)
XLA Ops:
  2.2 4.0 %collective-permute-start.7 = (bf16[88,512]{1,0:T(8,128)(2,1)S(1)}, bf16[88,512]{1,0:T(8,128)(2,1)S(1)}, u32[]{:S(2)}, u32[]{:S(2)}) collective-permute-start(bf16[88,512]{1,0:T(8,128)(2,1)S(1)} %pad_maximum_fusion.3), channel_id=1, source_target_pairs={{0,16},{16,0},{32,48},{48,32},{1,17},{17,1},{33,49},{49,33},{2,18}... | collective-permute-start | bytes 270344 | tf_op jit(solution)/shard_map/ppermute | solution.py:27
  6.2 4.1 %collective-permute-start.9 = (bf16[88,512]{1,0:T(8,128)(2,1)S(1)}, bf16[88,512]{1,0:T(8,128)(2,1)S(1)}, u32[]{:S(2)}, u32[]{:S(2)}) collective-permute-start(bf16[88,512]{1,0:T(8,128)(2,1)S(1)} %pad_maximum_fusion.3), channel_id=1, source_target_pairs={{0,48},{16,32},{32,16},{48,0},{1,49},{17,33},{33,17},{49,1},{2,50}... | collective-permute-start | bytes 270344 | tf_op jit(solution)/shard_map/ppermute | solution.py:27
  13.4 5.4 %collective-permute-done.8 = bf16[88,512]{1,0:T(8,128)(2,1)S(1)} collective-permute-done((bf16[88,512]{1,0:T(8,128)(2,1)S(1)}, bf16[88,512]{1,0:T(8,128)(2,1)S(1)}, u32[]{:S(2)}, u32[]{:S(2)}) %collective-permute-start.8) | collective-permute-done | bytes 90144 | tf_op jit(solution)/shard_map/ppermute | solution.py:27
  18.9 5.1 %collective-permute-start.10 = (bf16[4,1,88,512]{3,2,1,0:T(8,128)(2,1)S(1)}, bf16[4,1,88,512]{3,2,1,0:T(8,128)(2,1)S(1)}, u32[]{:S(2)}, u32[]{:S(2)}) collective-permute-start(bf16[4,1,88,512]{3,2,1,0:T(8,128)(2,1)S(1)} %bitcast.9), channel_id=1, source_target_pairs={{0,8},{8,0},{1,9},{9,1},{2,10},{10,2},{3,11},{11,3},{4,12},{12,4},... | collective-permute-start | bytes 1081352 | tf_op jit(solution)/shard_map/ppermute | solution.py:27
  25.6 8.9 %collective-permute-start.11 = (bf16[656,512]{1,0:T(8,128)(2,1)S(1)}, bf16[656,512]{1,0:T(8,128)(2,1)S(1)}, u32[]{:S(2)}, u32[]{:S(2)}) collective-permute-start(bf16[656,512]{1,0:T(8,128)(2,1)S(1)} %maximum_maximum_fusion.refs_8_), channel_id=1, source_target_pairs={{0,64},{8,456},{64,128},{72,8},{128,192},{136,72},{192,256},{200,1... | collective-permute-start | bytes 2015240 | tf_op jit(solution)/shard_map/ppermute | solution.py:39
  34.5 7.7 %collective-permute-done.11.refs_9_ = bf16[656,512]{1,0:T(8,128)(2,1)S(1)} collective-permute-done((bf16[656,512]{1,0:T(8,128)(2,1)S(1)}, bf16[656,512]{1,0:T(8,128)(2,1)S(1)}, u32[]{:S(2)}, u32[]{:S(2)}) %collective-permute-start.11) | collective-permute-done | bytes 671776 | tf_op jit(solution)/shard_map/ppermute | solution.py:39
  42.2 5.0 %collective-permute-start.12 = (bf16[656,512]{1,0:T(8,128)(2,1)S(1)}, bf16[656,512]{1,0:T(8,128)(2,1)S(1)}, u32[]{:S(2)}, u32[]{:S(2)}) collective-permute-start(bf16[656,512]{1,0:T(8,128)(2,1)S(1)} %collective-permute-done.11.refs_9_), channel_id=1, source_target_pairs={{0,64},{8,456},{64,128},{72,8},{128,192},{136,72},{192,256},{200,1... | collective-permute-start | bytes 2015240 | tf_op jit(solution)/shard_map/ppermute | solution.py:39
  47.2 6.2 %collective-permute-start.3 = (bf16[384,640]{1,0:T(8,128)(2,1)S(1)}, bf16[384,640]{1,0:T(8,128)(2,1)}, u32[]{:S(2)}, u32[]{:S(2)}) collective-permute-start(bf16[384,640]{1,0:T(8,128)(2,1)S(1)} %copy-done.5), channel_id=1, source_target_pairs={{0,1},{1,0},{2,3},{3,2},{4,5},{5,4},{6,7},{7,6},{8,9},{9,8},{10,11... | collective-permute-start | bytes 1474568 | tf_op jit(solution)/shard_map/ppermute | solution.py:27
  53.5 4.7 %collective-permute-start.2 = (bf16[384,640]{1,0:T(8,128)(2,1)S(1)}, bf16[384,640]{1,0:T(8,128)(2,1)S(1)}, u32[]{:S(2)}, u32[]{:S(2)}) collective-permute-start(bf16[384,640]{1,0:T(8,128)(2,1)S(1)} %copy-done.5), channel_id=1, source_target_pairs={{0,4},{2,6},{4,0},{6,2},{1,5},{3,7},{5,1},{7,3},{8,12},{10,14},{12... | collective-permute-start | bytes 1474568 | tf_op jit(solution)/shard_map/ppermute | solution.py:31
  60.1 4.2 %collective-permute-start.1 = (bf16[384,640]{1,0:T(8,128)(2,1)S(1)}, bf16[384,640]{1,0:T(8,128)(2,1)S(1)}, u32[]{:S(2)}, u32[]{:S(2)}) collective-permute-start(bf16[384,640]{1,0:T(8,128)(2,1)S(1)} %copy-done.5), channel_id=1, source_target_pairs={{0,6},{2,0},{4,2},{6,4},{1,7},{3,1},{5,3},{7,5},{8,14},{10,8},{12,... | collective-permute-start | bytes 1474568 | tf_op jit(solution)/shard_map/ppermute | solution.py:31
  66.2 9.6 %collective-permute-done.3.refs_4_ = bf16[384,640]{1,0:T(8,128)(2,1)} collective-permute-done((bf16[384,640]{1,0:T(8,128)(2,1)S(1)}, bf16[384,640]{1,0:T(8,128)(2,1)}, u32[]{:S(2)}, u32[]{:S(2)}) %collective-permute-start.3) | collective-permute-done | bytes 491552 | tf_op jit(solution)/shard_map/ppermute | solution.py:27
  75.8 4.6 %collective-permute-start.6 = (bf16[384,640]{1,0:T(8,128)(2,1)}, bf16[384,640]{1,0:T(8,128)(2,1)S(1)}, u32[]{:S(2)}, u32[]{:S(2)}) collective-permute-start(bf16[384,640]{1,0:T(8,128)(2,1)} %collective-permute-done.3.refs_4_), channel_id=1, source_target_pairs={{0,4},{2,6},{4,0},{6,2},{1,5},{3,7},{5,1},{7,3},{8,12},{10,14},{12... | collective-permute-start | bytes 1474568 | tf_op jit(solution)/shard_map/ppermute | solution.py:31
  80.5 2.8 %collective-permute-start.5 = (bf16[384,640]{1,0:T(8,128)(2,1)}, bf16[384,640]{1,0:T(8,128)(2,1)S(1)}, u32[]{:S(2)}, u32[]{:S(2)}) collective-permute-start(bf16[384,640]{1,0:T(8,128)(2,1)} %collective-permute-done.3.refs_4_), channel_id=1, source_target_pairs={{0,6},{2,0},{4,2},{6,4},{1,7},{3,1},{5,3},{7,5},{8,14},{10,8},{12,... | collective-permute-start | bytes 1474568 | tf_op jit(solution)/shard_map/ppermute | solution.py:31
  83.3 2.2 %collective-permute-start.15 = (bf16[656,512]{1,0:T(8,128)(2,1)S(1)}, bf16[656,512]{1,0:T(8,128)(2,1)S(1)}, u32[]{:S(2)}, u32[]{:S(2)}) collective-permute-start(bf16[656,512]{1,0:T(8,128)(2,1)S(1)} %collective-permute-done.11.refs_9_), channel_id=1, source_target_pairs={{0,8},{8,0},{1,9},{9,1},{2,10},{10,2},{3,11},{11,3},{4,12},{12,4},... | collective-permute-start | bytes 2015240 | tf_op jit(solution)/shard_map/ppermute | solution.py:27
  85.5 2.1 %collective-permute-start.16 = (bf16[656,512]{1,0:T(8,128)(2,1)S(1)}, bf16[656,512]{1,0:T(8,128)(2,1)}, u32[]{:S(2)}, u32[]{:S(2)}) collective-permute-start(bf16[656,512]{1,0:T(8,128)(2,1)S(1)} %collective-permute-done.12.refs_10_), channel_id=1, source_target_pairs={{0,8},{8,0},{1,9},{9,1},{2,10},{10,2},{3,11},{11,3},{4,12},{12,4},... | collective-permute-start | bytes 2015240 | tf_op jit(solution)/shard_map/ppermute | solution.py:27
  87.7 2.2 %collective-permute-start.17 = (bf16[656,512]{1,0:T(8,128)(2,1)S(1)}, bf16[656,512]{1,0:T(8,128)(2,1)}, u32[]{:S(2)}, u32[]{:S(2)}) collective-permute-start(bf16[656,512]{1,0:T(8,128)(2,1)S(1)} %collective-permute-done.13.refs_11_), channel_id=1, source_target_pairs={{0,8},{8,0},{1,9},{9,1},{2,10},{10,2},{3,11},{11,3},{4,12},{12,4},... | collective-permute-start | bytes 2015240 | tf_op jit(solution)/shard_map/ppermute | solution.py:27
  89.9 2.6 %collective-permute-done.6.refs_7_ = bf16[384,640]{1,0:T(8,128)(2,1)S(1)} collective-permute-done((bf16[384,640]{1,0:T(8,128)(2,1)}, bf16[384,640]{1,0:T(8,128)(2,1)S(1)}, u32[]{:S(2)}, u32[]{:S(2)}) %collective-permute-start.6) | collective-permute-done | bytes 491552 | tf_op jit(solution)/shard_map/ppermute | solution.py:31
  94.4 8.8 %collective-permute-done.5.refs_6_ = bf16[384,640]{1,0:T(8,128)(2,1)S(1)} collective-permute-done((bf16[384,640]{1,0:T(8,128)(2,1)}, bf16[384,640]{1,0:T(8,128)(2,1)S(1)}, u32[]{:S(2)}, u32[]{:S(2)}) %collective-permute-start.5) | collective-permute-done | bytes 491552 | tf_op jit(solution)/shard_map/ppermute | solution.py:31
  104.0 3.1 %collective-permute-start.4 = (bf16[384,640]{1,0:T(8,128)(2,1)}, bf16[384,640]{1,0:T(8,128)(2,1)}, u32[]{:S(2)}, u32[]{:S(2)}) collective-permute-start(bf16[384,640]{1,0:T(8,128)(2,1)} %collective-permute-done.3.refs_4_), channel_id=1, source_target_pairs={{0,2},{2,4},{4,6},{6,0},{1,3},{3,5},{5,7},{7,1},{8,10},{10,12},{12... | collective-permute-start | bytes 1474568 | tf_op jit(solution)/shard_map/ppermute | solution.py:31
  108.4 11.3 %collective-permute-done.4.refs_5_ = bf16[384,640]{1,0:T(8,128)(2,1)} collective-permute-done((bf16[384,640]{1,0:T(8,128)(2,1)}, bf16[384,640]{1,0:T(8,128)(2,1)}, u32[]{:S(2)}, u32[]{:S(2)}) %collective-permute-start.4) | collective-permute-done | bytes 491552 | tf_op jit(solution)/shard_map/ppermute | solution.py:31
  120.5 11.2 %shard_map.119 = (f32[64,4,256]{2,1,0:T(4,128)}, bf16[1536,128]{1,0:T(8,128)(2,1)}, bf16[384,512]{1,0:T(8,128)(2,1)}, bf16[512,512]{1,0:T(8,128)(2,1)}, bf16[640...) custom-call(s32[4]{0:T(128)} %pad_add_fusion.place_ref, ...), custom_call_target="tpu_custom_call" | custom-call | flops 2013265920 | bytes 4000000 | tf_op jit(solution)/shard_map/pallas_call | solution.py:197
  131.8 5.4 %all-to-all-start = ((f32[64,4,256]{2,1,0:T(4,128)}), f32[64,4,256]{2,1,0:T(4,128)S(1)}, u32[]{:S(2)}, u32[]{:S(2)}) async-start(f32[64,4,256]{2,1,0:T(4,128)} %get-tuple-element.28), calls=%async_computation | async-start | bytes 524288 | tf_op jit(solution)/shard_map/all_to_all | solution.py:260
  137.2 3.6 %shard_map.120 = (bf16[384,512]{1,0:T(8,128)(2,1)}, bf16[384,128]{1,0:T(8,128)(2,1)}, bf16[384,128]{1,0:T(8,128)(2,1)}) custom-call(bf16[1536,128]{1,0:T(8,128)(2,1)} %get-tuple-element.17.og_ref, bf16[384,512]{1,0:T(8,128)(2,1)} %get-tuple-element.18.s0, bf16[512,512]{1,0:T(8,128)(2,1)} %get-tuple-element.19.s1, bf16[640,512]{1,0:T(8,128)(2,1)} %get-tuple-element.20.s2, ...), custom_call_target="tpu_custom_call" | custom-call | flops 1073741824 | bytes 4000000 | tf_op jit(solution)/shard_map/pallas_call | solution.py:197
  140.7 10.1 %all-to-all-done = f32[64,4,256]{2,1,0:T(4,128)S(1)} async-done(((f32[64,4,256]{2,1,0:T(4,128)}), f32[64,4,256]{2,1,0:T(4,128)S(1)}, u32[]{:S(2)}, u32[]{:S(2)}) %all-to-all-start) | async-done | bytes 262176 | tf_op jit(solution)/shard_map/all_to_all | solution.py:260
  (53 shorter events, 14.8 us)
Async XLA Ops:
  2.2 10.2 %collective-permute-start.7 = (bf16[88,512]{1,0:T(8,128)(2,1)S(1)}, bf16[88,512]{1,0:T(8,128)(2,1)S(1)}, u32[]{:S(2)}, u32[]{:S(2)}) collective-permute-start(bf16[88,512]{1,0:T(8,128)(2,1)S(1)} %pad_maximum_fusion.3), channel_id=1, source_target_pairs={{0,16},{16,0},{32,48},{48,32},{1,17},{17,1},{33,49},{49,33},{2,18}... | collective-permute-start | bytes 270344 | tf_op jit(solution)/shard_map/ppermute | solution.py:27
  6.2 7.1 %collective-permute-start.9 = (bf16[88,512]{1,0:T(8,128)(2,1)S(1)}, bf16[88,512]{1,0:T(8,128)(2,1)S(1)}, u32[]{:S(2)}, u32[]{:S(2)}) collective-permute-start(bf16[88,512]{1,0:T(8,128)(2,1)S(1)} %pad_maximum_fusion.3), channel_id=1, source_target_pairs={{0,48},{16,32},{32,16},{48,0},{1,49},{17,33},{33,17},{49,1},{2,50}... | collective-permute-start | bytes 270344 | tf_op jit(solution)/shard_map/ppermute | solution.py:27
  10.4 8.5 %collective-permute-start.8 = (bf16[88,512]{1,0:T(8,128)(2,1)S(1)}, bf16[88,512]{1,0:T(8,128)(2,1)S(1)}, u32[]{:S(2)}, u32[]{:S(2)}) collective-permute-start(bf16[88,512]{1,0:T(8,128)(2,1)S(1)} %pad_maximum_fusion.3), channel_id=1, source_target_pairs={{0,32},{16,48},{32,0},{48,16},{1,33},{17,49},{33,1},{49,17},{2,34}... | collective-permute-start | bytes 270344 | tf_op jit(solution)/shard_map/ppermute | solution.py:27
  18.9 6.4 %collective-permute-start.10 = (bf16[4,1,88,512]{3,2,1,0:T(8,128)(2,1)S(1)}, bf16[4,1,88,512]{3,2,1,0:T(8,128)(2,1)S(1)}, u32[]{:S(2)}, u32[]{:S(2)}) collective-permute-start(bf16[4,1,88,512]{3,2,1,0:T(8,128)(2,1)S(1)} %bitcast.9), channel_id=1, source_target_pairs={{0,8},{8,0},{1,9},{9,1},{2,10},{10,2},{3,11},{11,3},{4,12},{12,4},... | collective-permute-start | bytes 1081352 | tf_op jit(solution)/shard_map/ppermute | solution.py:27
  25.5 21.7 %copy-start.5 = (bf16[384,640]{1,0:T(8,128)(2,1)S(1)}, bf16[384,640]{1,0:T(8,128)(2,1)}, u32[]{:S(2)}) copy-start(bf16[384,640]{1,0:T(8,128)(2,1)} %refs_0_.1) | copy-start | bytes 1474564
  25.6 94.1 %copy-start = (bf16[656,512]{1,0:T(8,128)(2,1)}, bf16[656,512]{1,0:T(8,128)(2,1)S(1)}, u32[]{:S(2)}) copy-start(bf16[656,512]{1,0:T(8,128)(2,1)S(1)} %maximum_maximum_fusion.refs_8_) | copy-start | bytes 2015236
  25.6 16.6 %collective-permute-start.11 = (bf16[656,512]{1,0:T(8,128)(2,1)S(1)}, bf16[656,512]{1,0:T(8,128)(2,1)S(1)}, u32[]{:S(2)}, u32[]{:S(2)}) collective-permute-start(bf16[656,512]{1,0:T(8,128)(2,1)S(1)} %maximum_maximum_fusion.refs_8_), channel_id=1, source_target_pairs={{0,64},{8,456},{64,128},{72,8},{128,192},{136,72},{192,256},{200,1... | collective-permute-start | bytes 2015240 | tf_op jit(solution)/shard_map/ppermute | solution.py:39
  42.2 77.6 %copy-start.1 = (bf16[656,512]{1,0:T(8,128)(2,1)}, bf16[656,512]{1,0:T(8,128)(2,1)S(1)}, u32[]{:S(2)}) copy-start(bf16[656,512]{1,0:T(8,128)(2,1)S(1)} %collective-permute-done.11.refs_9_) | copy-start | bytes 2015236
  42.2 15.9 %collective-permute-start.12 = (bf16[656,512]{1,0:T(8,128)(2,1)S(1)}, bf16[656,512]{1,0:T(8,128)(2,1)S(1)}, u32[]{:S(2)}, u32[]{:S(2)}) collective-permute-start(bf16[656,512]{1,0:T(8,128)(2,1)S(1)} %collective-permute-done.11.refs_9_), channel_id=1, source_target_pairs={{0,64},{8,456},{64,128},{72,8},{128,192},{136,72},{192,256},{200,1... | collective-permute-start | bytes 2015240 | tf_op jit(solution)/shard_map/ppermute | solution.py:39
  47.2 28.6 %collective-permute-start.3 = (bf16[384,640]{1,0:T(8,128)(2,1)S(1)}, bf16[384,640]{1,0:T(8,128)(2,1)}, u32[]{:S(2)}, u32[]{:S(2)}) collective-permute-start(bf16[384,640]{1,0:T(8,128)(2,1)S(1)} %copy-done.5), channel_id=1, source_target_pairs={{0,1},{1,0},{2,3},{3,2},{4,5},{5,4},{6,7},{7,6},{8,9},{9,8},{10,11... | collective-permute-start | bytes 1474568 | tf_op jit(solution)/shard_map/ppermute | solution.py:27
  53.5 27.0 %collective-permute-start.2 = (bf16[384,640]{1,0:T(8,128)(2,1)S(1)}, bf16[384,640]{1,0:T(8,128)(2,1)S(1)}, u32[]{:S(2)}, u32[]{:S(2)}) collective-permute-start(bf16[384,640]{1,0:T(8,128)(2,1)S(1)} %copy-done.5), channel_id=1, source_target_pairs={{0,4},{2,6},{4,0},{6,2},{1,5},{3,7},{5,1},{7,3},{8,12},{10,14},{12... | collective-permute-start | bytes 1474568 | tf_op jit(solution)/shard_map/ppermute | solution.py:31
  58.1 61.6 %copy-start.2 = (bf16[656,512]{1,0:T(8,128)(2,1)}, bf16[656,512]{1,0:T(8,128)(2,1)S(1)}, u32[]{:S(2)}) copy-start(bf16[656,512]{1,0:T(8,128)(2,1)S(1)} %collective-permute-done.12.refs_10_) | copy-start | bytes 2015236
  58.1 29.5 %collective-permute-start.13 = (bf16[656,512]{1,0:T(8,128)(2,1)S(1)}, bf16[656,512]{1,0:T(8,128)(2,1)S(1)}, u32[]{:S(2)}, u32[]{:S(2)}) collective-permute-start(bf16[656,512]{1,0:T(8,128)(2,1)S(1)} %collective-permute-done.12.refs_10_), channel_id=1, source_target_pairs={{0,64},{8,456},{64,128},{72,8},{128,192},{136,72},{192,256},{200,1... | collective-permute-start | bytes 2015240 | tf_op jit(solution)/shard_map/ppermute | solution.py:39
  60.1 23.2 %collective-permute-start.1 = (bf16[384,640]{1,0:T(8,128)(2,1)S(1)}, bf16[384,640]{1,0:T(8,128)(2,1)S(1)}, u32[]{:S(2)}, u32[]{:S(2)}) collective-permute-start(bf16[384,640]{1,0:T(8,128)(2,1)S(1)} %copy-done.5), channel_id=1, source_target_pairs={{0,6},{2,0},{4,2},{6,4},{1,7},{3,1},{5,3},{7,5},{8,14},{10,8},{12,... | collective-permute-start | bytes 1474568 | tf_op jit(solution)/shard_map/ppermute | solution.py:31
  64.3 21.2 %collective-permute-start = (bf16[384,640]{1,0:T(8,128)(2,1)S(1)}, bf16[384,640]{1,0:T(8,128)(2,1)S(1)}, u32[]{:S(2)}, u32[]{:S(2)}) collective-permute-start(bf16[384,640]{1,0:T(8,128)(2,1)S(1)} %copy-done.5), channel_id=1, source_target_pairs={{0,2},{2,4},{4,6},{6,0},{1,3},{3,5},{5,7},{7,1},{8,10},{10,12},{12... | collective-permute-start | bytes 1474568 | tf_op jit(solution)/shard_map/ppermute | solution.py:31
  75.8 16.6 %collective-permute-start.6 = (bf16[384,640]{1,0:T(8,128)(2,1)}, bf16[384,640]{1,0:T(8,128)(2,1)S(1)}, u32[]{:S(2)}, u32[]{:S(2)}) collective-permute-start(bf16[384,640]{1,0:T(8,128)(2,1)} %collective-permute-done.3.refs_4_), channel_id=1, source_target_pairs={{0,4},{2,6},{4,0},{6,2},{1,5},{3,7},{5,1},{7,3},{8,12},{10,14},{12... | collective-permute-start | bytes 1474568 | tf_op jit(solution)/shard_map/ppermute | solution.py:31
  80.5 22.7 %collective-permute-start.5 = (bf16[384,640]{1,0:T(8,128)(2,1)}, bf16[384,640]{1,0:T(8,128)(2,1)S(1)}, u32[]{:S(2)}, u32[]{:S(2)}) collective-permute-start(bf16[384,640]{1,0:T(8,128)(2,1)} %collective-permute-done.3.refs_4_), channel_id=1, source_target_pairs={{0,6},{2,0},{4,2},{6,4},{1,7},{3,1},{5,3},{7,5},{8,14},{10,8},{12,... | collective-permute-start | bytes 1474568 | tf_op jit(solution)/shard_map/ppermute | solution.py:31
  83.3 36.4 %collective-permute-start.15 = (bf16[656,512]{1,0:T(8,128)(2,1)S(1)}, bf16[656,512]{1,0:T(8,128)(2,1)S(1)}, u32[]{:S(2)}, u32[]{:S(2)}) collective-permute-start(bf16[656,512]{1,0:T(8,128)(2,1)S(1)} %collective-permute-done.11.refs_9_), channel_id=1, source_target_pairs={{0,8},{8,0},{1,9},{9,1},{2,10},{10,2},{3,11},{11,3},{4,12},{12,4},... | collective-permute-start | bytes 2015240 | tf_op jit(solution)/shard_map/ppermute | solution.py:27
  85.5 34.2 %collective-permute-start.16 = (bf16[656,512]{1,0:T(8,128)(2,1)S(1)}, bf16[656,512]{1,0:T(8,128)(2,1)}, u32[]{:S(2)}, u32[]{:S(2)}) collective-permute-start(bf16[656,512]{1,0:T(8,128)(2,1)S(1)} %collective-permute-done.12.refs_10_), channel_id=1, source_target_pairs={{0,8},{8,0},{1,9},{9,1},{2,10},{10,2},{3,11},{11,3},{4,12},{12,4},... | collective-permute-start | bytes 2015240 | tf_op jit(solution)/shard_map/ppermute | solution.py:27
  87.7 32.1 %copy-start.3 = (bf16[656,512]{1,0:T(8,128)(2,1)}, bf16[656,512]{1,0:T(8,128)(2,1)S(1)}, u32[]{:S(2)}) copy-start(bf16[656,512]{1,0:T(8,128)(2,1)S(1)} %collective-permute-done.13.refs_11_) | copy-start | bytes 2015236
  87.7 32.0 %collective-permute-start.17 = (bf16[656,512]{1,0:T(8,128)(2,1)S(1)}, bf16[656,512]{1,0:T(8,128)(2,1)}, u32[]{:S(2)}, u32[]{:S(2)}) collective-permute-start(bf16[656,512]{1,0:T(8,128)(2,1)S(1)} %collective-permute-done.13.refs_11_), channel_id=1, source_target_pairs={{0,8},{8,0},{1,9},{9,1},{2,10},{10,2},{3,11},{11,3},{4,12},{12,4},... | collective-permute-start | bytes 2015240 | tf_op jit(solution)/shard_map/ppermute | solution.py:27
  92.5 27.3 %collective-permute-start.14 = (bf16[656,512]{1,0:T(8,128)(2,1)S(1)}, bf16[656,512]{1,0:T(8,128)(2,1)}, u32[]{:S(2)}, u32[]{:S(2)}) collective-permute-start(bf16[656,512]{1,0:T(8,128)(2,1)S(1)} %collective-permute-done.13.refs_11_), channel_id=1, source_target_pairs={{0,64},{8,456},{64,128},{72,8},{128,192},{136,72},{192,256},{200,1... | collective-permute-start | bytes 2015240 | tf_op jit(solution)/shard_map/ppermute | solution.py:39
  104.0 15.7 %collective-permute-start.4 = (bf16[384,640]{1,0:T(8,128)(2,1)}, bf16[384,640]{1,0:T(8,128)(2,1)}, u32[]{:S(2)}, u32[]{:S(2)}) collective-permute-start(bf16[384,640]{1,0:T(8,128)(2,1)} %collective-permute-done.3.refs_4_), channel_id=1, source_target_pairs={{0,2},{2,4},{4,6},{6,0},{1,3},{3,5},{5,7},{7,1},{8,10},{10,12},{12... | collective-permute-start | bytes 1474568 | tf_op jit(solution)/shard_map/ppermute | solution.py:31
  131.8 19.0 %all-to-all-start = ((f32[64,4,256]{2,1,0:T(4,128)}), f32[64,4,256]{2,1,0:T(4,128)S(1)}, u32[]{:S(2)}, u32[]{:S(2)}) async-start(f32[64,4,256]{2,1,0:T(4,128)} %get-tuple-element.28), calls=%async_computation | async-start | bytes 524288 | tf_op jit(solution)/shard_map/all_to_all | solution.py:260
  (6 other events, 39.8 us)

commit v4 on v3

--- a/solution.py
+++ b/solution.py
@@ -14,6 +14,8 @@
 SCALE = HD**-0.5
 KB = 640
 TAIL = 16
+PIECE = KB + TAIL
+HALF = KB // 2
 F32 = jnp.float32
 BF16 = jnp.bfloat16
 ROLL = ("z", "yl", "c")
@@ -79,43 +81,34 @@
     return open_part * share, edge * share
 
 
-def front_kernel(place_ref, length_ref, *refs):
-    g_in, w_in, in_refs = refs[:8], refs[8:16], refs[16:19]
-    gp_ref, out_refs = refs[19], refs[20:28]
-    q_ref, rk_ref, rv_ref = refs[28:31]
+def front_kernel(length_ref, *refs):
+    g_in, a_in, b_in, across = refs[:8], refs[8:13], refs[13:18], refs[18]
+    q_ref, rk_ref, rv_ref = refs[19:22]
+    gp_ref, out_refs = refs[22], refs[23:31]
     og_ref, s0, s1, s2, l0, l1, l2, pkv_ref = refs[31:39]
-    g_buf, w_buf, p_buf0, p_buf1, p_buf2 = refs[39:44]
-    sem, w_sem, tail_sem, out_sem, g_sem = refs[44:]
-    small = [
-        pltpu.make_async_copy(src, dst, sem.at[2 + k])
-        for k, (src, dst) in enumerate(zip(in_refs, (q_ref, rk_ref, rv_ref)))
-    ]
+    w_buf, p_buf0, p_buf1, p_buf2, out_sem = refs[39:]
     outs = [
         pltpu.make_async_copy(src, dst, out_sem.at[k])
         for k, (src, dst) in enumerate(
             zip((og_ref, s0, s1, s2, l0, l1, l2, pkv_ref), out_refs)
         )
     ]
-    yh, z, core, x = place_ref[0], place_ref[1], place_ref[2], place_ref[3]
+    yh, z = lax.axis_index("yh"), lax.axis_index("z")
+    core, x = lax.axis_index("c"), lax.axis_index("x")
     way = 1 - 2 * core
     p_bufs = (p_buf0, p_buf1, p_buf2)
     steps = (0, -way, -2 * way, -3 * way, 4, way, 2 * way, 3 * way)
-    copies, tails = [], []
-    for k, (src, step) in enumerate(zip(w_in, steps)):
+    for k, step in enumerate(steps):
         to = lax.rem(z + step + 8, 8)
         place = pl.ds(pl.multiple_of(TAIL * to, TAIL), TAIL)
-        tails.append(
-            pltpu.make_async_copy(src.at[pl.ds(KB, TAIL)], pkv_ref.at[place], tail_sem.at[k])
-        )
-        copies.append(pltpu.make_async_copy(src.at[pl.ds(0, KB)], w_buf.at[to], w_sem.at[k]))
-    for k, src in enumerate(g_in):
-        side = yh if k < 4 else 1 - yh
-        dst = g_buf.at[side, lax.rem(x - (0, 1, 3, 2)[k % 4] + 4, 4)]
-        copies.append(pltpu.make_async_copy(src, dst, g_sem.at[k]))
-    for c in small + tails + copies:
-        c.start()
-    for c in small + tails:
-        c.wait()
+        if k < 5:
+            first, second, at, then = a_in[k], b_in[k], 0, 0
+        else:
+            first, second, at = across, across, (k - 5) * PIECE
+            then = at + HALF + TAIL
+        pkv_ref[place] = first[at + HALF : at + HALF + TAIL]
+        w_buf[to, :HALF] = first[at : at + HALF]
+        w_buf[to, HALF:] = second[then : then + HALF]
     outs[7].start()
     keys = jnp.concatenate([prefix_part(pkv_ref, 0), rk_ref[...]], axis=0)
     for i, (p_ref, l_ref) in enumerate(zip(p_bufs, (l0, l1, l2))):
@@ -127,10 +120,11 @@
         l_ref[BLOCK * i :] = edge.astype(BF16)
         outs[4 + i].start()
 
-    for c in copies:
-        c.wait()
-    grow = jnp.concatenate([g_buf[t % 2, t // 2] for t in range(8)], axis=1)
-    total = jnp.dot(grow, w_buf[...].reshape(5120, 512), preferred_element_type=F32)
+    total = jnp.zeros((ROWS, 512), F32)
+    for k, src in enumerate(g_in):
+        side = yh if k < 4 else 1 - yh
+        block = 2 * lax.rem(x - (0, 1, 3, 2)[k % 4] + 4, 4) + side
+        total += jnp.dot(src[...], w_buf[block], preferred_element_type=F32)
     row = lax.broadcasted_iota(jnp.int32, (ROWS, GROUP * HD), 0)
     out_grad = jnp.where(row < length_ref[0], total, 0.0).astype(BF16)
     for i in range(3):
@@ -155,8 +149,8 @@
         key_grad += jnp.dot(score_low[:PREFIX], stacked(q_ref, i), preferred_element_type=F32)
         value_grad += jnp.dot(weights[:PREFIX].astype(BF16), grads, preferred_element_type=F32)
     for j in range(PREFIX // 4):
-        gp_ref[j, :, :HD] = key_grad[4 * j : 4 * j + 4]
-        gp_ref[j, :, HD:] = value_grad[4 * j : 4 * j + 4]
+        gp_ref[j, :, :HD] = key_grad[4 * j : 4 * j + 4].astype(BF16)
+        gp_ref[j, :, HD:] = value_grad[4 * j : 4 * j + 4].astype(BF16)
     for c in outs:
         c.wait()
 
@@ -190,76 +184,82 @@
 VM = pl.BlockSpec(memory_space=pltpu.VMEM)
 SM = pl.BlockSpec(memory_space=pltpu.SMEM)
 ANY = pl.BlockSpec(memory_space=pl.ANY)
+VMEM_MIB = {"front": 34, "back": 59}
 WIDTHS = tuple(PREFIX + BLOCK * (i + 1) for i in range(3))
 
 
-def call(kernel, outs, in_specs, args, flops, scratch=(), out_specs=None):
+def call(kernel, name, outs, in_specs, args, flops, scratch=(), out_specs=None):
     return pl.pallas_call(
         kernel,
-        out_shape=[jax.ShapeDtypeStruct(s, d) for s, d in outs],
+        out_shape=[
+            pltpu.HBM(s, d) if out_specs and k else jax.ShapeDtypeStruct(s, d)
+            for k, (s, d) in enumerate(outs)
+        ],
         in_specs=in_specs,
         out_specs=out_specs or [VM] * len(outs),
         scratch_shapes=scratch,
         cost_estimate=pl.CostEstimate(flops=flops, bytes_accessed=4000000, transcendentals=0),
+        compiler_params=pltpu.CompilerParams(vmem_limit_bytes=VMEM_MIB[name] << 20),
     )(*args)
 
 
-def front(place, lengths, g, w, queries, resp_key, resp_value):
-    outs = [((64, 4, 2 * HD), F32), ((GROUP * ROWS, HD), BF16)]
+def front(lengths, g, w, queries, resp_key, resp_value):
+    outs = [((64, 4, 2 * HD), BF16), ((GROUP * ROWS, HD), BF16)]
     outs += [((w, GROUP * BLOCK), BF16) for w in WIDTHS]
     outs += [((w - PREFIX, GROUP * BLOCK), BF16) for w in WIDTHS]
     outs += [((NZ * TAIL, 512), BF16)]
     return call(
         front_kernel,
+        "front",
         outs,
-        [SM] * 2 + [ANY] * 19,
-        (place, lengths, *g, *w, queries, resp_key, resp_value),
+        [SM] + [VM] * 22,
+        (lengths, *g, *w, queries, resp_key, resp_value),
         2 * 384 * 5120 * 512,
-        [pltpu.VMEM((ROWS, n), BF16) for n in (512, HD, HD)]
-        + [pltpu.VMEM(*o) for o in outs[1:]]
-        + [pltpu.VMEM((2, NX, ROWS, KB), BF16), pltpu.VMEM((8, KB, 512), BF16)]
+        [pltpu.VMEM(*o) for o in outs[1:]]
+        + [pltpu.VMEM((8, KB, 512), BF16)]
         + [pltpu.VMEM((w, GROUP * BLOCK), F32) for w in WIDTHS]
-        + [pltpu.SemaphoreType.DMA((8,)) for _ in range(5)],
-        [VM] + [ANY] * 8,
+        + [pltpu.SemaphoreType.DMA((8,))],
+        [VM] + [pl.BlockSpec(memory_space=pltpu.HBM)] * 8,
     )
 
 
 def back(og, s, low, queries, resp_key, prefix):
     outs = [((ROWS, GROUP * HD), BF16), ((ROWS, HD), BF16), ((ROWS, HD), BF16)]
-    return call(back_kernel, outs, [VM] * 10, (og, *s, *low, queries, resp_key, prefix), 1 << 30)
+    return call(
+        back_kernel, "back", outs, [VM] * 10, (og, *s, *low, queries, resp_key, prefix), 1 << 30
+    )
 
 
 def steps(grad_out, out_weight, queries, resp_key, resp_value, prefix_key, prefix_value, lengths):
-    x, yh, yl = lax.axis_index("x"), lax.axis_index("yh"), lax.axis_index("yl")
-    z, core = lax.axis_index("z"), lax.axis_index("c")
+    core = lax.axis_index("c")
     both = jnp.concatenate([prefix_key, prefix_value], axis=1)
 
     shard = jnp.concatenate([out_weight, jnp.pad(both, ((0, 4), (0, 256)))], axis=0)
-    shards = [shard] + [swap(shard, "yl", k) for k in (1, 2, 3)]
-    near = in_pair(shards[0], shards[1], yl % 2, 0)
-    far = in_pair(shards[2], shards[3], yl % 2, 0)
-    four = in_pair(near, far, yl // 2, 0).reshape(4, 1, 88, 512)
+    four = lax.all_to_all(jnp.broadcast_to(shard[None], (NY, 88, 512)), "yl", 0, 0, tiled=True)
+    four = four[:, None]
     pair = in_pair(four, swap(four, "c"), core, 1)
     tail = pair[:, :, 80:84, :256].reshape(2, TAIL, 256)
-    piece = jnp.concatenate(
-        [pair[:, :, :80].reshape(KB, 512), jnp.concatenate([tail[0], tail[1]], axis=1)], axis=0
-    )
+    rows = pair[:, :, :80].reshape(KB, 512)
+    tail = jnp.concatenate([tail[0], tail[1]], axis=1)
+    near, then = [jnp.concatenate([rows[:HALF], tail], axis=0)], [rows[HALF:]]
+    for _ in range(1, 5):
+        near.append(ring_z(near[-1]))
+        then.append(ring_z(then[-1]))
+
     def along_x(v):
         return [v] + [shift_x(v, k) for k in (1, 3, 2)]
 
     g = along_x(grad_out) + along_x(swap(grad_out, "yh"))
-    aheads = [piece]
-    for _ in range(4):
-        aheads.append(ring_z(aheads[-1]))
-    across = [swap(aheads[k], "c") for k in (1, 2, 3)]
-    place = jnp.stack([yh, z, core, x]).astype(jnp.int32)
+    joined = [half for k in (1, 2, 3) for half in (near[k], then[k])]
+    joined = jnp.concatenate(joined, axis=0)
+    across = swap(joined, "c")
     gp, og, *rest = front(
-        place, lengths, g, (*aheads, *across), queries, resp_key, resp_value
+        lengths, g, (*near, *then, across), queries, resp_key, resp_value
     )
     s, low, prefix = rest[:3], rest[3:6], rest[6]
     parts = lax.all_to_all(gp, ROLL, 0, 0, tiled=True)
     gq, grk, grv = back(og, s, low, queries, resp_key, prefix)
-    total = jnp.sum(parts, axis=0)
+    total = jnp.sum(parts.astype(F32), axis=0)
     return gq, grk, grv, total[:, :HD], total[:, HD:]
 
 

time: 152 us -> 148 us (0.974)
  waiting for transfers between devices: 56.7 us -> 41.9 us
  blocking collectives: 0 us -> 12.7 us
  starting transfers between devices: 72.5 us -> 77.4 us
  Pallas kernels: 14.8 us -> 10.7 us
  other arithmetic: 3.49 us -> 1.83 us
    ppermute x4 -> x8, starting transfers between devices: 17.7 us -> 33.2 us  [ring_z(): return lax.ppermute(v, ('z', 'c'), pairs)]
    all_to_all x0 -> x1, blocking collectives: none -> 12.7 us  [steps(): lax.all_to_all(jnp.broadcast_to(shard[None], (NY, 88, 512)), 'yl', 0, 0,...]
    ppermute x8 -> x3, starting transfers between devices: 28.1 us -> 17.8 us  [swap(): return lax.ppermute(v, axis, [(i, i ^ bit) for i in range(size)])]
    ppermute x6, waiting for transfers between devices: 22.7 us -> 12.6 us  [shift_x(): return lax.ppermute(v, 'x', [(x, (x + step) % NX) for x in range(NX)])]
    pallas_call x2, Pallas kernels: 14.8 us -> 10.7 us  [call(): pl.pallas_call(kernel, out_shape=[pltpu.HBM(s, d) if out_specs and k else...]
    all_to_all x1, waiting for transfers between devices: 10.1 us -> 7.25 us  [steps(): parts = lax.all_to_all(gp, ROLL, 0, 0, tiled=True)]
    ppermute x8 -> x3, waiting for transfers between devices: 16.3 us -> 15 us  [swap(): return lax.ppermute(v, axis, [(i, i ^ bit) for i in range(size)])]
    ppermute x4 -> x8, waiting for transfers between devices: 7.69 us -> 7 us  [ring_z(): return lax.ppermute(v, ('z', 'c'), pairs)]
  transfers between devices with their start and end apart: 19 -> 18, of which waited for: 8 -> 10; matrix products, arithmetic and copies ran while one was open for 1% -> 0% of each run, Pallas kernels for 2% -> 2%
where the time goes in v4:
time: 148 us; the launch traced here: 147 us
  starting transfers between devices  77.4 us (52%)
  waiting for transfers between devices  41.9 us (28%)
  blocking collectives  12.7 us (9%)
  Pallas kernels  10.7 us (7%)
  other arithmetic  1.83 us (1%)
  between operations  1.62 us (1%)
    ppermute x8, starting transfers between devices, ring_z(): return lax.ppermute(v, ('z', 'c'), pairs)  33.2 us
    ppermute x6, starting transfers between devices, shift_x(): return lax.ppermute(v, 'x', [(x, (x + step) % NX) for x in range(NX)])  19.9 us
    ppermute x3, starting transfers between devices, swap(): return lax.ppermute(v, axis, [(i, i ^ bit) for i in range(size)])  17.8 us
    ppermute x3, waiting for transfers between devices, swap(): return lax.ppermute(v, axis, [(i, i ^ bit) for i in range(size)])  15 us
    all_to_all x1, blocking collectives, steps(): lax.all_to_all(jnp.broadcast_to(shard[None], (NY, 88, 512)), 'yl', 0, 0,...  12.7 us
    ppermute x6, waiting for transfers between devices, shift_x(): return lax.ppermute(v, 'x', [(x, (x + step) % NX) for x in range(NX)])  12.6 us
    pallas_call x2, Pallas kernels, call(): pl.pallas_call(kernel, out_shape=[pltpu.HBM(s, d) if out_specs and k else...  10.7 us
    all_to_all x1, waiting for transfers between devices, steps(): parts = lax.all_to_all(gp, ROLL, 0, 0, tiled=True)  7.25 us
  transfers between devices with their start and end apart: 18, of which 10 were waited for; matrix products, arithmetic and copies ran while one was open for 0% of the time, Pallas kernels for 2%

profile of v4, /device:TPU:1, one launch (start us, length us, event | category | flops | bytes accessed | tf_op | source)
XLA Modules:
  0.0 146.9 jit_solution(9852024619774542965)
XLA Ops:
  2.3 12.7 %all_to_all.10 = bf16[4,88,512]{2,1,0:T(8,128)(2,1)S(1)} all-to-all(bf16[4,88,512]{2,1,0:T(8,128)(2,1)S(1)} %broadcast_in_dim.4), channel_id=1, replica_groups=mesh['z'=8,'yl'=4,'c'=2,'x'=4,'yh'=2] {'yl'}, dimensions={0} | all-to-all | bytes 720896 | tf_op jit(solution)/shard_map/all_to_all | solution.py:238
  15.0 7.0 %collective-permute-start.7 = (bf16[4,1,88,512]{3,2,1,0:T(8,128)(2,1)S(1)}, bf16[4,1,88,512]{3,2,1,0:T(8,128)(2,1)S(1)}, u32[]{:S(2)}, u32[]{:S(2)}) collective-permute-start(bf16[4,1,88,512]{3,2,1,0:T(8,128)(2,1)S(1)} %bitcast.7), channel_id=1, source_target_pairs={{0,8},{8,0},{1,9},{9,1},{2,10},{10,2},{3,11},{11,3},{4,12},{12,4},... | collective-permute-start | bytes 1081352 | tf_op jit(solution)/shard_map/ppermute | solution.py:29
  23.4 10.1 %collective-permute-start.8 = (bf16[336,512]{1,0:T(8,128)(2,1)S(1)}, bf16[336,512]{1,0:T(8,128)(2,1)S(1)}, u32[]{:S(2)}, u32[]{:S(2)}) collective-permute-start(bf16[336,512]{1,0:T(8,128)(2,1)S(1)} %maximum_maximum_fusion.refs_8_), channel_id=1, source_target_pairs={{0,64},{8,456},{64,128},{72,8},{128,192},{136,72},{192,256},{200,1... | collective-permute-start | bytes 1032200 | tf_op jit(solution)/shard_map/ppermute | solution.py:41
  33.5 2.3 %collective-permute-start.12 = (bf16[320,512]{1,0:T(8,128)(2,1)S(1)}, bf16[320,512]{1,0:T(8,128)(2,1)S(1)}, u32[]{:S(2)}, u32[]{:S(2)}) collective-permute-start(bf16[320,512]{1,0:T(8,128)(2,1)S(1)} %bitcast.5), channel_id=1, source_target_pairs={{0,64},{8,456},{64,128},{72,8},{128,192},{136,72},{192,256},{200,1... | collective-permute-start | bytes 983048 | tf_op jit(solution)/shard_map/ppermute | solution.py:41
  37.6 5.0 %collective-permute-start.9 = (bf16[336,512]{1,0:T(8,128)(2,1)S(1)}, bf16[336,512]{1,0:T(8,128)(2,1)S(1)}, u32[]{:S(2)}, u32[]{:S(2)}) collective-permute-start(bf16[336,512]{1,0:T(8,128)(2,1)S(1)} %collective-permute-done.8.refs_9_), channel_id=1, source_target_pairs={{0,64},{8,456},{64,128},{72,8},{128,192},{136,72},{192,256},{200,1... | collective-permute-start | bytes 1032200 | tf_op jit(solution)/shard_map/ppermute | solution.py:41
  42.7 3.5 %collective-permute-start.13 = (bf16[320,512]{1,0:T(8,128)(2,1)S(1)}, bf16[320,512]{1,0:T(8,128)(2,1)S(1)}, u32[]{:S(2)}, u32[]{:S(2)}) collective-permute-start(bf16[320,512]{1,0:T(8,128)(2,1)S(1)} %collective-permute-done.12.refs_14_), channel_id=1, source_target_pairs={{0,64},{8,456},{64,128},{72,8},{128,192},{136,72},{192,256},{200,1... | collective-permute-start | bytes 983048 | tf_op jit(solution)/shard_map/ppermute | solution.py:41
  46.8 5.0 %collective-permute-start.10 = (bf16[336,512]{1,0:T(8,128)(2,1)S(1)}, bf16[336,512]{1,0:T(8,128)(2,1)S(1)}, u32[]{:S(2)}, u32[]{:S(2)}) collective-permute-start(bf16[336,512]{1,0:T(8,128)(2,1)S(1)} %collective-permute-done.9.refs_10_), channel_id=1, source_target_pairs={{0,64},{8,456},{64,128},{72,8},{128,192},{136,72},{192,256},{200,1... | collective-permute-start | bytes 1032200 | tf_op jit(solution)/shard_map/ppermute | solution.py:41
  51.9 3.5 %collective-permute-start.14 = (bf16[320,512]{1,0:T(8,128)(2,1)S(1)}, bf16[320,512]{1,0:T(8,128)(2,1)S(1)}, u32[]{:S(2)}, u32[]{:S(2)}) collective-permute-start(bf16[320,512]{1,0:T(8,128)(2,1)S(1)} %collective-permute-done.13.refs_15_), channel_id=1, source_target_pairs={{0,64},{8,456},{64,128},{72,8},{128,192},{136,72},{192,256},{200,1... | collective-permute-start | bytes 983048 | tf_op jit(solution)/shard_map/ppermute | solution.py:41
  56.0 4.0 %collective-permute-done.14.refs_16_ = bf16[320,512]{1,0:T(8,128)(2,1)S(1)} collective-permute-done((bf16[320,512]{1,0:T(8,128)(2,1)S(1)}, bf16[320,512]{1,0:T(8,128)(2,1)S(1)}, u32[]{:S(2)}, u32[]{:S(2)}) %collective-permute-start.14) | collective-permute-done | bytes 327712 | tf_op jit(solution)/shard_map/ppermute | solution.py:41
  60.0 5.4 %collective-permute-start.16 = (bf16[1968,512]{1,0:T(8,128)(2,1)S(1)}, bf16[1968,512]{1,0:T(8,128)(2,1)S(1)}, u32[]{:S(2)}, u32[]{:S(2)}) collective-permute-start(bf16[1968,512]{1,0:T(8,128)(2,1)S(1)} %constant_dynamic-update-slice_fusion), channel_id=1, source_target_pairs={{0,8},{8,0},{1,9},{9,1},{2,10},{10,2},{3,11},{11,3},{4,12},{12,4},... | collective-permute-start | bytes 6045704 | tf_op jit(solution)/shard_map/ppermute | solution.py:29
  65.5 5.4 %collective-permute-start.3 = (bf16[384,640]{1,0:T(8,128)(2,1)S(1)}, bf16[384,640]{1,0:T(8,128)(2,1)S(1)}, u32[]{:S(2)}, u32[]{:S(2)}) collective-permute-start(bf16[384,640]{1,0:T(8,128)(2,1)S(1)} %copy-done), channel_id=1, source_target_pairs={{0,1},{1,0},{2,3},{3,2},{4,5},{5,4},{6,7},{7,6},{8,9},{9,8},{10,11... | collective-permute-start | bytes 1474568 | tf_op jit(solution)/shard_map/ppermute | solution.py:29
  70.9 4.7 %collective-permute-start.2 = (bf16[384,640]{1,0:T(8,128)(2,1)S(1)}, bf16[384,640]{1,0:T(8,128)(2,1)S(1)}, u32[]{:S(2)}, u32[]{:S(2)}) collective-permute-start(bf16[384,640]{1,0:T(8,128)(2,1)S(1)} %copy-done), channel_id=1, source_target_pairs={{0,4},{2,6},{4,0},{6,2},{1,5},{3,7},{5,1},{7,3},{8,12},{10,14},{12... | collective-permute-start | bytes 1474568 | tf_op jit(solution)/shard_map/ppermute | solution.py:33
  75.6 2.8 %collective-permute-start.1 = (bf16[384,640]{1,0:T(8,128)(2,1)S(1)}, bf16[384,640]{1,0:T(8,128)(2,1)S(1)}, u32[]{:S(2)}, u32[]{:S(2)}) collective-permute-start(bf16[384,640]{1,0:T(8,128)(2,1)S(1)} %copy-done), channel_id=1, source_target_pairs={{0,6},{2,0},{4,2},{6,4},{1,7},{3,1},{5,3},{7,5},{8,14},{10,8},{12,... | collective-permute-start | bytes 1474568 | tf_op jit(solution)/shard_map/ppermute | solution.py:33
  78.4 2.5 %collective-permute-start = (bf16[384,640]{1,0:T(8,128)(2,1)S(1)}, bf16[384,640]{1,0:T(8,128)(2,1)S(1)}, u32[]{:S(2)}, u32[]{:S(2)}) collective-permute-start(bf16[384,640]{1,0:T(8,128)(2,1)S(1)} %copy-done), channel_id=1, source_target_pairs={{0,2},{2,4},{4,6},{6,0},{1,3},{3,5},{5,7},{7,1},{8,10},{10,12},{12... | collective-permute-start | bytes 1474568 | tf_op jit(solution)/shard_map/ppermute | solution.py:33
  80.9 13.8 %collective-permute-done.3.refs_4_ = bf16[384,640]{1,0:T(8,128)(2,1)S(1)} collective-permute-done((bf16[384,640]{1,0:T(8,128)(2,1)S(1)}, bf16[384,640]{1,0:T(8,128)(2,1)S(1)}, u32[]{:S(2)}, u32[]{:S(2)}) %collective-permute-start.3) | collective-permute-done | bytes 491552 | tf_op jit(solution)/shard_map/ppermute | solution.py:29
  94.7 4.6 %collective-permute-start.6 = (bf16[384,640]{1,0:T(8,128)(2,1)S(1)}, bf16[384,640]{1,0:T(8,128)(2,1)S(1)}, u32[]{:S(2)}, u32[]{:S(2)}) collective-permute-start(bf16[384,640]{1,0:T(8,128)(2,1)S(1)} %collective-permute-done.3.refs_4_), channel_id=1, source_target_pairs={{0,4},{2,6},{4,0},{6,2},{1,5},{3,7},{5,1},{7,3},{8,12},{10,14},{12... | collective-permute-start | bytes 1474568 | tf_op jit(solution)/shard_map/ppermute | solution.py:33
  99.3 2.8 %collective-permute-start.5 = (bf16[384,640]{1,0:T(8,128)(2,1)S(1)}, bf16[384,640]{1,0:T(8,128)(2,1)S(1)}, u32[]{:S(2)}, u32[]{:S(2)}) collective-permute-start(bf16[384,640]{1,0:T(8,128)(2,1)S(1)} %collective-permute-done.3.refs_4_), channel_id=1, source_target_pairs={{0,6},{2,0},{4,2},{6,4},{1,7},{3,1},{5,3},{7,5},{8,14},{10,8},{12,... | collective-permute-start | bytes 1474568 | tf_op jit(solution)/shard_map/ppermute | solution.py:33
  102.1 2.5 %collective-permute-start.4 = (bf16[384,640]{1,0:T(8,128)(2,1)S(1)}, bf16[384,640]{1,0:T(8,128)(2,1)S(1)}, u32[]{:S(2)}, u32[]{:S(2)}) collective-permute-start(bf16[384,640]{1,0:T(8,128)(2,1)S(1)} %collective-permute-done.3.refs_4_), channel_id=1, source_target_pairs={{0,2},{2,4},{4,6},{6,0},{1,3},{3,5},{5,7},{7,1},{8,10},{10,12},{12... | collective-permute-start | bytes 1474568 | tf_op jit(solution)/shard_map/ppermute | solution.py:33
  106.6 3.4 %collective-permute-done.6.refs_7_ = bf16[384,640]{1,0:T(8,128)(2,1)S(1)} collective-permute-done((bf16[384,640]{1,0:T(8,128)(2,1)S(1)}, bf16[384,640]{1,0:T(8,128)(2,1)S(1)}, u32[]{:S(2)}, u32[]{:S(2)}) %collective-permute-start.6) | collective-permute-done | bytes 491552 | tf_op jit(solution)/shard_map/ppermute | solution.py:33
  112.5 8.3 %collective-permute-done.5.refs_6_ = bf16[384,640]{1,0:T(8,128)(2,1)S(1)} collective-permute-done((bf16[384,640]{1,0:T(8,128)(2,1)S(1)}, bf16[384,640]{1,0:T(8,128)(2,1)S(1)}, u32[]{:S(2)}, u32[]{:S(2)}) %collective-permute-start.5) | collective-permute-done | bytes 491552 | tf_op jit(solution)/shard_map/ppermute | solution.py:33
  121.8 7.1 %shard_map.119 = (bf16[64,4,256]{2,1,0:T(4,128)(2,1)}, bf16[1536,128]{1,0:T(8,128)(2,1)}, bf16[384,512]{1,0:T(8,128)(2,1)}, bf16[512,512]{1,0:T(8,128)(2,1)}, bf...) custom-call(s32[1]{0:T(128)S(6)} %copy.18.length_ref, ...), custom_call_target="tpu_custom_call" | custom-call | flops 2013265920 | bytes 4000000 | tf_op jit(solution)/shard_map/pallas_call | solution.py:192
  128.9 6.6 %all-to-all-start.1 = ((bf16[64,4,256]{2,1,0:T(4,128)(2,1)}), bf16[64,4,256]{2,1,0:T(4,128)(2,1)S(1)}, u32[]{:S(2)}, u32[]{:S(2)}) async-start(bf16[64,4,256]{2,1,0:T(4,128)(2,1)} %get-tuple-element.28), calls=%async_computation.1 | async-start | bytes 262144 | tf_op jit(solution)/shard_map/all_to_all | solution.py:260
  135.4 3.6 %shard_map.120 = (bf16[384,512]{1,0:T(8,128)(2,1)}, bf16[384,128]{1,0:T(8,128)(2,1)}, bf16[384,128]{1,0:T(8,128)(2,1)}) custom-call(bf16[1536,128]{1,0:T(8,128)(2,1)} %get-tuple-element.17.og_ref, bf16[384,512]{1,0:T(8,128)(2,1)} %get-tuple-element.18.s0, bf16[512,512]{1,0:T(8,128)(2,1)} %get-tuple-element.19.s1, bf16[640,512]{1,0:T(8,128)(2,1)} %get-tuple-element.20.s2, ...), custom_call_target="tpu_custom_call" | custom-call | flops 1073741824 | bytes 4000000 | tf_op jit(solution)/shard_map/pallas_call | solution.py:192
  139.0 7.3 %all-to-all-done.1 = bf16[64,4,256]{2,1,0:T(4,128)(2,1)S(1)} async-done(((bf16[64,4,256]{2,1,0:T(4,128)(2,1)}), bf16[64,4,256]{2,1,0:T(4,128)(2,1)S(1)}, u32[]{:S(2)}, u32[]{:S(2)}) %all-to-all-start.1) | async-done | bytes 131104 | tf_op jit(solution)/shard_map/all_to_all | solution.py:260
  (40 shorter events, 11.7 us)
Async XLA Ops:
  15.0 8.2 %collective-permute-start.7 = (bf16[4,1,88,512]{3,2,1,0:T(8,128)(2,1)S(1)}, bf16[4,1,88,512]{3,2,1,0:T(8,128)(2,1)S(1)}, u32[]{:S(2)}, u32[]{:S(2)}) collective-permute-start(bf16[4,1,88,512]{3,2,1,0:T(8,128)(2,1)S(1)} %bitcast.7), channel_id=1, source_target_pairs={{0,8},{8,0},{1,9},{9,1},{2,10},{10,2},{3,11},{11,3},{4,12},{12,4},... | collective-permute-start | bytes 1081352 | tf_op jit(solution)/shard_map/ppermute | solution.py:29
  23.4 14.2 %collective-permute-start.8 = (bf16[336,512]{1,0:T(8,128)(2,1)S(1)}, bf16[336,512]{1,0:T(8,128)(2,1)S(1)}, u32[]{:S(2)}, u32[]{:S(2)}) collective-permute-start(bf16[336,512]{1,0:T(8,128)(2,1)S(1)} %maximum_maximum_fusion.refs_8_), channel_id=1, source_target_pairs={{0,64},{8,456},{64,128},{72,8},{128,192},{136,72},{192,256},{200,1... | collective-permute-start | bytes 1032200 | tf_op jit(solution)/shard_map/ppermute | solution.py:41
  33.5 32.0 %copy-start = (bf16[384,640]{1,0:T(8,128)(2,1)S(1)}, bf16[384,640]{1,0:T(8,128)(2,1)}, u32[]{:S(2)}) copy-start(bf16[384,640]{1,0:T(8,128)(2,1)} %refs_0_.1) | copy-start | bytes 1474564
  33.5 88.3 %copy-start.1 = (bf16[384,512]{1,0:T(8,128)(2,1)S(1)}, bf16[384,512]{1,0:T(8,128)(2,1)}, u32[]{:S(2)}) copy-start(bf16[384,512]{1,0:T(8,128)(2,1)} %q_ref.1) | copy-start | bytes 1179652
  33.5 88.3 %copy-start.2 = (bf16[384,128]{1,0:T(8,128)(2,1)S(1)}, bf16[384,128]{1,0:T(8,128)(2,1)}, u32[]{:S(2)}) copy-start(bf16[384,128]{1,0:T(8,128)(2,1)} %refs_21_.1) | copy-start | bytes 294916
  33.5 88.3 %copy-start.3 = (bf16[384,128]{1,0:T(8,128)(2,1)S(1)}, bf16[384,128]{1,0:T(8,128)(2,1)}, u32[]{:S(2)}) copy-start(bf16[384,128]{1,0:T(8,128)(2,1)} %rk_ref.1) | copy-start | bytes 294916
  33.5 9.1 %collective-permute-start.12 = (bf16[320,512]{1,0:T(8,128)(2,1)S(1)}, bf16[320,512]{1,0:T(8,128)(2,1)S(1)}, u32[]{:S(2)}, u32[]{:S(2)}) collective-permute-start(bf16[320,512]{1,0:T(8,128)(2,1)S(1)} %bitcast.5), channel_id=1, source_target_pairs={{0,64},{8,456},{64,128},{72,8},{128,192},{136,72},{192,256},{200,1... | collective-permute-start | bytes 983048 | tf_op jit(solution)/shard_map/ppermute | solution.py:41
  37.6 9.2 %collective-permute-start.9 = (bf16[336,512]{1,0:T(8,128)(2,1)S(1)}, bf16[336,512]{1,0:T(8,128)(2,1)S(1)}, u32[]{:S(2)}, u32[]{:S(2)}) collective-permute-start(bf16[336,512]{1,0:T(8,128)(2,1)S(1)} %collective-permute-done.8.refs_9_), channel_id=1, source_target_pairs={{0,64},{8,456},{64,128},{72,8},{128,192},{136,72},{192,256},{200,1... | collective-permute-start | bytes 1032200 | tf_op jit(solution)/shard_map/ppermute | solution.py:41
  42.7 9.2 %collective-permute-start.13 = (bf16[320,512]{1,0:T(8,128)(2,1)S(1)}, bf16[320,512]{1,0:T(8,128)(2,1)S(1)}, u32[]{:S(2)}, u32[]{:S(2)}) collective-permute-start(bf16[320,512]{1,0:T(8,128)(2,1)S(1)} %collective-permute-done.12.refs_14_), channel_id=1, source_target_pairs={{0,64},{8,456},{64,128},{72,8},{128,192},{136,72},{192,256},{200,1... | collective-permute-start | bytes 983048 | tf_op jit(solution)/shard_map/ppermute | solution.py:41
  46.8 9.2 %collective-permute-start.10 = (bf16[336,512]{1,0:T(8,128)(2,1)S(1)}, bf16[336,512]{1,0:T(8,128)(2,1)S(1)}, u32[]{:S(2)}, u32[]{:S(2)}) collective-permute-start(bf16[336,512]{1,0:T(8,128)(2,1)S(1)} %collective-permute-done.9.refs_10_), channel_id=1, source_target_pairs={{0,64},{8,456},{64,128},{72,8},{128,192},{136,72},{192,256},{200,1... | collective-permute-start | bytes 1032200 | tf_op jit(solution)/shard_map/ppermute | solution.py:41
  51.9 8.1 %collective-permute-start.14 = (bf16[320,512]{1,0:T(8,128)(2,1)S(1)}, bf16[320,512]{1,0:T(8,128)(2,1)S(1)}, u32[]{:S(2)}, u32[]{:S(2)}) collective-permute-start(bf16[320,512]{1,0:T(8,128)(2,1)S(1)} %collective-permute-done.13.refs_15_), channel_id=1, source_target_pairs={{0,64},{8,456},{64,128},{72,8},{128,192},{136,72},{192,256},{200,1... | collective-permute-start | bytes 983048 | tf_op jit(solution)/shard_map/ppermute | solution.py:41
  60.0 61.7 %collective-permute-start.16 = (bf16[1968,512]{1,0:T(8,128)(2,1)S(1)}, bf16[1968,512]{1,0:T(8,128)(2,1)S(1)}, u32[]{:S(2)}, u32[]{:S(2)}) collective-permute-start(bf16[1968,512]{1,0:T(8,128)(2,1)S(1)} %constant_dynamic-update-slice_fusion), channel_id=1, source_target_pairs={{0,8},{8,0},{1,9},{9,1},{2,10},{10,2},{3,11},{11,3},{4,12},{12,4},... | collective-permute-start | bytes 6045704 | tf_op jit(solution)/shard_map/ppermute | solution.py:29
  65.5 29.2 %collective-permute-start.3 = (bf16[384,640]{1,0:T(8,128)(2,1)S(1)}, bf16[384,640]{1,0:T(8,128)(2,1)S(1)}, u32[]{:S(2)}, u32[]{:S(2)}) collective-permute-start(bf16[384,640]{1,0:T(8,128)(2,1)S(1)} %copy-done), channel_id=1, source_target_pairs={{0,1},{1,0},{2,3},{3,2},{4,5},{5,4},{6,7},{7,6},{8,9},{9,8},{10,11... | collective-permute-start | bytes 1474568 | tf_op jit(solution)/shard_map/ppermute | solution.py:29
  70.9 28.4 %collective-permute-start.2 = (bf16[384,640]{1,0:T(8,128)(2,1)S(1)}, bf16[384,640]{1,0:T(8,128)(2,1)S(1)}, u32[]{:S(2)}, u32[]{:S(2)}) collective-permute-start(bf16[384,640]{1,0:T(8,128)(2,1)S(1)} %copy-done), channel_id=1, source_target_pairs={{0,4},{2,6},{4,0},{6,2},{1,5},{3,7},{5,1},{7,3},{8,12},{10,14},{12... | collective-permute-start | bytes 1474568 | tf_op jit(solution)/shard_map/ppermute | solution.py:33
  75.6 26.5 %collective-permute-start.1 = (bf16[384,640]{1,0:T(8,128)(2,1)S(1)}, bf16[384,640]{1,0:T(8,128)(2,1)S(1)}, u32[]{:S(2)}, u32[]{:S(2)}) collective-permute-start(bf16[384,640]{1,0:T(8,128)(2,1)S(1)} %copy-done), channel_id=1, source_target_pairs={{0,6},{2,0},{4,2},{6,4},{1,7},{3,1},{5,3},{7,5},{8,14},{10,8},{12,... | collective-permute-start | bytes 1474568 | tf_op jit(solution)/shard_map/ppermute | solution.py:33
  78.4 26.3 %collective-permute-start = (bf16[384,640]{1,0:T(8,128)(2,1)S(1)}, bf16[384,640]{1,0:T(8,128)(2,1)S(1)}, u32[]{:S(2)}, u32[]{:S(2)}) collective-permute-start(bf16[384,640]{1,0:T(8,128)(2,1)S(1)} %copy-done), channel_id=1, source_target_pairs={{0,2},{2,4},{4,6},{6,0},{1,3},{3,5},{5,7},{7,1},{8,10},{10,12},{12... | collective-permute-start | bytes 1474568 | tf_op jit(solution)/shard_map/ppermute | solution.py:33
  94.7 15.3 %collective-permute-start.6 = (bf16[384,640]{1,0:T(8,128)(2,1)S(1)}, bf16[384,640]{1,0:T(8,128)(2,1)S(1)}, u32[]{:S(2)}, u32[]{:S(2)}) collective-permute-start(bf16[384,640]{1,0:T(8,128)(2,1)S(1)} %collective-permute-done.3.refs_4_), channel_id=1, source_target_pairs={{0,4},{2,6},{4,0},{6,2},{1,5},{3,7},{5,1},{7,3},{8,12},{10,14},{12... | collective-permute-start | bytes 1474568 | tf_op jit(solution)/shard_map/ppermute | solution.py:33
  99.3 21.5 %collective-permute-start.5 = (bf16[384,640]{1,0:T(8,128)(2,1)S(1)}, bf16[384,640]{1,0:T(8,128)(2,1)S(1)}, u32[]{:S(2)}, u32[]{:S(2)}) collective-permute-start(bf16[384,640]{1,0:T(8,128)(2,1)S(1)} %collective-permute-done.3.refs_4_), channel_id=1, source_target_pairs={{0,6},{2,0},{4,2},{6,4},{1,7},{3,1},{5,3},{7,5},{8,14},{10,8},{12,... | collective-permute-start | bytes 1474568 | tf_op jit(solution)/shard_map/ppermute | solution.py:33
  102.1 19.6 %collective-permute-start.4 = (bf16[384,640]{1,0:T(8,128)(2,1)S(1)}, bf16[384,640]{1,0:T(8,128)(2,1)S(1)}, u32[]{:S(2)}, u32[]{:S(2)}) collective-permute-start(bf16[384,640]{1,0:T(8,128)(2,1)S(1)} %collective-permute-done.3.refs_4_), channel_id=1, source_target_pairs={{0,2},{2,4},{4,6},{6,0},{1,3},{3,5},{5,7},{7,1},{8,10},{10,12},{12... | collective-permute-start | bytes 1474568 | tf_op jit(solution)/shard_map/ppermute | solution.py:33
  104.6 17.1 %collective-permute-start.11 = (bf16[336,512]{1,0:T(8,128)(2,1)S(1)}, bf16[336,512]{1,0:T(8,128)(2,1)S(1)}, u32[]{:S(2)}, u32[]{:S(2)}) collective-permute-start(bf16[336,512]{1,0:T(8,128)(2,1)S(1)} %collective-permute-done.10.refs_11_), channel_id=1, source_target_pairs={{0,64},{8,456},{64,128},{72,8},{128,192},{136,72},{192,256},{200,1... | collective-permute-start | bytes 1032200 | tf_op jit(solution)/shard_map/ppermute | solution.py:41
  109.9 11.8 %collective-permute-start.15 = (bf16[320,512]{1,0:T(8,128)(2,1)S(1)}, bf16[320,512]{1,0:T(8,128)(2,1)S(1)}, u32[]{:S(2)}, u32[]{:S(2)}) collective-permute-start(bf16[320,512]{1,0:T(8,128)(2,1)S(1)} %collective-permute-done.14.refs_16_), channel_id=1, source_target_pairs={{0,64},{8,456},{64,128},{72,8},{128,192},{136,72},{192,256},{200,1... | collective-permute-start | bytes 983048 | tf_op jit(solution)/shard_map/ppermute | solution.py:41
  128.9 17.4 %all-to-all-start.1 = ((bf16[64,4,256]{2,1,0:T(4,128)(2,1)}), bf16[64,4,256]{2,1,0:T(4,128)(2,1)S(1)}, u32[]{:S(2)}, u32[]{:S(2)}) async-start(bf16[64,4,256]{2,1,0:T(4,128)(2,1)} %get-tuple-element.28), calls=%async_computation.1 | async-start | bytes 262144 | tf_op jit(solution)/shard_map/all_to_all | solution.py:260

commit v5 on v4

--- a/solution.py
+++ b/solution.py
@@ -79,6 +79,14 @@
     total = jnp.sum(open_part, axis=0, keepdims=True) + jnp.sum(edge, axis=0, keepdims=True)
     share = 1.0 / total
     return open_part * share, edge * share
+
+
+def shard_kernel(w_ref, pk_ref, pv_ref, out_ref):
+    for k in range(NY):
+        out_ref[k, :80] = w_ref[...]
+        out_ref[k, 80:88] = jnp.zeros((8, 512), BF16)
+        out_ref[k, 80:84, :HD] = pk_ref[...]
+        out_ref[k, 80:84, HD : 2 * HD] = pv_ref[...]
 
 
 def front_kernel(length_ref, *refs):
@@ -184,7 +192,7 @@
 VM = pl.BlockSpec(memory_space=pltpu.VMEM)
 SM = pl.BlockSpec(memory_space=pltpu.SMEM)
 ANY = pl.BlockSpec(memory_space=pl.ANY)
-VMEM_MIB = {"front": 34, "back": 59}
+VMEM_MIB = {"shard": 59, "front": 34, "back": 59}
 WIDTHS = tuple(PREFIX + BLOCK * (i + 1) for i in range(3))
 
 
@@ -223,6 +231,12 @@
     )
 
 
+def shard(out_weight, prefix_key, prefix_value):
+    outs = [((NY, 88, 512), BF16)]
+    args = (out_weight, prefix_key, prefix_value)
+    return call(shard_kernel, "shard", outs, [VM] * 3, args, 1 << 20)[0]
+
+
 def back(og, s, low, queries, resp_key, prefix):
     outs = [((ROWS, GROUP * HD), BF16), ((ROWS, HD), BF16), ((ROWS, HD), BF16)]
     return call(
@@ -232,10 +246,8 @@
 
 def steps(grad_out, out_weight, queries, resp_key, resp_value, prefix_key, prefix_value, lengths):
     core = lax.axis_index("c")
-    both = jnp.concatenate([prefix_key, prefix_value], axis=1)
-
-    shard = jnp.concatenate([out_weight, jnp.pad(both, ((0, 4), (0, 256)))], axis=0)
-    four = lax.all_to_all(jnp.broadcast_to(shard[None], (NY, 88, 512)), "yl", 0, 0, tiled=True)
+    copies = shard(out_weight, prefix_key, prefix_value)
+    four = lax.all_to_all(copies, "yl", 0, 0, tiled=True)
     four = four[:, None]
     pair = in_pair(four, swap(four, "c"), core, 1)
     tail = pair[:, :, 80:84, :256].reshape(2, TAIL, 256)

time: 148 us -> 148 us (level)
  Pallas kernels: 10.7 us -> 12.3 us
  other arithmetic: 1.83 us -> 0.23 us
    ppermute x3, starting transfers between devices: 17.8 us -> 19.6 us  [swap(): return lax.ppermute(v, axis, [(i, i ^ bit) for i in range(size)])]
    pallas_call x2 -> x3, Pallas kernels: 10.7 us -> 12.3 us  [call(): pl.pallas_call(kernel, out_shape=[pltpu.HBM(s, d) if out_specs and k else...]
    concatenate x2 -> x0, other arithmetic: 1.6 us -> none  [the longest x1 0.89 us: steps(): jnp.concatenate([out_weight, jnp.pad(both, ((0, 4), (0, 256)))], axis=0)]
where the time goes in v5:
time: 148 us; the launch traced here: 147 us
  starting transfers between devices  78.4 us (53%)
  waiting for transfers between devices  41 us (28%)
  blocking collectives  12.8 us (9%)
  Pallas kernels  12.3 us (8%)
  between operations  1.65 us (1%)
    ppermute x8, starting transfers between devices, ring_z(): return lax.ppermute(v, ('z', 'c'), pairs)  32.3 us
    ppermute x6, starting transfers between devices, shift_x(): return lax.ppermute(v, 'x', [(x, (x + step) % NX) for x in range(NX)])  19.9 us
    ppermute x3, starting transfers between devices, swap(): return lax.ppermute(v, axis, [(i, i ^ bit) for i in range(size)])  19.6 us
    ppermute x3, waiting for transfers between devices, swap(): return lax.ppermute(v, axis, [(i, i ^ bit) for i in range(size)])  14.2 us
    all_to_all x1, blocking collectives, steps(): four = lax.all_to_all(copies, 'yl', 0, 0, tiled=True)  12.8 us
    ppermute x6, waiting for transfers between devices, shift_x(): return lax.ppermute(v, 'x', [(x, (x + step) % NX) for x in range(NX)])  12.6 us
    pallas_call x3, Pallas kernels, call(): pl.pallas_call(kernel, out_shape=[pltpu.HBM(s, d) if out_specs and k else...  12.3 us
    all_to_all x1, waiting for transfers between devices, steps(): parts = lax.all_to_all(gp, ROLL, 0, 0, tiled=True)  7.24 us
  transfers between devices with their start and end apart: 18, of which 10 were waited for; matrix products, arithmetic and copies ran while one was open for 0% of the time, Pallas kernels for 2%

profile of v5, /device:TPU:1, one launch (start us, length us, event | category | flops | bytes accessed | tf_op | source)
XLA Modules:
  0.0 147.3 jit_solution(17700105747345267741)
XLA Ops:
  2.3 12.8 %all_to_all.10 = bf16[4,88,512]{2,1,0:T(8,128)(2,1)S(1)} all-to-all(bf16[4,88,512]{2,1,0:T(8,128)(2,1)} %shard_map.119), channel_id=1, replica_groups=mesh['z'=8,'yl'=4,'c'=2,'x'=4,'yh'=2] {'yl'}, dimensions={0} | all-to-all | bytes 720896 | tf_op jit(solution)/shard_map/all_to_all | solution.py:250
  15.1 7.9 %collective-permute-start.7 = (bf16[4,1,88,512]{3,2,0,1:T(8,128)(2,1)S(1)}, bf16[4,1,88,512]{3,2,0,1:T(8,128)(2,1)S(1)}, u32[]{:S(2)}, u32[]{:S(2)}) collective-permute-start(bf16[4,1,88,512]{3,2,0,1:T(8,128)(2,1)S(1)} %bitcast.7), channel_id=1, source_target_pairs={{0,8},{8,0},{1,9},{9,1},{2,10},{10,2},{3,11},{11,3},{4,12},{12,4},... | collective-permute-start | bytes 1081352 | tf_op jit(solution)/shard_map/ppermute | solution.py:29
  24.5 9.2 %collective-permute-start.8 = (bf16[336,512]{1,0:T(8,128)(2,1)S(1)}, bf16[336,512]{1,0:T(8,128)(2,1)S(1)}, u32[]{:S(2)}, u32[]{:S(2)}) collective-permute-start(bf16[336,512]{1,0:T(8,128)(2,1)S(1)} %maximum_maximum_fusion.refs_8_), channel_id=1, source_target_pairs={{0,64},{8,456},{64,128},{72,8},{128,192},{136,72},{192,256},{200,1... | collective-permute-start | bytes 1032200 | tf_op jit(solution)/shard_map/ppermute | solution.py:41
  33.8 2.3 %collective-permute-start.12 = (bf16[320,512]{1,0:T(8,128)(2,1)S(1)}, bf16[320,512]{1,0:T(8,128)(2,1)S(1)}, u32[]{:S(2)}, u32[]{:S(2)}) collective-permute-start(bf16[320,512]{1,0:T(8,128)(2,1)S(1)} %bitcast.5), channel_id=1, source_target_pairs={{0,64},{8,456},{64,128},{72,8},{128,192},{136,72},{192,256},{200,1... | collective-permute-start | bytes 983048 | tf_op jit(solution)/shard_map/ppermute | solution.py:41
  37.9 5.0 %collective-permute-start.9 = (bf16[336,512]{1,0:T(8,128)(2,1)S(1)}, bf16[336,512]{1,0:T(8,128)(2,1)S(1)}, u32[]{:S(2)}, u32[]{:S(2)}) collective-permute-start(bf16[336,512]{1,0:T(8,128)(2,1)S(1)} %collective-permute-done.8.refs_9_), channel_id=1, source_target_pairs={{0,64},{8,456},{64,128},{72,8},{128,192},{136,72},{192,256},{200,1... | collective-permute-start | bytes 1032200 | tf_op jit(solution)/shard_map/ppermute | solution.py:41
  43.0 3.5 %collective-permute-start.13 = (bf16[320,512]{1,0:T(8,128)(2,1)S(1)}, bf16[320,512]{1,0:T(8,128)(2,1)S(1)}, u32[]{:S(2)}, u32[]{:S(2)}) collective-permute-start(bf16[320,512]{1,0:T(8,128)(2,1)S(1)} %collective-permute-done.12.refs_14_), channel_id=1, source_target_pairs={{0,64},{8,456},{64,128},{72,8},{128,192},{136,72},{192,256},{200,1... | collective-permute-start | bytes 983048 | tf_op jit(solution)/shard_map/ppermute | solution.py:41
  47.1 5.0 %collective-permute-start.10 = (bf16[336,512]{1,0:T(8,128)(2,1)S(1)}, bf16[336,512]{1,0:T(8,128)(2,1)S(1)}, u32[]{:S(2)}, u32[]{:S(2)}) collective-permute-start(bf16[336,512]{1,0:T(8,128)(2,1)S(1)} %collective-permute-done.9.refs_10_), channel_id=1, source_target_pairs={{0,64},{8,456},{64,128},{72,8},{128,192},{136,72},{192,256},{200,1... | collective-permute-start | bytes 1032200 | tf_op jit(solution)/shard_map/ppermute | solution.py:41
  52.2 3.5 %collective-permute-start.14 = (bf16[320,512]{1,0:T(8,128)(2,1)S(1)}, bf16[320,512]{1,0:T(8,128)(2,1)S(1)}, u32[]{:S(2)}, u32[]{:S(2)}) collective-permute-start(bf16[320,512]{1,0:T(8,128)(2,1)S(1)} %collective-permute-done.13.refs_15_), channel_id=1, source_target_pairs={{0,64},{8,456},{64,128},{72,8},{128,192},{136,72},{192,256},{200,1... | collective-permute-start | bytes 983048 | tf_op jit(solution)/shard_map/ppermute | solution.py:41
  56.3 4.0 %collective-permute-done.14.refs_16_ = bf16[320,512]{1,0:T(8,128)(2,1)S(1)} collective-permute-done((bf16[320,512]{1,0:T(8,128)(2,1)S(1)}, bf16[320,512]{1,0:T(8,128)(2,1)S(1)}, u32[]{:S(2)}, u32[]{:S(2)}) %collective-permute-start.14) | collective-permute-done | bytes 327712 | tf_op jit(solution)/shard_map/ppermute | solution.py:41
  60.3 5.4 %collective-permute-start.16 = (bf16[1968,512]{1,0:T(8,128)(2,1)S(1)}, bf16[1968,512]{1,0:T(8,128)(2,1)S(1)}, u32[]{:S(2)}, u32[]{:S(2)}) collective-permute-start(bf16[1968,512]{1,0:T(8,128)(2,1)S(1)} %constant_dynamic-update-slice_fusion), channel_id=1, source_target_pairs={{0,8},{8,0},{1,9},{9,1},{2,10},{10,2},{3,11},{11,3},{4,12},{12,4},... | collective-permute-start | bytes 6045704 | tf_op jit(solution)/shard_map/ppermute | solution.py:29
  65.8 6.3 %collective-permute-start.3 = (bf16[384,640]{1,0:T(8,128)(2,1)S(1)}, bf16[384,640]{1,0:T(8,128)(2,1)S(1)}, u32[]{:S(2)}, u32[]{:S(2)}) collective-permute-start(bf16[384,640]{1,0:T(8,128)(2,1)S(1)} %copy-done), channel_id=1, source_target_pairs={{0,1},{1,0},{2,3},{3,2},{4,5},{5,4},{6,7},{7,6},{8,9},{9,8},{10,11... | collective-permute-start | bytes 1474568 | tf_op jit(solution)/shard_map/ppermute | solution.py:29
  72.1 4.7 %collective-permute-start.2 = (bf16[384,640]{1,0:T(8,128)(2,1)S(1)}, bf16[384,640]{1,0:T(8,128)(2,1)S(1)}, u32[]{:S(2)}, u32[]{:S(2)}) collective-permute-start(bf16[384,640]{1,0:T(8,128)(2,1)S(1)} %copy-done), channel_id=1, source_target_pairs={{0,4},{2,6},{4,0},{6,2},{1,5},{3,7},{5,1},{7,3},{8,12},{10,14},{12... | collective-permute-start | bytes 1474568 | tf_op jit(solution)/shard_map/ppermute | solution.py:33
  76.7 2.8 %collective-permute-start.1 = (bf16[384,640]{1,0:T(8,128)(2,1)S(1)}, bf16[384,640]{1,0:T(8,128)(2,1)S(1)}, u32[]{:S(2)}, u32[]{:S(2)}) collective-permute-start(bf16[384,640]{1,0:T(8,128)(2,1)S(1)} %copy-done), channel_id=1, source_target_pairs={{0,6},{2,0},{4,2},{6,4},{1,7},{3,1},{5,3},{7,5},{8,14},{10,8},{12,... | collective-permute-start | bytes 1474568 | tf_op jit(solution)/shard_map/ppermute | solution.py:33
  79.5 2.5 %collective-permute-start = (bf16[384,640]{1,0:T(8,128)(2,1)S(1)}, bf16[384,640]{1,0:T(8,128)(2,1)S(1)}, u32[]{:S(2)}, u32[]{:S(2)}) collective-permute-start(bf16[384,640]{1,0:T(8,128)(2,1)S(1)} %copy-done), channel_id=1, source_target_pairs={{0,2},{2,4},{4,6},{6,0},{1,3},{3,5},{5,7},{7,1},{8,10},{10,12},{12... | collective-permute-start | bytes 1474568 | tf_op jit(solution)/shard_map/ppermute | solution.py:33
  82.0 13.0 %collective-permute-done.3.refs_4_ = bf16[384,640]{1,0:T(8,128)(2,1)S(1)} collective-permute-done((bf16[384,640]{1,0:T(8,128)(2,1)S(1)}, bf16[384,640]{1,0:T(8,128)(2,1)S(1)}, u32[]{:S(2)}, u32[]{:S(2)}) %collective-permute-start.3) | collective-permute-done | bytes 491552 | tf_op jit(solution)/shard_map/ppermute | solution.py:29
  95.0 4.6 %collective-permute-start.6 = (bf16[384,640]{1,0:T(8,128)(2,1)S(1)}, bf16[384,640]{1,0:T(8,128)(2,1)S(1)}, u32[]{:S(2)}, u32[]{:S(2)}) collective-permute-start(bf16[384,640]{1,0:T(8,128)(2,1)S(1)} %collective-permute-done.3.refs_4_), channel_id=1, source_target_pairs={{0,4},{2,6},{4,0},{6,2},{1,5},{3,7},{5,1},{7,3},{8,12},{10,14},{12... | collective-permute-start | bytes 1474568 | tf_op jit(solution)/shard_map/ppermute | solution.py:33
  99.6 2.8 %collective-permute-start.5 = (bf16[384,640]{1,0:T(8,128)(2,1)S(1)}, bf16[384,640]{1,0:T(8,128)(2,1)S(1)}, u32[]{:S(2)}, u32[]{:S(2)}) collective-permute-start(bf16[384,640]{1,0:T(8,128)(2,1)S(1)} %collective-permute-done.3.refs_4_), channel_id=1, source_target_pairs={{0,6},{2,0},{4,2},{6,4},{1,7},{3,1},{5,3},{7,5},{8,14},{10,8},{12,... | collective-permute-start | bytes 1474568 | tf_op jit(solution)/shard_map/ppermute | solution.py:33
  102.4 2.5 %collective-permute-start.4 = (bf16[384,640]{1,0:T(8,128)(2,1)S(1)}, bf16[384,640]{1,0:T(8,128)(2,1)S(1)}, u32[]{:S(2)}, u32[]{:S(2)}) collective-permute-start(bf16[384,640]{1,0:T(8,128)(2,1)S(1)} %collective-permute-done.3.refs_4_), channel_id=1, source_target_pairs={{0,2},{2,4},{4,6},{6,0},{1,3},{3,5},{5,7},{7,1},{8,10},{10,12},{12... | collective-permute-start | bytes 1474568 | tf_op jit(solution)/shard_map/ppermute | solution.py:33
  106.9 3.4 %collective-permute-done.6.refs_7_ = bf16[384,640]{1,0:T(8,128)(2,1)S(1)} collective-permute-done((bf16[384,640]{1,0:T(8,128)(2,1)S(1)}, bf16[384,640]{1,0:T(8,128)(2,1)S(1)}, u32[]{:S(2)}, u32[]{:S(2)}) %collective-permute-start.6) | collective-permute-done | bytes 491552 | tf_op jit(solution)/shard_map/ppermute | solution.py:33
  112.8 8.3 %collective-permute-done.5.refs_6_ = bf16[384,640]{1,0:T(8,128)(2,1)S(1)} collective-permute-done((bf16[384,640]{1,0:T(8,128)(2,1)S(1)}, bf16[384,640]{1,0:T(8,128)(2,1)S(1)}, u32[]{:S(2)}, u32[]{:S(2)}) %collective-permute-start.5) | collective-permute-done | bytes 491552 | tf_op jit(solution)/shard_map/ppermute | solution.py:33
  122.1 7.1 %shard_map.120 = (bf16[64,4,256]{2,1,0:T(4,128)(2,1)}, bf16[1536,128]{1,0:T(8,128)(2,1)}, bf16[384,512]{1,0:T(8,128)(2,1)}, bf16[512,512]{1,0:T(8,128)(2,1)}, bf...) custom-call(s32[1]{0:T(128)S(6)} %copy.22.length_ref, ...), custom_call_target="tpu_custom_call" | custom-call | flops 2013265920 | bytes 4000000 | tf_op jit(solution)/shard_map/pallas_call | solution.py:200
  129.2 6.6 %all-to-all-start.1 = ((bf16[64,4,256]{2,1,0:T(4,128)(2,1)}), bf16[64,4,256]{2,1,0:T(4,128)(2,1)S(1)}, u32[]{:S(2)}, u32[]{:S(2)}) async-start(bf16[64,4,256]{2,1,0:T(4,128)(2,1)} %get-tuple-element.28), calls=%async_computation.1 | async-start | bytes 262144 | tf_op jit(solution)/shard_map/all_to_all | solution.py:272
  135.8 3.6 %shard_map.121 = (bf16[384,512]{1,0:T(8,128)(2,1)}, bf16[384,128]{1,0:T(8,128)(2,1)}, bf16[384,128]{1,0:T(8,128)(2,1)}) custom-call(bf16[1536,128]{1,0:T(8,128)(2,1)} %get-tuple-element.17.og_ref, bf16[384,512]{1,0:T(8,128)(2,1)} %get-tuple-element.18.s0, bf16[512,512]{1,0:T(8,128)(2,1)} %get-tuple-element.19.s1, bf16[640,512]{1,0:T(8,128)(2,1)} %get-tuple-element.20.s2, ...), custom_call_target="tpu_custom_call" | custom-call | flops 1073741824 | bytes 4000000 | tf_op jit(solution)/shard_map/pallas_call | solution.py:200
  139.3 7.2 %all-to-all-done.1 = bf16[64,4,256]{2,1,0:T(4,128)(2,1)S(1)} async-done(((bf16[64,4,256]{2,1,0:T(4,128)(2,1)}), bf16[64,4,256]{2,1,0:T(4,128)(2,1)S(1)}, u32[]{:S(2)}, u32[]{:S(2)}) %all-to-all-start.1) | async-done | bytes 131104 | tf_op jit(solution)/shard_map/all_to_all | solution.py:272
  (42 shorter events, 11.8 us)
Async XLA Ops:
  15.1 9.2 %collective-permute-start.7 = (bf16[4,1,88,512]{3,2,0,1:T(8,128)(2,1)S(1)}, bf16[4,1,88,512]{3,2,0,1:T(8,128)(2,1)S(1)}, u32[]{:S(2)}, u32[]{:S(2)}) collective-permute-start(bf16[4,1,88,512]{3,2,0,1:T(8,128)(2,1)S(1)} %bitcast.7), channel_id=1, source_target_pairs={{0,8},{8,0},{1,9},{9,1},{2,10},{10,2},{3,11},{11,3},{4,12},{12,4},... | collective-permute-start | bytes 1081352 | tf_op jit(solution)/shard_map/ppermute | solution.py:29
  24.5 13.4 %collective-permute-start.8 = (bf16[336,512]{1,0:T(8,128)(2,1)S(1)}, bf16[336,512]{1,0:T(8,128)(2,1)S(1)}, u32[]{:S(2)}, u32[]{:S(2)}) collective-permute-start(bf16[336,512]{1,0:T(8,128)(2,1)S(1)} %maximum_maximum_fusion.refs_8_), channel_id=1, source_target_pairs={{0,64},{8,456},{64,128},{72,8},{128,192},{136,72},{192,256},{200,1... | collective-permute-start | bytes 1032200 | tf_op jit(solution)/shard_map/ppermute | solution.py:41
  33.8 32.0 %copy-start = (bf16[384,640]{1,0:T(8,128)(2,1)S(1)}, bf16[384,640]{1,0:T(8,128)(2,1)}, u32[]{:S(2)}) copy-start(bf16[384,640]{1,0:T(8,128)(2,1)} %refs_0_.1) | copy-start | bytes 1474564
  33.8 88.3 %copy-start.1 = (bf16[384,512]{1,0:T(8,128)(2,1)S(1)}, bf16[384,512]{1,0:T(8,128)(2,1)}, u32[]{:S(2)}) copy-start(bf16[384,512]{1,0:T(8,128)(2,1)} %q_ref.1) | copy-start | bytes 1179652
  33.8 88.3 %copy-start.2 = (bf16[384,128]{1,0:T(8,128)(2,1)S(1)}, bf16[384,128]{1,0:T(8,128)(2,1)}, u32[]{:S(2)}) copy-start(bf16[384,128]{1,0:T(8,128)(2,1)} %refs_21_.1) | copy-start | bytes 294916
  33.8 88.3 %copy-start.3 = (bf16[384,128]{1,0:T(8,128)(2,1)S(1)}, bf16[384,128]{1,0:T(8,128)(2,1)}, u32[]{:S(2)}) copy-start(bf16[384,128]{1,0:T(8,128)(2,1)} %rk_ref.1) | copy-start | bytes 294916
  33.8 9.1 %collective-permute-start.12 = (bf16[320,512]{1,0:T(8,128)(2,1)S(1)}, bf16[320,512]{1,0:T(8,128)(2,1)S(1)}, u32[]{:S(2)}, u32[]{:S(2)}) collective-permute-start(bf16[320,512]{1,0:T(8,128)(2,1)S(1)} %bitcast.5), channel_id=1, source_target_pairs={{0,64},{8,456},{64,128},{72,8},{128,192},{136,72},{192,256},{200,1... | collective-permute-start | bytes 983048 | tf_op jit(solution)/shard_map/ppermute | solution.py:41
  37.9 9.2 %collective-permute-start.9 = (bf16[336,512]{1,0:T(8,128)(2,1)S(1)}, bf16[336,512]{1,0:T(8,128)(2,1)S(1)}, u32[]{:S(2)}, u32[]{:S(2)}) collective-permute-start(bf16[336,512]{1,0:T(8,128)(2,1)S(1)} %collective-permute-done.8.refs_9_), channel_id=1, source_target_pairs={{0,64},{8,456},{64,128},{72,8},{128,192},{136,72},{192,256},{200,1... | collective-permute-start | bytes 1032200 | tf_op jit(solution)/shard_map/ppermute | solution.py:41
  43.0 9.2 %collective-permute-start.13 = (bf16[320,512]{1,0:T(8,128)(2,1)S(1)}, bf16[320,512]{1,0:T(8,128)(2,1)S(1)}, u32[]{:S(2)}, u32[]{:S(2)}) collective-permute-start(bf16[320,512]{1,0:T(8,128)(2,1)S(1)} %collective-permute-done.12.refs_14_), channel_id=1, source_target_pairs={{0,64},{8,456},{64,128},{72,8},{128,192},{136,72},{192,256},{200,1... | collective-permute-start | bytes 983048 | tf_op jit(solution)/shard_map/ppermute | solution.py:41
  47.1 9.2 %collective-permute-start.10 = (bf16[336,512]{1,0:T(8,128)(2,1)S(1)}, bf16[336,512]{1,0:T(8,128)(2,1)S(1)}, u32[]{:S(2)}, u32[]{:S(2)}) collective-permute-start(bf16[336,512]{1,0:T(8,128)(2,1)S(1)} %collective-permute-done.9.refs_10_), channel_id=1, source_target_pairs={{0,64},{8,456},{64,128},{72,8},{128,192},{136,72},{192,256},{200,1... | collective-permute-start | bytes 1032200 | tf_op jit(solution)/shard_map/ppermute | solution.py:41
  52.2 8.1 %collective-permute-start.14 = (bf16[320,512]{1,0:T(8,128)(2,1)S(1)}, bf16[320,512]{1,0:T(8,128)(2,1)S(1)}, u32[]{:S(2)}, u32[]{:S(2)}) collective-permute-start(bf16[320,512]{1,0:T(8,128)(2,1)S(1)} %collective-permute-done.13.refs_15_), channel_id=1, source_target_pairs={{0,64},{8,456},{64,128},{72,8},{128,192},{136,72},{192,256},{200,1... | collective-permute-start | bytes 983048 | tf_op jit(solution)/shard_map/ppermute | solution.py:41
  60.3 61.7 %collective-permute-start.16 = (bf16[1968,512]{1,0:T(8,128)(2,1)S(1)}, bf16[1968,512]{1,0:T(8,128)(2,1)S(1)}, u32[]{:S(2)}, u32[]{:S(2)}) collective-permute-start(bf16[1968,512]{1,0:T(8,128)(2,1)S(1)} %constant_dynamic-update-slice_fusion), channel_id=1, source_target_pairs={{0,8},{8,0},{1,9},{9,1},{2,10},{10,2},{3,11},{11,3},{4,12},{12,4},... | collective-permute-start | bytes 6045704 | tf_op jit(solution)/shard_map/ppermute | solution.py:29
  65.8 29.2 %collective-permute-start.3 = (bf16[384,640]{1,0:T(8,128)(2,1)S(1)}, bf16[384,640]{1,0:T(8,128)(2,1)S(1)}, u32[]{:S(2)}, u32[]{:S(2)}) collective-permute-start(bf16[384,640]{1,0:T(8,128)(2,1)S(1)} %copy-done), channel_id=1, source_target_pairs={{0,1},{1,0},{2,3},{3,2},{4,5},{5,4},{6,7},{7,6},{8,9},{9,8},{10,11... | collective-permute-start | bytes 1474568 | tf_op jit(solution)/shard_map/ppermute | solution.py:29
  72.1 27.6 %collective-permute-start.2 = (bf16[384,640]{1,0:T(8,128)(2,1)S(1)}, bf16[384,640]{1,0:T(8,128)(2,1)S(1)}, u32[]{:S(2)}, u32[]{:S(2)}) collective-permute-start(bf16[384,640]{1,0:T(8,128)(2,1)S(1)} %copy-done), channel_id=1, source_target_pairs={{0,4},{2,6},{4,0},{6,2},{1,5},{3,7},{5,1},{7,3},{8,12},{10,14},{12... | collective-permute-start | bytes 1474568 | tf_op jit(solution)/shard_map/ppermute | solution.py:33
  76.7 25.7 %collective-permute-start.1 = (bf16[384,640]{1,0:T(8,128)(2,1)S(1)}, bf16[384,640]{1,0:T(8,128)(2,1)S(1)}, u32[]{:S(2)}, u32[]{:S(2)}) collective-permute-start(bf16[384,640]{1,0:T(8,128)(2,1)S(1)} %copy-done), channel_id=1, source_target_pairs={{0,6},{2,0},{4,2},{6,4},{1,7},{3,1},{5,3},{7,5},{8,14},{10,8},{12,... | collective-permute-start | bytes 1474568 | tf_op jit(solution)/shard_map/ppermute | solution.py:33
  79.5 25.4 %collective-permute-start = (bf16[384,640]{1,0:T(8,128)(2,1)S(1)}, bf16[384,640]{1,0:T(8,128)(2,1)S(1)}, u32[]{:S(2)}, u32[]{:S(2)}) collective-permute-start(bf16[384,640]{1,0:T(8,128)(2,1)S(1)} %copy-done), channel_id=1, source_target_pairs={{0,2},{2,4},{4,6},{6,0},{1,3},{3,5},{5,7},{7,1},{8,10},{10,12},{12... | collective-permute-start | bytes 1474568 | tf_op jit(solution)/shard_map/ppermute | solution.py:33
  95.0 15.3 %collective-permute-start.6 = (bf16[384,640]{1,0:T(8,128)(2,1)S(1)}, bf16[384,640]{1,0:T(8,128)(2,1)S(1)}, u32[]{:S(2)}, u32[]{:S(2)}) collective-permute-start(bf16[384,640]{1,0:T(8,128)(2,1)S(1)} %collective-permute-done.3.refs_4_), channel_id=1, source_target_pairs={{0,4},{2,6},{4,0},{6,2},{1,5},{3,7},{5,1},{7,3},{8,12},{10,14},{12... | collective-permute-start | bytes 1474568 | tf_op jit(solution)/shard_map/ppermute | solution.py:33
  99.6 21.5 %collective-permute-start.5 = (bf16[384,640]{1,0:T(8,128)(2,1)S(1)}, bf16[384,640]{1,0:T(8,128)(2,1)S(1)}, u32[]{:S(2)}, u32[]{:S(2)}) collective-permute-start(bf16[384,640]{1,0:T(8,128)(2,1)S(1)} %collective-permute-done.3.refs_4_), channel_id=1, source_target_pairs={{0,6},{2,0},{4,2},{6,4},{1,7},{3,1},{5,3},{7,5},{8,14},{10,8},{12,... | collective-permute-start | bytes 1474568 | tf_op jit(solution)/shard_map/ppermute | solution.py:33
  102.4 19.6 %collective-permute-start.4 = (bf16[384,640]{1,0:T(8,128)(2,1)S(1)}, bf16[384,640]{1,0:T(8,128)(2,1)S(1)}, u32[]{:S(2)}, u32[]{:S(2)}) collective-permute-start(bf16[384,640]{1,0:T(8,128)(2,1)S(1)} %collective-permute-done.3.refs_4_), channel_id=1, source_target_pairs={{0,2},{2,4},{4,6},{6,0},{1,3},{3,5},{5,7},{7,1},{8,10},{10,12},{12... | collective-permute-start | bytes 1474568 | tf_op jit(solution)/shard_map/ppermute | solution.py:33
  105.0 17.1 %collective-permute-start.11 = (bf16[336,512]{1,0:T(8,128)(2,1)S(1)}, bf16[336,512]{1,0:T(8,128)(2,1)S(1)}, u32[]{:S(2)}, u32[]{:S(2)}) collective-permute-start(bf16[336,512]{1,0:T(8,128)(2,1)S(1)} %collective-permute-done.10.refs_11_), channel_id=1, source_target_pairs={{0,64},{8,456},{64,128},{72,8},{128,192},{136,72},{192,256},{200,1... | collective-permute-start | bytes 1032200 | tf_op jit(solution)/shard_map/ppermute | solution.py:41
  110.3 11.8 %collective-permute-start.15 = (bf16[320,512]{1,0:T(8,128)(2,1)S(1)}, bf16[320,512]{1,0:T(8,128)(2,1)S(1)}, u32[]{:S(2)}, u32[]{:S(2)}) collective-permute-start(bf16[320,512]{1,0:T(8,128)(2,1)S(1)} %collective-permute-done.14.refs_16_), channel_id=1, source_target_pairs={{0,64},{8,456},{64,128},{72,8},{128,192},{136,72},{192,256},{200,1... | collective-permute-start | bytes 983048 | tf_op jit(solution)/shard_map/ppermute | solution.py:41
  129.2 17.4 %all-to-all-start.1 = ((bf16[64,4,256]{2,1,0:T(4,128)(2,1)}), bf16[64,4,256]{2,1,0:T(4,128)(2,1)S(1)}, u32[]{:S(2)}, u32[]{:S(2)}) async-start(bf16[64,4,256]{2,1,0:T(4,128)(2,1)} %get-tuple-element.28), calls=%async_computation.1 | async-start | bytes 262144 | tf_op jit(solution)/shard_map/all_to_all | solution.py:272
